TPU v7x, 64 devices: a 2x2x8 block of a 4x4x8 slice. The times are simulated.
64 devices in a mesh: data: 4 (over x, y), dap: 16 (over z, core).
Axes of the slice: x: 2, y: 2, z: 8, core: 2. Of those that a mesh axis runs over, the one named last changes fastest.
The devices are a block of a 4x4x8 slice.
Arguments:
- msa_act: bfloat16 [8192, 128, 64], P(('data', 'dap')), parts along dimension 0
- pair_act: bfloat16 [512, 128, 128], P(('data', 'dap')), parts along dimension 0
- msa_mask: int32 [8192, 128], P('data'), parts along dimension 0
- res_mask: int32 [512], P('data'), parts along dimension 0
- row_bias_w: bfloat16 [128, 8], replicated
- row_qkvg_w: bfloat16 [64, 4, 8, 8], replicated
- row_out_w: bfloat16 [8, 8, 64], replicated
- col_query_w: bfloat16 [64, 8, 8], replicated
- col_kv_w: bfloat16 [64, 2, 8], replicated
- col_gate_w: bfloat16 [64, 8, 8], replicated
- col_out_w: bfloat16 [8, 8, 64], replicated
- opm_proj_w: bfloat16 [64, 2, 32], replicated
- opm_out_w: bfloat16 [32, 32, 128], replicated
- start_bias_w: bfloat16 [128, 4], replicated
- start_qkvg_w: bfloat16 [128, 4, 4, 32], replicated
- start_out_w: bfloat16 [4, 32, 128], replicated
- end_bias_w: bfloat16 [128, 4], replicated
- end_qkvg_w: bfloat16 [128, 4, 4, 32], replicated
- end_out_w: bfloat16 [4, 32, 128], replicated
Outputs:
- output 1: bfloat16 [8192, 128, 64], P(('data', 'dap')), parts along dimension 0
- output 2: bfloat16 [512, 128, 128], P(('data', 'dap')), parts along dimension 0
There are 4 independent parts. A program takes and returns all parts, laid end to end along the dimension named above; an argument that names none is the same for every part.
All inputs are finite; a program needn't handle non-finite values.
Results may differ from a plain program's by a relative error of at most 0.0148932.
Values are sent between devices in bfloat16 or wider.
A program may use at most 768 MiB of HBM per device.

v0:
```python
import jax
import jax.numpy as jnp
from jax import lax
from jax.sharding import PartitionSpec as P


def layer_norm(values):
    widened = values.astype(jnp.float32)
    mean_val = jnp.mean(widened, axis=-1, keepdims=True)
    centered = widened - mean_val
    variance = jnp.mean(centered * centered, axis=-1, keepdims=True)
    return (centered * lax.rsqrt(variance + 1e-5)).astype(jnp.bfloat16)


def mask_bias(mask_vals):
    return (mask_vals.astype(jnp.float32) - 1.0) * 1e4


def matmul_bf(einsum_form, left_arr, right_arr):
    return jnp.einsum(einsum_form, left_arr, right_arr, preferred_element_type=jnp.float32).astype(jnp.bfloat16)


def gated_out(einsum_form, gate_proj, attended, out_w):
    gated_vals = (jax.nn.sigmoid(gate_proj.astype(jnp.float32)) * attended).astype(jnp.bfloat16)
    return jnp.einsum(einsum_form, gated_vals, out_w, preferred_element_type=jnp.float32)


def row_attention(value_a7, bias_full, seq_mask, qkvg_w, out_w):
    projected = matmul_bf('sic,cahd->asihd', layer_norm(value_a7), qkvg_w)
    logits = jnp.einsum('sihd,sjhd->shij', projected[0], projected[1], preferred_element_type=jnp.float32) * (qkvg_w.shape[-1] ** -0.5) + bias_full[None] + mask_bias(seq_mask)[:, None, None, :]
    attn_probs = jax.nn.softmax(logits, axis=-1).astype(jnp.bfloat16)
    attended = jnp.einsum('shij,sjhd->sihd', attn_probs, projected[2], preferred_element_type=jnp.float32)
    return (value_a7 + gated_out('sihd,hdc->sic', projected[3], attended, out_w)).astype(jnp.bfloat16)


def column_attention(value_a7, col_mask, query_w, kv_w, gate_w, out_w):
    value_a6 = layer_norm(value_a7)
    mask_count = jnp.sum(col_mask, axis=0).astype(jnp.float32) + 1e-10
    mean_query = (jnp.einsum('sr,src->rc', col_mask.astype(jnp.bfloat16), value_a6, preferred_element_type=jnp.float32) / mask_count[:, None]).astype(jnp.bfloat16)
    query_proj = matmul_bf('rc,chd->rhd', mean_query, query_w)
    key_val = matmul_bf('src,cad->asrd', value_a6, kv_w)
    gate_proj = matmul_bf('src,chd->srhd', value_a6, gate_w)
    logits = jnp.einsum('rhd,srd->rhs', query_proj, key_val[0], preferred_element_type=jnp.float32) * (kv_w.shape[-1] ** -0.5) + mask_bias(col_mask).T[:, None, :]
    attn_probs = jax.nn.softmax(logits, axis=-1).astype(jnp.bfloat16)
    attended = jnp.einsum('rhs,srd->rhd', attn_probs, key_val[1], preferred_element_type=jnp.float32)
    return (value_a7 + gated_out('srhd,hdc->src', gate_proj, attended[None], out_w)).astype(jnp.bfloat16)


def outer_update(pair_act, left_proj, right_full, counts, out_w):
    outer_sum = matmul_bf('sie,sjf->ijef', left_proj, right_full)
    update = jnp.einsum('ijef,efc->ijc', outer_sum, out_w, preferred_element_type=jnp.float32) / (1e-3 + counts)[:, :, None]
    return (pair_act + update).astype(jnp.bfloat16)


def triangle_rows(pair_act, pair_ln, bias_full, res_mask, qkvg_w, out_w):
    projected = matmul_bf('ijc,cahd->aijhd', pair_ln, qkvg_w)
    logits = jnp.einsum('ijhd,ikhd->ihjk', projected[0], projected[1], preferred_element_type=jnp.float32) * (qkvg_w.shape[-1] ** -0.5) + bias_full[None] + mask_bias(res_mask)[None, None, None, :]
    attn_probs = jax.nn.softmax(logits, axis=-1).astype(jnp.bfloat16)
    attended = jnp.einsum('ihjk,ikhd->ijhd', attn_probs, projected[2], preferred_element_type=jnp.float32)
    return (pair_act + gated_out('ijhd,hdc->ijc', projected[3], attended, out_w)).astype(jnp.bfloat16)


def triangle_cols(pair_cols, pair_ln, bias_full, res_mask, qkvg_w, out_w):
    projected = matmul_bf('ijc,cahd->aijhd', pair_ln, qkvg_w)
    logits = jnp.einsum('ijhd,kjhd->jhik', projected[0], projected[1], preferred_element_type=jnp.float32) * (qkvg_w.shape[-1] ** -0.5) + bias_full[None] + mask_bias(res_mask)[None, None, None, :]
    attn_probs = jax.nn.softmax(logits, axis=-1).astype(jnp.bfloat16)
    attended = jnp.einsum('jhik,kjhd->ijhd', attn_probs, projected[2], preferred_element_type=jnp.float32)
    return (pair_cols + gated_out('ijhd,hdc->ijc', projected[3], attended, out_w)).astype(jnp.bfloat16)


def solution(mesh):
    def evoformer_block(value_a7, pair_act, array_b8, res_mask, row_bias_w, row_qkvg_w, row_out_w, col_query_w, col_kv_w, col_gate_w, col_out_w, opm_proj_w, opm_out_w, start_bias_w, start_qkvg_w, start_out_w, end_bias_w, end_qkvg_w, end_out_w):
        seq_local = value_a7.shape[0]
        res_local = pair_act.shape[0]
        dev_index = lax.axis_index('dap')
        seq_mask = lax.dynamic_slice_in_dim(array_b8, dev_index * seq_local, seq_local, axis=0)
        col_mask = lax.dynamic_slice_in_dim(array_b8, dev_index * res_local, res_local, axis=1)

        row_bias = matmul_bf('ijc,ch->hij', layer_norm(pair_act), row_bias_w)
        row_bias_full = lax.all_gather(row_bias, 'dap', axis=1, tiled=True)
        value_a7 = row_attention(value_a7, row_bias_full, seq_mask, row_qkvg_w, row_out_w)

        value_a8 = lax.all_to_all(value_a7, 'dap', 1, 0, tiled=True)
        value_a8 = column_attention(value_a8, col_mask, col_query_w, col_kv_w, col_gate_w, col_out_w)

        projected = matmul_bf('src,cae->asre', layer_norm(value_a8), opm_proj_w) * col_mask.astype(jnp.bfloat16)[None, :, :, None]
        right_full = lax.all_gather(projected[1], 'dap', axis=1, tiled=True)
        counts = jnp.einsum('si,sj->ij', col_mask.astype(jnp.bfloat16), array_b8.astype(jnp.bfloat16), preferred_element_type=jnp.float32)
        pair_act = outer_update(pair_act, projected[0], right_full, counts, opm_out_w)
        array_b7 = lax.all_to_all(value_a8, 'dap', 0, 1, tiled=True)

        pair_ln = layer_norm(pair_act)
        start_full = lax.all_gather(matmul_bf('ijc,ch->hij', pair_ln, start_bias_w), 'dap', axis=1, tiled=True)
        pair_act = triangle_rows(pair_act, pair_ln, start_full, res_mask, start_qkvg_w, start_out_w)

        pair_cols = lax.all_to_all(pair_act, 'dap', 1, 0, tiled=True)
        cols_ln = layer_norm(pair_cols)
        end_full = lax.all_gather(matmul_bf('ijc,ch->hji', cols_ln, end_bias_w), 'dap', axis=1, tiled=True)
        pair_cols = triangle_cols(pair_cols, cols_ln, end_full, res_mask, end_qkvg_w, end_out_w)
        pair_out = lax.all_to_all(pair_cols, 'dap', 0, 1, tiled=True)
        return array_b7, pair_out

    row_spec = P(('data', 'dap'), None, None)
    in_specs = (row_spec, row_spec, P('data', None), P('data')) + (P(),) * 15
    return jax.shard_map(evoformer_block, mesh=mesh, in_specs=in_specs, out_specs=(row_spec, row_spec), check_vma=False)
```

profile of v0, /device:TPU:21, one launch (start us, length us, event | category | flops | bytes accessed | tf_op | source)
XLA Modules:
  0.0 456.0 jit_solution(13620802890155551551)
XLA Ops:
  12.3 23.3 %all_gather.12 = bf16[8,128,128]{2,0,1:T(8,128)(2,1)} all-gather(bf16[8,8,128]{2,0,1:T(8,128)(2,1)S(1)} %fusion.73), channel_id=1, replica_groups=mesh['data'=4,'dap'=16] {'dap'}, dimensions={1}, use_global_device_ids=true | all-gather | bytes 278528 | tf_op jit(solution)/shard_map/all_gather | solution.py:80
  41.5 6.4 %convert_bitcast_fusion.1 = bf16[4,128,128,8,8]{2,4,3,0,1:T(8,128)(2,1)} fusion(bf16[128,128,64]{1,2,0:T(8,128)(2,1)S(1)} %copy-done.1, f32[128,128]{1,0:T(8,128)S(1)} %add_rsqrt_fusion.1, f32[128,128]{1,0:T(8,128)S(1)} %broadcast_multiply_fusion.2, bf16[64,4,8,8]{0,3,2,1:T(8,128)(2,1)} %param.24), kind=kOutput, calls=%fused_computation.15 | convolution fusion | flops 545259520 | bytes 10649600 | tf_op jit(solution)/shard_map/sic,cahd->asihd/dot_general | solution.py:20
  47.9 33.0 %fusion.159 = (f32[128,8,128]{2,1,0:T(8,128)}, f32[128,8,128,128]{2,3,1,0:T(8,128)}) fusion(f32[128,128]{1,0:T(8,128)} %add_multiply_fusion, f32[8,128,128]{1,2,0:T(8,128)} %copy.158, bf16[4,128,128,8,8]{2,4,3,0,1:T(8,128)(2,1)} %convert_bitcast_fusion.1), kind=kOutput, calls=%fused_computation.218 | convolution fusion | flops 352321664 | bytes 72417280 | tf_op jit(solution)/shard_map/sub | solution.py:31
  80.9 25.8 %fusion.27 = bf16[128,128,64]{1,2,0:T(8,128)(2,1)} fusion(bf16[128,128,64]{1,2,0:T(8,128)(2,1)S(1)} %copy-done.1, f32[128,8,128,128]{2,3,1,0:T(8,128)} %get-tuple-element.17, f32[128,8,128]{2,1,0:T(8,128)} %get-tuple-element.16, bf16[4,128,128,8,8]{2,4,3,0,1:T(8,128)(2,1)} %convert_bitcast_fusion.1, bf16[8,8,64]{2,1,0:T(8,128)(2,1)S(1)} %copy-done.13), kind=kOutput, calls=%fused_computation.36 | convolution fusion | flops 445644800 | bytes 76029952 | tf_op jit(solution)/shard_map/sihd,hdc->sic/dot_general | solution.py:25
  106.7 4.6 %copy.160 = bf16[128,128,64]{0,2,1:T(8,128)(2,1)} copy(bf16[128,128,64]{1,2,0:T(8,128)(2,1)} %fusion.27) | data formatting | bytes 4194304 | tf_op jit(solution)/shard_map/convert_element_type | solution.py:33
  111.2 3.9 all-to-all-start
  118.7 45.8 %all-to-all-done = bf16[128,128,64]{0,2,1:T(8,128)(2,1)S(1)} async-done(((bf16[128,128,64]{0,2,1:T(8,128)(2,1)}), bf16[128,128,64]{0,2,1:T(8,128)(2,1)S(1)}, u32[]{:S(2)}, u32[]{:S(2)}) %all-to-all-start) | async-done | bytes 2097184 | tf_op jit(solution)/shard_map/all_to_all | solution.py:83
  173.3 5.0 %convert_reduce_fusion.1 = (f32[2048,8]{0,1:T(8,128)}, bf16[2048,8,64]{0,2,1:T(8,128)(2,1)}) fusion(bf16[8,8,64]{2,1,0:T(8,128)(2,1)S(1)} %copy-done.15, f32[8,8,8]{1,2,0:T(8,128)} %fusion.107, bf16[64,8,8]{0,2,1:T(8,128)(2,1)S(1)} %copy-done.16, f32[2048,8]{0,1:T(8,128)} %copy-done.8, f32[2048,8]{0,1:T(8,128)S(1)} %get-tuple-element.14, ...), kind=kOutput, calls=%fused_computation.25 | convolution fusion | flops 285196288 | bytes 4409344 | tf_op jit(solution)/shard_map/srhd,hdc->src/dot_general | solution.py:25
  181.4 2.4 fusion.33
  185.2 91.3 %all-gather.3.cloned.1.call-done = bf16[1,2048,128,32]{1,3,0,2:T(8,128)(2,1)} async-done(((bf16[1,2048,8,32]{1,3,0,2:T(8,128)(2,1)}), bf16[1,2048,128,32]{1,3,0,2:T(8,128)(2,1)}) %all-gather.3.cloned.1.call-update) | async-done | bytes 16777232 | tf_op jit(solution)/shard_map/all_gather | solution.py:87
  276.5 21.6 %convert_bitcast_fusion = bf16[8,128,32,32]{2,3,0,1:T(8,128)(2,1)} fusion(bf16[1,2048,128,32]{1,3,0,2:T(8,128)(2,1)} %all-gather.3.cloned.1.call-done, bf16[2,2048,8,32]{1,3,0,2:T(8,128)(2,1)S(1)} %fusion.33), kind=kOutput, calls=%fused_computation.14 | convolution fusion | flops 4296015872 | bytes 19922944 | tf_op jit(solution)/shard_map/sie,sjf->ijef/dot_general | solution.py:20
  298.1 13.3 %copy.170 = bf16[8,128,32,32]{1,3,2,0:T(8,128)(2,1)} copy(bf16[8,128,32,32]{2,3,0,1:T(8,128)(2,1)} %convert_bitcast_fusion) | data formatting | bytes 4194304 | tf_op jit(solution)/shard_map/convert_element_type | solution.py:20
  314.4 16.0 %all_gather.14 = bf16[4,128,128]{2,0,1:T(4,128)(2,1)S(1)} all-gather(bf16[4,8,128]{2,0,1:T(4,128)(2,1)S(1)} %fusion.74), channel_id=1, replica_groups=mesh['data'=4,'dap'=16] {'dap'}, dimensions={1}, use_global_device_ids=true | all-gather | bytes 139264 | tf_op jit(solution)/shard_map/all_gather | solution.py:93
  336.1 6.3 %all-to-all-start.2 = ((bf16[8,128,128]{2,0,1:T(8,128)(2,1)}), bf16[8,128,128]{2,0,1:T(8,128)(2,1)S(1)}, u32[]{:S(2)}, u32[]{:S(2)}) async-start(bf16[8,128,128]{2,0,1:T(8,128)(2,1)} %copy.177), calls=%async_computation.2 | async-start | bytes 524288 | tf_op jit(solution)/shard_map/all_to_all | solution.py:96
  342.4 4.3 copy.167
  346.7 7.5 %reshape.203 = bf16[16,2,32768]{2,1,0:T(2,128)(2,1)} reshape(bf16[2048,8,64]{2,1,0:T(8,128)(2,1)} %copy.167) | data formatting | bytes 4194304
  354.2 7.4 %all-to-all-start.1 = ((bf16[16,2,32768]{2,1,0:T(2,128)(2,1)}), bf16[16,2,32768]{2,1,0:T(2,128)(2,1)S(1)}, u32[]{:S(2)}, u32[]{:S(2)}) async-start(bf16[16,2,32768]{2,1,0:T(2,128)(2,1)} %reshape.203), calls=%async_computation.1 | async-start | bytes 4194304 | tf_op jit(solution)/shard_map/all_to_all | solution.py:90
  363.4 58.0 %all_gather.15 = bf16[4,128,128]{2,0,1:T(4,128)(2,1)S(1)} all-gather(bf16[4,8,128]{2,0,1:T(4,128)(2,1)S(1)} %fusion.75), channel_id=1, replica_groups=mesh['data'=4,'dap'=16] {'dap'}, dimensions={1}, use_global_device_ids=true | all-gather | bytes 139264 | tf_op jit(solution)/shard_map/all_gather | solution.py:98
  423.2 3.3 fusion.169
  426.5 2.4 fusion.67
  429.8 5.7 %all-to-all-start.3 = ((bf16[128,8,128]{2,1,0:T(8,128)(2,1)}), bf16[128,8,128]{2,1,0:T(8,128)(2,1)S(1)}, u32[]{:S(2)}, u32[]{:S(2)}) async-start(bf16[128,8,128]{2,1,0:T(8,128)(2,1)} %copy.188), calls=%async_computation.3 | async-start | bytes 524288 | tf_op jit(solution)/shard_map/all_to_all | solution.py:100
  435.6 5.0 %reshape.204 = bf16[2048,8,64]{2,1,0:T(8,128)(2,1)} reshape(bf16[16,2,32768]{2,1,0:T(2,128)(2,1)S(1)} %all-to-all-done.1) | data formatting | bytes 4194304
  440.6 4.1 copy.169
  444.7 3.3 copy.190
  (109 shorter events, 41.3 us)
Async XLA Ops:
  7.2 304.3 %copy-start = (bf16[32,32,128]{2,1,0:T(8,128)(2,1)S(1)}, bf16[32,32,128]{2,1,0:T(8,128)(2,1)}, u32[]{:S(2)}) copy-start(bf16[32,32,128]{2,1,0:T(8,128)(2,1)} %param.31) | copy-start | bytes 786436
  7.2 32.7 %copy-start.1 = (bf16[128,128,64]{1,2,0:T(8,128)(2,1)S(1)}, bf16[128,128,64]{1,2,0:T(8,128)(2,1)}, u32[]{:S(2)}) copy-start(bf16[128,128,64]{1,2,0:T(8,128)(2,1)} %param.19) | copy-start | bytes 6291460
  7.2 33.7 %copy-start.3 = (s32[2048,128]{1,0:T(8,128)S(1)}, s32[2048,128]{1,0:T(8,128)}, u32[]{:S(2)}) copy-start(s32[2048,128]{1,0:T(8,128)} %param.21) | copy-start | bytes 3145732
  47.9 33.0 %copy-start.13 = (bf16[8,8,64]{2,1,0:T(8,128)(2,1)S(1)}, bf16[8,8,64]{2,1,0:T(8,128)(2,1)}, u32[]{:S(2)}) copy-start(bf16[8,8,64]{2,1,0:T(8,128)(2,1)} %param.25) | copy-start | bytes 24580
  111.2 53.2 %all-to-all-start = ((bf16[128,128,64]{0,2,1:T(8,128)(2,1)}), bf16[128,128,64]{0,2,1:T(8,128)(2,1)S(1)}, u32[]{:S(2)}, u32[]{:S(2)}) async-start(bf16[128,128,64]{0,2,1:T(8,128)(2,1)} %copy.160), calls=%async_computation | async-start | bytes 4194304 | tf_op jit(solution)/shard_map/all_to_all | solution.py:83
  115.1 161.4 %all-gather.3.cloned.1.call-start = ((), (), s32[]{:S(2)}) async-start(), calls=%async_computation.4 | async-start | bytes 17825792 | tf_op jit(solution)/shard_map/all_gather | solution.py:87
  164.5 2.4 copy-start.14
  164.5 3.2 copy-start.18
  167.7 5.6 %copy-start.15 = (bf16[8,8,64]{2,1,0:T(8,128)(2,1)S(1)}, bf16[8,8,64]{2,1,0:T(8,128)(2,1)}, u32[]{:S(2)}) copy-start(bf16[8,8,64]{2,1,0:T(8,128)(2,1)} %param.29) | copy-start | bytes 24580
  167.7 5.6 %copy-start.16 = (bf16[64,8,8]{0,2,1:T(8,128)(2,1)S(1)}, bf16[64,8,8]{0,2,1:T(8,128)(2,1)}, u32[]{:S(2)}) copy-start(bf16[64,8,8]{0,2,1:T(8,128)(2,1)} %param.28) | copy-start | bytes 24580
  173.3 8.2 %copy-start.17 = (bf16[64,2,32]{0,2,1:T(8,128)(2,1)S(1)}, bf16[64,2,32]{0,2,1:T(8,128)(2,1)}, u32[]{:S(2)}) copy-start(bf16[64,2,32]{0,2,1:T(8,128)(2,1)} %param.30) | copy-start | bytes 24580
  181.4 3.6 copy-start.19
  298.1 13.4 %copy-start.4 = (bf16[8,128,128]{1,2,0:T(8,128)(2,1)S(1)}, bf16[8,128,128]{1,2,0:T(8,128)(2,1)}, u32[]{:S(2)}) copy-start(bf16[8,128,128]{1,2,0:T(8,128)(2,1)} %copy.156) | copy-start | bytes 786436
  311.5 2.3 copy-start.6
  311.5 2.7 copy-start.9
  313.6 19.2 %copy-start.11 = (bf16[4,32,128]{2,1,0:T(8,128)(2,1)S(1)}, bf16[4,32,128]{2,1,0:T(8,128)(2,1)}, u32[]{:S(2)}) copy-start(bf16[4,32,128]{2,1,0:T(8,128)(2,1)} %param.34) | copy-start | bytes 98308
  314.2 18.6 %copy-start.5 = (bf16[4,8,128,4,32]{2,4,3,0,1:T(8,128)(2,1)}, bf16[4,8,128,4,32]{2,4,3,0,1:T(8,128)(2,1)S(1)}, u32[]{:S(2)}) copy-start(bf16[4,8,128,4,32]{2,4,3,0,1:T(8,128)(2,1)S(1)} %fusion.59) | copy-start | bytes 3145732
  332.8 9.6 %copy-start.2 = (bf16[2048,8,64]{0,2,1:T(8,128)(2,1)S(1)}, bf16[2048,8,64]{0,2,1:T(8,128)(2,1)}, u32[]{:S(2)}) copy-start(bf16[2048,8,64]{0,2,1:T(8,128)(2,1)} %get-tuple-element.19) | copy-start | bytes 6291460
  336.1 18.1 %all-to-all-start.2 = ((bf16[8,128,128]{2,0,1:T(8,128)(2,1)}), bf16[8,128,128]{2,0,1:T(8,128)(2,1)S(1)}, u32[]{:S(2)}, u32[]{:S(2)}) async-start(bf16[8,128,128]{2,0,1:T(8,128)(2,1)} %copy.177), calls=%async_computation.2 | async-start | bytes 524288 | tf_op jit(solution)/shard_map/all_to_all | solution.py:96
  354.2 8.7 %copy-start.10 = (bf16[128,4]{0,1:T(4,128)(2,1)S(1)}, bf16[128,4]{0,1:T(4,128)(2,1)}, u32[]{:S(2)}) copy-start(bf16[128,4]{0,1:T(4,128)(2,1)} %param.35) | copy-start | bytes 3076
  354.2 67.3 %copy-start.7 = (bf16[128,4,4,32]{0,3,2,1:T(8,128)(2,1)S(1)}, bf16[128,4,4,32]{0,3,2,1:T(8,128)(2,1)}, u32[]{:S(2)}) copy-start(bf16[128,4,4,32]{0,3,2,1:T(8,128)(2,1)} %param.36) | copy-start | bytes 393220
  354.2 75.6 %all-to-all-start.1 = ((bf16[16,2,32768]{2,1,0:T(2,128)(2,1)}), bf16[16,2,32768]{2,1,0:T(2,128)(2,1)S(1)}, u32[]{:S(2)}, u32[]{:S(2)}) async-start(bf16[16,2,32768]{2,1,0:T(2,128)(2,1)} %reshape.203), calls=%async_computation.1 | async-start | bytes 4194304 | tf_op jit(solution)/shard_map/all_to_all | solution.py:90
  423.2 3.3 copy-start.12
  429.8 18.2 %all-to-all-start.3 = ((bf16[128,8,128]{2,1,0:T(8,128)(2,1)}), bf16[128,8,128]{2,1,0:T(8,128)(2,1)S(1)}, u32[]{:S(2)}, u32[]{:S(2)}) async-start(bf16[128,8,128]{2,1,0:T(8,128)(2,1)} %copy.188), calls=%async_computation.3 | async-start | bytes 524288 | tf_op jit(solution)/shard_map/all_to_all | solution.py:100
  (2 other events, 2.9 us)
Sparse Core Ops, SparseCore 0:
  185.1 91.3 all-gather.2
where the time goes:
time: 462 us; the launch traced here: 456 us
  waiting for transfers between devices  137 us (30%)
  matrix products  118 us (26%)
  blocking collectives  97.3 us (21%)
  local copies, waits for them, and re-layouts  52.1 us (11%)
  starting transfers between devices  23.4 us (5%)
  between operations  14.9 us (3%)
  other arithmetic  13.4 us (3%)
    all_gather x1, waiting for transfers between devices, evoformer_block(): right_full = lax.all_gather(projected[1], 'dap', axis=1, tiled=True)  91.3 us
    all_gather x1, blocking collectives, evoformer_block(): lax.all_gather(matmul_bf('ijc,ch->hji', cols_ln, end_bias_w), 'dap', axis...  58 us
    all_to_all x1, waiting for transfers between devices, evoformer_block(): value_a8 = lax.all_to_all(value_a7, 'dap', 1, 0, tiled=True)  45.8 us
    dot_general x10, matrix products, matmul_bf(): jnp.einsum(einsum_form, left_arr, right_arr, preferred_element_type=jnp.f...  36.5 us
    dot_general x4, matrix products, gated_out(): jnp.einsum(einsum_form, gated_vals, out_w, preferred_element_type=jnp.flo...  35.6 us
    sub x1, matrix products, row_attention(): attn_probs = jax.nn.softmax(logits, axis=-1).astype(jnp.bfloat16)  33 us
    all_gather x1, blocking collectives, evoformer_block(): row_bias_full = lax.all_gather(row_bias, 'dap', axis=1, tiled=True)  23.3 us
    unnamed x47, local copies, waits for them, and re-layouts  19.4 us
  transfers between devices with their start and end apart: 5, of which 2 were waited for; matrix products, arithmetic and copies ran while one was open for 8% of the time, Pallas kernels for 0%

commit v1 on v0

v1 whole, which is shorter than its diff:
```python
import functools
import math

import jax
import jax.numpy as jnp
from jax import lax
from jax.experimental import pallas as pl
from jax.experimental.pallas import tpu as pltpu
from jax.sharding import PartitionSpec as P

F32 = jnp.float32
BF16 = jnp.bfloat16
MESH = pl.DeviceIdType.MESH
LOG2E = math.log2(math.e)
VMEM = pltpu.VMEM


def layer_norm(values):
    widened = values.astype(jnp.float32)
    mean_val = jnp.mean(widened, axis=-1, keepdims=True)
    centered = widened - mean_val
    variance = jnp.mean(centered * centered, axis=-1, keepdims=True)
    return (centered * lax.rsqrt(variance + 1e-5)).astype(jnp.bfloat16)


def mask_bias(mask_vals):
    return (mask_vals.astype(jnp.float32) - 1.0) * 1e4


def matmul_bf(einsum_form, left_arr, right_arr):
    return jnp.einsum(einsum_form, left_arr, right_arr, preferred_element_type=jnp.float32).astype(jnp.bfloat16)


def gated_out(einsum_form, gate_proj, attended, out_w):
    gated_vals = (jax.nn.sigmoid(gate_proj.astype(jnp.float32)) * attended).astype(jnp.bfloat16)
    return jnp.einsum(einsum_form, gated_vals, out_w, preferred_element_type=jnp.float32)


def triangle_rows(pair_act, pair_ln, bias_full, res_mask, qkvg_w, out_w):
    projected = matmul_bf('ijc,cahd->aijhd', pair_ln, qkvg_w)
    logits = jnp.einsum('ijhd,ikhd->ihjk', projected[0], projected[1], preferred_element_type=jnp.float32) * (qkvg_w.shape[-1] ** -0.5) + bias_full[None] + mask_bias(res_mask)[None, None, None, :]
    attn_probs = jax.nn.softmax(logits, axis=-1).astype(jnp.bfloat16)
    attended = jnp.einsum('ihjk,ikhd->ijhd', attn_probs, projected[2], preferred_element_type=jnp.float32)
    return (pair_act + gated_out('ijhd,hdc->ijc', projected[3], attended, out_w)).astype(jnp.bfloat16)


def triangle_cols(pair_cols, pair_ln, bias_full, res_mask, qkvg_w, out_w):
    projected = matmul_bf('ijc,cahd->aijhd', pair_ln, qkvg_w)
    logits = jnp.einsum('ijhd,kjhd->jhik', projected[0], projected[1], preferred_element_type=jnp.float32) * (qkvg_w.shape[-1] ** -0.5) + bias_full[None] + mask_bias(res_mask)[None, None, None, :]
    attn_probs = jax.nn.softmax(logits, axis=-1).astype(jnp.bfloat16)
    attended = jnp.einsum('jhik,kjhd->ijhd', attn_probs, projected[2], preferred_element_type=jnp.float32)
    return (pair_cols + gated_out('ijhd,hdc->ijc', projected[3], attended, out_w)).astype(jnp.bfloat16)


def mm(left, right):
    return jnp.dot(left, right, preferred_element_type=F32)


def mm_nt(left, right):
    return lax.dot_general(left, right, (((1,), (1,)), ((), ())), preferred_element_type=F32)


def ln_rows(x):
    n = x.shape[0]
    xc = x - jnp.sum(x, axis=0, keepdims=True) * (1.0 / n)
    var = jnp.sum(xc * xc, axis=0, keepdims=True) * (1.0 / n)
    return (xc * lax.rsqrt(var + 1e-5)).astype(BF16)


def ln_lanes(x):
    n = x.shape[1]
    xc = x - jnp.sum(x, axis=1, keepdims=True) * (1.0 / n)
    var = jnp.sum(xc * xc, axis=1, keepdims=True) * (1.0 / n)
    return (xc * lax.rsqrt(var + 1e-5)).astype(BF16)


def bf16_split(value, terms):
    import numpy as np
    out = []
    for _ in range(terms):
        t = float(np.asarray(value, dtype=jnp.bfloat16))
        out.append(t)
        value = value - t
    return out


def bias_kernel(z_ref, w_ref, out_ref):
    heads = w_ref.shape[0]
    for r in range(z_ref.shape[0]):
        ln = ln_lanes(z_ref[r].astype(F32))
        out_ref[r * heads:(r + 1) * heads, :] = mm_nt(w_ref[...], ln).astype(BF16).astype(F32)


def row_kernel(m_ref, braw_ref, mask_ref, wqkvg_ref, wout_ref, wkvg_ref, m1_ref, kv_ref, g_ref, qsum_ref, bias_ref, wo_ref, *, heads, hd):
    seqs, chans, res = m_ref.shape
    width = heads * hd
    scale2 = hd ** -0.5 * LOG2E
    wo_ref[...] = wout_ref[...].astype(F32).T.astype(BF16)
    for h in range(heads):
        plane = braw_ref[pl.ds(h, res, stride=heads), :]
        bias_ref[:, h * res:(h + 1) * res] = plane.T * LOG2E
    qsum_ref[...] = jnp.zeros_like(qsum_ref)
    terms = bf16_split(1e4 / hd ** -0.5, 3)
    rows16 = lax.broadcasted_iota(jnp.int32, (16, res), 0)
    first = rows16 < hd
    mvec = jnp.where(rows16 == 0, terms[0], jnp.where(rows16 == 1, terms[1], jnp.where(rows16 == 2, terms[2], 0.0)))
    zero16 = jnp.zeros((16, res), BF16)
    one16 = jnp.ones((16, res), BF16)
    npairs = heads // 2

    def attend(qkvg, mrow):
        q = qkvg[0:width]
        kaug = jnp.concatenate([qkvg[width:2 * width], (mrow - 1.0) * mvec], axis=0)
        kt = kaug.T.astype(BF16)
        vT = qkvg[2 * width:3 * width].astype(BF16)
        outs = []
        for t in range(npairs):
            q16 = q[t * 16:(t + 1) * 16]
            qa = jnp.where(first, q16, 0.0).astype(BF16)
            qb = jnp.where(first, 0.0, q16).astype(BF16)
            left = jnp.concatenate([zero16] * t + [qa] + [zero16] * (npairs - 1 - t) + [one16], axis=0)
            right = jnp.concatenate([zero16] * t + [qb] + [zero16] * (npairs - 1 - t) + [one16], axis=0)
            s = mm(kt, jnp.concatenate([left, right], axis=1))
            s = s * scale2 + bias_ref[:, t * 2 * res:(t + 1) * 2 * res]
            p = jnp.exp2(s - jnp.max(s, axis=0, keepdims=True))
            inv = 1.0 / jnp.sum(p, axis=0, keepdims=True)
            o = mm(vT[t * 16:(t + 1) * 16], p.astype(BF16)) * inv
            outs += [o[0:hd, 0:res], o[hd:2 * hd, res:2 * res]]
        att = jnp.concatenate(outs, axis=0)
        return (jax.nn.sigmoid(qkvg[3 * width:4 * width]) * att).astype(BF16)

    def body(it, _):
        s0 = it * 2
        xs = [m_ref[s0 + u].astype(F32) for u in range(2)]
        lns = [ln_rows(x) for x in xs]
        proj = mm(wqkvg_ref[...], jnp.concatenate(lns, axis=1)).astype(BF16).astype(F32)
        mrows = [mask_ref[pl.ds(s0 + u, 1), :] for u in range(2)]
        ys = [attend(proj[:, u * res:(u + 1) * res], mrows[u]) for u in range(2)]
        upd = mm(wo_ref[...], jnp.concatenate(ys, axis=1))
        ln1 = []
        for u in range(2):
            m1 = (xs[u] + upd[:, u * res:(u + 1) * res]).astype(BF16)
            m1_ref[s0 + u] = m1
            l1 = ln_rows(m1.astype(F32))
            qsum_ref[...] += l1.astype(F32) * mrows[u]
            ln1.append(l1)
        kvg = mm(wkvg_ref[...], jnp.concatenate(ln1, axis=1)).astype(BF16)
        for u in range(2):
            kv_ref[pl.ds((s0 + u) * 2 * hd, 2 * hd), :] = kvg[0:2 * hd, u * res:(u + 1) * res].astype(F32)
            g_ref[s0 + u] = kvg[2 * hd:, u * res:(u + 1) * res]
        return 0

    lax.fori_loop(0, seqs // 2, body, 0)


def col_stats(qtot, cnt, kv_ref, mask_ref, wq_ref, planes_ref, stats_ref, heads, hd):
    seqs, res = mask_ref.shape
    qbar = (qtot / (cnt + 1e-10)).astype(BF16)
    q = mm(wq_ref[...], qbar).astype(BF16).astype(F32)
    for d in range(2 * hd):
        planes_ref[d] = kv_ref[pl.ds(d, seqs, stride=2 * hd), :]
    mb = (mask_ref[...] - 1.0) * (1e4 * LOG2E)
    for h in range(heads):
        acc = q[h * hd:h * hd + 1] * planes_ref[0]
        for d in range(1, hd):
            acc = acc + q[h * hd + d:h * hd + d + 1] * planes_ref[d]
        t = acc * (hd ** -0.5 * LOG2E) + mb
        mx = jnp.max(t, axis=0, keepdims=True)
        p = jnp.exp2(t - mx)
        stats_ref[h:h + 1, :] = mx
        stats_ref[heads + h:heads + h + 1, :] = jnp.sum(p, axis=0, keepdims=True)
        pb = p.astype(BF16).astype(F32)
        for d in range(hd):
            r = 2 * heads + h * hd + d
            stats_ref[r:r + 1, :] = jnp.sum(pb * planes_ref[hd + d], axis=0, keepdims=True)


def col1_kernel(qtot_ref, fmask_ref, kv_ref, mask_ref, wq_ref, stats_ref, planes_ref, *, heads, hd):
    cnt = jnp.sum(fmask_ref[...], axis=0, keepdims=True).astype(F32)
    col_stats(qtot_ref[...], cnt, kv_ref, mask_ref, wq_ref, planes_ref, stats_ref, heads, hd)


def combine_stats(stats, heads, hd):
    gm = stats[0][0:heads]
    for st in stats[1:]:
        gm = jnp.maximum(gm, st[0:heads])
    tot = None
    wv = None
    for st in stats:
        f = jnp.exp2(st[0:heads] - gm)
        fx = jnp.concatenate([jnp.broadcast_to(f[h:h + 1], (hd, f.shape[1])) for h in range(heads)], axis=0)
        tot = f * st[heads:2 * heads] if tot is None else tot + f * st[heads:2 * heads]
        wv = fx * st[2 * heads:] if wv is None else wv + fx * st[2 * heads:]
    totx = jnp.concatenate([jnp.broadcast_to(tot[h:h + 1], (hd, tot.shape[1])) for h in range(heads)], axis=0)
    return wv / totx


def col2_kernel(stats_ref, g_ref, m1_ref, mask_ref, wout_ref, wac_ref, m2_ref, a_ref, c_ref, o_ref, wo_ref, as_ref, cs_ref, at_ref, *, heads, hd):
    seqs, chans, res = m1_ref.shape
    wide = wac_ref.shape[0] // 2
    wo_ref[...] = wout_ref[...].astype(F32).T.astype(BF16)
    o_ref[...] = combine_stats([stats_ref[d] for d in range(stats_ref.shape[0])], heads, hd)

    def body(it, _):
        s0 = it * 2
        ys = [(jax.nn.sigmoid(g_ref[s0 + u].astype(F32)) * o_ref[...]).astype(BF16) for u in range(2)]
        upd = mm(wo_ref[...], jnp.concatenate(ys, axis=1))
        lns = []
        for u in range(2):
            m2 = (m1_ref[s0 + u].astype(F32) + upd[:, u * res:(u + 1) * res]).astype(BF16)
            m2_ref[s0 + u] = m2
            lns.append(ln_rows(m2.astype(F32)))
        ac = mm(wac_ref[...], jnp.concatenate(lns, axis=1)).astype(BF16).astype(F32)
        for u in range(2):
            mrow = mask_ref[pl.ds(s0 + u, 1), :]
            as_ref[pl.ds((s0 + u) * wide, wide), :] = ac[0:wide, u * res:(u + 1) * res] * mrow
            cs_ref[pl.ds((s0 + u) * wide, wide), :] = ac[wide:, u * res:(u + 1) * res] * mrow
        return 0

    lax.fori_loop(0, seqs // 2, body, 0)

    def planes(e, _):
        c_ref[e] = cs_ref[pl.ds(e, seqs, stride=wide), :].astype(BF16)
        at_ref[pl.ds(e, res, stride=wide), :] = as_ref[pl.ds(e, seqs, stride=wide), :].T
        return 0

    lax.fori_loop(0, wide, planes, 0)
    a_ref[...] = at_ref[...].astype(BF16)


def dap_index(chip, core, chips):
    return lax.rem(chip + 2 * chips, chips) * 2 + core


def opm_kernel(a_ref, c_ref, z_ref, mask_ref, w_ref, out_ref, ap_ref, cp_ref, part_ref, xhi_ref, xlo_ref, wt_ref, w32_ref, cnt_ref, pos_ref, neg_ref, ex_send, ex_recv, send_sem, recv_sem, *, chips):
    me = lax.axis_index('dap')
    chip, core = me // 2, lax.rem(me, 2)
    wide, seqs, res = c_ref.shape
    rows = z_ref.shape[0]
    brow = rows * wide
    outc = w_ref.shape[1]
    partner = chip * 2 + 1 - core
    peer = {1: dap_index(chip + 1, core, chips), -1: dap_index(chip - 1, core, chips)}
    half_chips = chips // 2

    barrier = pltpu.get_barrier_semaphore()
    for dev in (partner, peer[1], peer[-1]):
        pl.semaphore_signal(barrier, inc=1, device_id={'dap': dev}, device_id_type=MESH)
    pl.semaphore_wait(barrier, 3)

    swaps = []
    for n, (src, dst) in enumerate(((a_ref.at[:, 1 - core], ap_ref), (c_ref, cp_ref))):
        cp = pltpu.make_async_remote_copy(src, dst, ex_send.at[n], ex_recv.at[n], device_id={'dap': partner}, device_id_type=MESH)
        cp.start()
        swaps.append(cp)

    w32_ref[...] = w_ref[...].astype(F32)
    per = 128 // wide
    for b in range(wide // per):
        cols = [w32_ref[pl.ds(b * per + f, wide, stride=wide), :] for f in range(per)]
        wt_ref[:, b * 128:(b + 1) * 128] = jnp.concatenate(cols, axis=0).T.astype(BF16)

    def count_step(n, acc):
        blk = mask_ref[pl.ds(n * 128, 128), :].astype(F32)
        return acc + mm(blk.T.astype(BF16), blk.astype(BF16))

    cnt_ref[...] = lax.fori_loop(0, mask_ref.shape[0] // 128, count_step, jnp.zeros((res, res), F32))

    for cp in swaps:
        cp.wait()

    def block(dest, slot):
        lhs = jnp.concatenate([a_ref[dest, core], ap_ref[dest]], axis=1)

        def outer(fp, _):
            f0 = fp * 2
            rhs = jnp.concatenate([
                jnp.concatenate([c_ref[f0], c_ref[f0 + 1]], axis=1),
                jnp.concatenate([cp_ref[f0], cp_ref[f0 + 1]], axis=1)], axis=0)
            o = mm(lhs, rhs)
            hi = o.astype(BF16)
            lo = (o - hi.astype(F32)).astype(BF16)
            for i in range(rows):
                for u in range(2):
                    r0 = pl.multiple_of((f0 + u) * wide, wide)
                    src = (slice(i * wide, (i + 1) * wide), slice(u * res, (u + 1) * res))
                    xhi_ref[i // 2, pl.ds(r0, wide), (i % 2) * res:(i % 2 + 1) * res] = hi[src]
                    xlo_ref[i // 2, pl.ds(r0, wide), (i % 2) * res:(i % 2 + 1) * res] = lo[src]
            return 0

        lax.fori_loop(0, wide // 2, outer, 0)

        def inner(n, _):
            part_ref[slot, n] = mm(wt_ref[...], xhi_ref[n]) + mm(wt_ref[...], xlo_ref[n])
            return 0

        lax.fori_loop(0, rows // 2, inner, 0)

    sends = []
    arrivals = {}
    bufs = {1: pos_ref, -1: neg_ref}
    hq = rows // 4

    def hops(d, half):
        return half_chips if (half == 1) == (d == 1) else half_chips - 1

    slot_of = {}
    nbuf = 2 * half_chips - 1

    def buf_index(d, half, k):
        return (k - 1) + (0 if (half == 1) == (d == 1) else half_chips)

    def message(d, half, k, slot):
        idx = buf_index(d, half, k)
        src = part_ref.at[slot, pl.ds(half * hq, hq)]
        cp = pltpu.make_async_remote_copy(src, bufs[d].at[idx], send_sem.at[(d + 1) // 2, idx], recv_sem.at[(d + 1) // 2, idx], device_id={'dap': peer[d]}, device_id_type=MESH)
        arrivals[(d, half, k)] = cp
        sends.append(cp)
        cp.start()

    def take(d, half, k, slot):
        arrivals[(d, half, k)].wait_recv()
        part_ref[slot, half * hq:(half + 1) * hq] += bufs[d][buf_index(d, half, k)]

    def relay(d, k, slot):
        for half in ((0, 1) if d == 1 else (1, 0)):
            if k < hops(d, half):
                take(d, half, k + 1, slot)
            if k <= hops(d, half):
                message(d, half, k, slot)

    def dest_of(d, k):
        return lax.rem(chip + d * k + 2 * chips, chips)

    far = half_chips
    block(dest_of(1, far), 0)
    message(1, 1, far, 0)
    message(-1, 0, far, 0)
    slot = 1
    pending = []
    for k in range(far - 1, 0, -1):
        for d in (1, -1):
            block(dest_of(d, k), slot)
            if k == far - 1:
                message(d, 0 if d == 1 else 1, k, slot)
                pending.append((d, slot))
            else:
                relay(d, k, slot)
            slot += 1
        if k == far - 1:
            for d, sl in pending:
                half = 1 if d == 1 else 0
                take(d, half, far, sl)
                message(d, half, k, sl)
    block(chip, slot)
    for half in (0, 1):
        for d in (1, -1):
            take(d, half, 1, slot)
    for n in range(rows // 2):
        pair = part_ref[slot, n]
        for u in range(2):
            i = n * 2 + u
            cnt = cnt_ref[pl.ds(me * rows + i, 1), :] + 1e-3
            upd = (pair[:, u * res:(u + 1) * res] / cnt).T
            out_ref[i] = (z_ref[i].astype(F32) + upd).astype(BF16)
    for cp in sends:
        cp.wait_send()


def vspec():
    return pl.BlockSpec(memory_space=VMEM)


def call(kernel, outs, n_in, scratch, name, cid=None, flops=10 ** 9):
    params = dict(vmem_limit_bytes=60 * 2 ** 20)
    if cid is not None:
        params.update(collective_id=cid, has_side_effects=True)
    return pl.pallas_call(
        kernel,
        out_shape=outs,
        in_specs=[vspec()] * n_in,
        out_specs=jax.tree.map(lambda _: vspec(), outs),
        scratch_shapes=scratch,
        compiler_params=pltpu.CompilerParams(**params),
        cost_estimate=pl.CostEstimate(flops=flops, bytes_accessed=10 ** 6, transcendentals=0),
        name=name,
    )


def sds(shape, dtype):
    return jax.ShapeDtypeStruct(shape, dtype)


def solution(mesh):
    ndap = mesh.shape['dap']
    chips = ndap // 2

    def evoformer_block(msa, pair_act, full_mask, res_mask, row_bias_w, row_qkvg_w, row_out_w, col_query_w, col_kv_w, col_gate_w, col_out_w, opm_proj_w, opm_out_w, start_bias_w, start_qkvg_w, start_out_w, end_bias_w, end_qkvg_w, end_out_w):
        seqs, res, chans = msa.shape
        rows = pair_act.shape[0]
        heads, hd = row_qkvg_w.shape[2], row_qkvg_w.shape[3]
        width = heads * hd
        wide = opm_proj_w.shape[2]
        outc = opm_out_w.shape[2]
        me = lax.axis_index('dap')
        mask = lax.dynamic_slice_in_dim(full_mask, me * seqs, seqs, axis=0).astype(F32)
        m_t = jnp.swapaxes(msa, 1, 2)
        wt = lambda w: w.reshape(w.shape[0], -1).T

        braw = call(bias_kernel, sds((rows * heads, res), F32), 2, [], 'row_bias')(pair_act, row_bias_w.T)
        braw = lax.all_gather(braw, 'dap', axis=0, tiled=True)

        wkvg = jnp.concatenate([wt(col_kv_w), wt(col_gate_w)], axis=0)
        m1, kv, g, qsum = call(
            functools.partial(row_kernel, heads=heads, hd=hd),
            [sds((seqs, chans, res), BF16), sds((seqs * 2 * hd, res), F32), sds((seqs, width, res), BF16), sds((chans, res), F32)], 6,
            [VMEM((res, heads * res), F32), VMEM((chans, width), BF16)], 'row_attention',
        )(m_t, braw, mask, wt(row_qkvg_w), row_out_w.reshape(width, chans), wkvg)

        qtot = lax.psum(qsum, 'dap')
        nstat = 2 * heads + width
        stats = call(
            functools.partial(col1_kernel, heads=heads, hd=hd),
            sds((nstat, res), F32), 5, [VMEM((2 * hd, seqs, res), F32)], 'col_stats',
        )(qtot, full_mask, kv, mask, wt(col_query_w))
        stats = lax.all_gather(stats, 'dap', axis=0)

        m2, a, c = call(
            functools.partial(col2_kernel, heads=heads, hd=hd),
            [sds((seqs, chans, res), BF16), sds((res * wide, seqs), BF16), sds((wide, seqs, res), BF16)], 6,
            [VMEM((width, res), F32), VMEM((chans, width), BF16), VMEM((seqs * wide, res), F32), VMEM((seqs * wide, res), F32), VMEM((res * wide, seqs), F32)], 'col_out',
        )(stats, g, m1, mask, col_out_w.reshape(width, chans), wt(opm_proj_w))
        msa_out = jnp.swapaxes(m2, 1, 2)

        npair = rows // 2
        nbuf = 2 * (chips // 2) - 1
        pair_act = call(
            functools.partial(opm_kernel, chips=chips),
            sds(pair_act.shape, BF16), 5,
            [VMEM((chips, rows * wide, seqs), BF16), VMEM((wide, seqs, res), BF16),
             VMEM((chips, npair, outc, 2 * res), F32),
             VMEM((npair, wide * wide, 2 * res), BF16), VMEM((npair, wide * wide, 2 * res), BF16),
             VMEM((outc, wide * wide), BF16), VMEM((wide * wide, outc), F32), VMEM((res, res), F32),
             VMEM((nbuf, npair // 2, outc, 2 * res), F32), VMEM((nbuf, npair // 2, outc, 2 * res), F32),
             pltpu.SemaphoreType.DMA((2,)), pltpu.SemaphoreType.DMA((2,)),
             pltpu.SemaphoreType.DMA((2, nbuf)), pltpu.SemaphoreType.DMA((2, nbuf))],
            'outer_mean', cid=1,
        )(a.reshape(chips, 2, rows * wide, seqs), c, pair_act, full_mask, opm_out_w.reshape(wide * wide, outc))

        pair_ln = layer_norm(pair_act)
        start_full = lax.all_gather(matmul_bf('ijc,ch->hij', pair_ln, start_bias_w), 'dap', axis=1, tiled=True)
        pair_act = triangle_rows(pair_act, pair_ln, start_full, res_mask, start_qkvg_w, start_out_w)

        pair_cols = lax.all_to_all(pair_act, 'dap', 1, 0, tiled=True)
        cols_ln = layer_norm(pair_cols)
        end_full = lax.all_gather(matmul_bf('ijc,ch->hji', cols_ln, end_bias_w), 'dap', axis=1, tiled=True)
        pair_cols = triangle_cols(pair_cols, cols_ln, end_full, res_mask, end_qkvg_w, end_out_w)
        pair_out = lax.all_to_all(pair_cols, 'dap', 0, 1, tiled=True)
        return msa_out, pair_out

    row_spec = P(('data', 'dap'), None, None)
    in_specs = (row_spec, row_spec, P('data', None), P('data')) + (P(),) * 15
    return jax.shard_map(evoformer_block, mesh=mesh, in_specs=in_specs, out_specs=(row_spec, row_spec), check_vma=False)
```

time: 462 us -> 423 us (0.916); the launches traced: 456 us -> 423 us
  Pallas kernels: 0 us -> 249 us
  waiting for transfers between devices: 137 us -> 0 us
  matrix products: 118 us -> 13 us
  blocking collectives: 97.3 us -> 153 us
  local copies, waits for them, and re-layouts: 52.1 us -> 2 us
  starting transfers between devices: 23.4 us -> 0 us
  between operations: 14.9 us -> 0.9 us
  other arithmetic: 13.4 us -> 5.26 us
    pallas_call x0 -> x5, Pallas kernels: none -> 249 us  [the longest x1 151 us: evoformer_block(): call(functools.partial(row_kernel, heads=heads, hd=hd), [sds((seqs, chans...]
    all_gather x1 -> x0, waiting for transfers between devices: 91.3 us -> none  [evoformer_block(): right_full = lax.all_gather(projected[1], 'dap', axis=1, tiled=True)]
    all_to_all x4 -> x0, waiting for transfers between devices: 45.8 us -> none  [the longest x1 45.8 us: evoformer_block(): value_a8 = lax.all_to_all(value_a7, 'dap', 1, 0, tiled=True)]
    all_gather x1, blocking collectives: 58 us -> 14.9 us  [evoformer_block(): lax.all_gather(matmul_bf('ijc,ch->hji', cols_ln, end_bias_w), 'dap', axis...]
    psum x0 -> x1, blocking collectives: none -> 43 us  [evoformer_block(): qtot = lax.psum(qsum, 'dap')]
    sub x2 -> x0, matrix products: 34.9 us -> none  [the longest x1 33 us: row_attention(): attn_probs = jax.nn.softmax(logits, axis=-1).astype(jnp.bfloat16)]
    dot_general x10 -> x4, matrix products: 36.5 us -> 4.03 us  [matmul_bf(): jnp.einsum(einsum_form, left_arr, right_arr, preferred_element_type=jnp.f...]
    all_to_all x0 -> x2, blocking collectives: none -> 31.7 us  [the longest x1 16.3 us: evoformer_block(): pair_out = lax.all_to_all(pair_cols, 'dap', 0, 1, tiled=True)]
  transfers between devices with their start and end apart: 5 -> 0, of which waited for: 2 -> 0; matrix products, arithmetic and copies ran while one was open for 8% -> 0% of each run, Pallas kernels for 0% -> 0%
where the time goes in v1:
time: 423 us
  Pallas kernels  249 us (59%)
  blocking collectives  153 us (36%)
  matrix products  13 us (3%)
  other arithmetic  5.26 us (1%)
    pallas_call x1, Pallas kernels, evoformer_block(): call(functools.partial(row_kernel, heads=heads, hd=hd), [sds((seqs, chans...  151 us
    pallas_call x1, Pallas kernels, evoformer_block(): call(functools.partial(opm_kernel, chips=chips), sds(pair_act.shape, BF16...  59.2 us
    psum x1, blocking collectives, evoformer_block(): qtot = lax.psum(qsum, 'dap')  43 us
    pallas_call x1, Pallas kernels, evoformer_block(): call(functools.partial(col2_kernel, heads=heads, hd=hd), [sds((seqs, chan...  33 us
    all_gather x1, blocking collectives, evoformer_block(): braw = lax.all_gather(braw, 'dap', axis=0, tiled=True)  24.1 us
    all_gather x1, blocking collectives, evoformer_block(): stats = lax.all_gather(stats, 'dap', axis=0)  20.2 us
    all_gather x1, blocking collectives, evoformer_block(): lax.all_gather(matmul_bf('ijc,ch->hij', pair_ln, start_bias_w), 'dap', ax...  18.9 us
    all_to_all x1, blocking collectives, evoformer_block(): pair_out = lax.all_to_all(pair_cols, 'dap', 0, 1, tiled=True)  16.3 us

profile of v1, /device:TPU:21, one launch (start us, length us, event | category | flops | bytes accessed | tf_op | source)
XLA Modules:
  0.0 422.8 jit_solution(7200960873791949265)
XLA Ops:
  0.7 2.1 row_bias.1
  2.8 24.1 %all_gather.15.braw_ref = f32[1024,128]{1,0:T(8,128)} all-gather(f32[64,128]{1,0:T(8,128)} %row_bias.1), channel_id=1, replica_groups=mesh['data'=4,'dap'=16] {'dap'}, dimensions={0}, use_global_device_ids=true | all-gather | bytes 557056 | tf_op jit(solution)/shard_map/all_gather | solution.py:411
  26.9 1.5 dynamic-slice_convert_fusion.mask_ref
  28.3 0.6 pad_maximum_fusion.wkvg_ref
  28.9 150.8 %row_attention.1 = (bf16[128,64,128]{2,1,0:T(8,128)(2,1)}, f32[2048,128]{1,0:T(8,128)}, bf16[128,64,128]{2,1,0:T(8,128)(2,1)}, f32[64,128]{1,0:T(8,128)}) custom-call(bf16[128,64,128]{2,1,0:T(8,128)(2,1)} %bitcast.194, f32[1024,128]{1,0:T(8,128)} %all_gather.15.braw_ref, f32[128,128]{1,0:T(8,128)} %dynamic-slice_convert_fusion.mask_ref, ...), custom_call_target="tpu_custom_call" | custom-call | flops 1000000000 | bytes 1000000 | tf_op jit(solution)/shard_map/row_attention/pallas_call | solution.py:414
  179.7 43.0 %psum.7.qtot_ref = f32[64,128]{1,0:T(8,128)} all-reduce(f32[64,128]{1,0:T(8,128)} %get-tuple-element.9), channel_id=1, replica_groups=mesh['data'=4,'dap'=16] {'dap'}, use_global_device_ids=true, to_apply=%region_0.0 | all-reduce | flops 8192 | bytes 65536 | tf_op jit(solution)/shard_map/psum | solution.py:420
  222.7 3.7 col_stats.1
  226.4 20.2 %all-gather = f32[1280,128]{1,0:T(8,128)} all-gather(f32[80,128]{1,0:T(8,128)} %col_stats.1), channel_id=2, replica_groups=mesh['data'=4,'dap'=16] {'dap'}, dimensions={0}, use_global_device_ids=true | all-gather | bytes 696320 | tf_op jit(solution)/shard_map/all_gather | solution.py:426
  246.6 33.0 %col_out.1 = (bf16[128,64,128]{2,1,0:T(8,128)(2,1)}, bf16[4096,128]{1,0:T(8,128)(2,1)}, bf16[32,128,128]{2,1,0:T(8,128)(2,1)}) custom-call(f32[16,80,128]{2,1,0:T(8,128)} %bitcast.185, bf16[128,64,128]{2,1,0:T(8,128)(2,1)} %get-tuple-element.11.g_ref, bf16[128,64,128]{2,1,0:T(8,128)(2,1)} %get-tuple-element.12.m1_ref, ...), custom_call_target="tpu_custom_call" | custom-call | flops 1000000000 | bytes 1000000 | tf_op jit(solution)/shard_map/col_out/pallas_call | solution.py:428
  279.6 59.2 %outer_mean.1 = bf16[8,128,128]{2,1,0:T(8,128)(2,1)} custom-call(bf16[8,2,256,128]{3,2,1,0:T(8,128)(2,1)} %bitcast.187, bf16[32,128,128]{2,1,0:T(8,128)(2,1)} %get-tuple-element.15.c_ref, bf16[8,128,128]{2,1,0:T(8,128)(2,1)} %z_ref.3, s32[2048,128]{1,0:T(8,128)} %mask_ref.1, bf16[1024,128]{1,0:T(8,128)(2,1)} %bitcast.189), custom_call_target="tpu_custom_call" | custom-call | flops 1000000000 | bytes 1000000 | tf_op jit(solution)/shard_map/outer_mean/pallas_call | solution.py:437
  338.9 1.1 convert_reduce_fusion
  340.0 1.3 fusion.24
  341.3 1.6 fusion.4
  342.9 1.4 fusion.14
  344.3 18.9 %all_gather.18 = bf16[4,128,128]{2,0,1:T(4,128)(2,1)S(1)} all-gather(bf16[4,8,128]{2,0,1:T(4,128)(2,1)S(1)} %fusion.14), channel_id=1, replica_groups=mesh['data'=4,'dap'=16] {'dap'}, dimensions={1}, use_global_device_ids=true | all-gather | bytes 139264 | tf_op jit(solution)/shard_map/all_gather | solution.py:451
  363.5 2.3 fusion.64
  365.8 2.2 fusion.13
  368.2 15.4 %all_to_all.27 = bf16[8,128,128]{2,0,1:T(8,128)(2,1)S(1)} all-to-all(bf16[8,128,128]{2,0,1:T(8,128)(2,1)S(1)} %copy.46), channel_id=1, replica_groups=mesh['data'=4,'dap'=16] {'dap'}, dimensions={1} | all-to-all | bytes 524288 | tf_op jit(solution)/shard_map/all_to_all | solution.py:454
  384.9 0.6 fusion.5
  386.0 14.9 %all_gather.19 = bf16[4,128,128]{2,0,1:T(4,128)(2,1)S(1)} all-gather(bf16[4,8,128]{2,0,1:T(4,128)(2,1)S(1)} %fusion.15), channel_id=1, replica_groups=mesh['data'=4,'dap'=16] {'dap'}, dimensions={1}, use_global_device_ids=true | all-gather | bytes 139264 | tf_op jit(solution)/shard_map/all_gather | solution.py:456
  401.1 2.3 fusion.65
  403.4 2.2 fusion.12
  405.8 16.3 %all_to_all.28 = bf16[128,8,128]{2,1,0:T(8,128)(2,1)S(1)} all-to-all(bf16[128,8,128]{2,1,0:T(8,128)(2,1)S(1)} %copy.57), channel_id=1, replica_groups=mesh['data'=4,'dap'=16] {'dap'}, dimensions={0} | all-to-all | bytes 524288 | tf_op jit(solution)/shard_map/all_to_all | solution.py:458
  422.0 0.8 copy.77
  (42 shorter events, 2.5 us)
Async XLA Ops:
  0.6 340.7 %copy-start = (bf16[128,4,4,32]{0,3,2,1:T(8,128)(2,1)S(1)}, bf16[128,4,4,32]{0,3,2,1:T(8,128)(2,1)}, u32[]{:S(2)}) copy-start(bf16[128,4,4,32]{0,3,2,1:T(8,128)(2,1)} %param.33) | copy-start | bytes 393220
  0.7 27.7 %copy-start.3 = (bf16[64,8,8]{0,2,1:T(8,128)(2,1)S(1)}, bf16[64,8,8]{0,2,1:T(8,128)(2,1)}, u32[]{:S(2)}) copy-start(bf16[64,8,8]{0,2,1:T(8,128)(2,1)} %param.28) | copy-start | bytes 24580
  0.7 27.7 %copy-start.4 = (bf16[64,2,8]{0,2,1:T(8,128)(2,1)S(1)}, bf16[64,2,8]{0,2,1:T(8,128)(2,1)}, u32[]{:S(2)}) copy-start(bf16[64,2,8]{0,2,1:T(8,128)(2,1)} %param.27) | copy-start | bytes 6148
  279.6 63.3 %copy-start.8 = (bf16[128,4]{0,1:T(4,128)(2,1)S(1)}, bf16[128,4]{0,1:T(4,128)(2,1)}, u32[]{:S(2)}) copy-start(bf16[128,4]{0,1:T(4,128)(2,1)} %param.32) | copy-start | bytes 3076
  338.8 24.6 %copy-start.9 = (s32[128]{0:T(128)S(1)}, s32[128]{0:T(128)}, u32[]{:S(2)}) copy-start(s32[128]{0:T(128)} %param.22) | copy-start | bytes 1540
  363.4 2.3 copy-start.1
  363.4 2.3 copy-start.6
  368.0 17.0 %copy-start.2 = (bf16[128,4,4,32]{0,3,2,1:T(8,128)(2,1)S(1)}, bf16[128,4,4,32]{0,3,2,1:T(8,128)(2,1)}, u32[]{:S(2)}) copy-start(bf16[128,4,4,32]{0,3,2,1:T(8,128)(2,1)} %param.36) | copy-start | bytes 393220
  383.6 1.9 copy-start.5
  401.0 2.3 copy-start.7

commit v2 on v1

--- a/solution.py
+++ b/solution.py
@@ -91,66 +91,125 @@
         out_ref[r * heads:(r + 1) * heads, :] = mm_nt(w_ref[...], ln).astype(BF16).astype(F32)
 
 
-def row_kernel(m_ref, braw_ref, mask_ref, wqkvg_ref, wout_ref, wkvg_ref, m1_ref, kv_ref, g_ref, qsum_ref, bias_ref, wo_ref, *, heads, hd):
+def row_kernel(m_ref, braw_ref, mask_ref, wqkvg_ref, wout_ref, wkvg_ref, m1_ref, kv_ref, g_ref, qsum_ref, bias_ref, wo_ref, q_ref, kt_ref, v_ref, y_ref, s0_ref, s1_ref, p0_ref, p1_ref, l0_ref, l1_ref, *, heads, hd):
     seqs, chans, res = m_ref.shape
     width = heads * hd
-    scale2 = hd ** -0.5 * LOG2E
     wo_ref[...] = wout_ref[...].astype(F32).T.astype(BF16)
     for h in range(heads):
         plane = braw_ref[pl.ds(h, res, stride=heads), :]
         bias_ref[:, h * res:(h + 1) * res] = plane.T * LOG2E
     qsum_ref[...] = jnp.zeros_like(qsum_ref)
+    row_project(m_ref, mask_ref, wqkvg_ref, q_ref, kt_ref, v_ref, g_ref, heads, hd)
+    row_attend(bias_ref, q_ref, kt_ref, v_ref, g_ref, y_ref, s0_ref, s1_ref, p0_ref, p1_ref, l0_ref, l1_ref, heads, hd)
+    row_finish(m_ref, mask_ref, wo_ref, wkvg_ref, y_ref, m1_ref, kv_ref, g_ref, qsum_ref, hd)
+
+
+def row_project(m_ref, mask_ref, wqkvg_ref, q_ref, kt_ref, v_ref, g_ref, heads, hd, unroll=8):
+    seqs, chans, res = m_ref.shape
+    width = heads * hd
+    aug = kt_ref.shape[2] - width
     terms = bf16_split(1e4 / hd ** -0.5, 3)
-    rows16 = lax.broadcasted_iota(jnp.int32, (16, res), 0)
+    rowi = lax.broadcasted_iota(jnp.int32, (aug, res), 0)
+    mvec = jnp.where(rowi == 0, terms[0], jnp.where(rowi == 1, terms[1], jnp.where(rowi == 2, terms[2], 0.0)))
+
+    def body(it, _):
+        for n in range(unroll // 2):
+            s0 = it * unroll + n * 2
+            lns = [ln_rows(m_ref[s0 + u].astype(F32)) for u in range(2)]
+            proj = mm(wqkvg_ref[...], jnp.concatenate(lns, axis=1))
+            for u in range(2):
+                cols = slice(u * res, (u + 1) * res)
+                s = s0 + u
+                q_ref[s] = proj[0:width, cols].astype(BF16)
+                mrow = mask_ref[pl.ds(s, 1), :] - 1.0
+                k = proj[width:2 * width, cols].astype(BF16).astype(F32)
+                kt_ref[s] = jnp.concatenate([k, mrow * mvec], axis=0).T.astype(BF16)
+                v_ref[s] = proj[2 * width:3 * width, cols].astype(BF16)
+                g_ref[s] = proj[3 * width:, cols].astype(BF16)
+        return 0
+
+    lax.fori_loop(0, seqs // unroll, body, 0)
+
+
+def row_attend(bias_ref, q_ref, kt_ref, v_ref, g_ref, y_ref, s0_ref, s1_ref, p0_ref, p1_ref, l0_ref, l1_ref, heads, hd):
+    seqs, width, res = q_ref.shape
+    scale2 = hd ** -0.5 * LOG2E
+    npairs = heads // 2
+    aug = kt_ref.shape[2] - width
+    rows16 = lax.broadcasted_iota(jnp.int32, (2 * hd, res), 0)
     first = rows16 < hd
-    mvec = jnp.where(rows16 == 0, terms[0], jnp.where(rows16 == 1, terms[1], jnp.where(rows16 == 2, terms[2], 0.0)))
-    zero16 = jnp.zeros((16, res), BF16)
-    one16 = jnp.ones((16, res), BF16)
-    npairs = heads // 2
-
-    def attend(qkvg, mrow):
-        q = qkvg[0:width]
-        kaug = jnp.concatenate([qkvg[width:2 * width], (mrow - 1.0) * mvec], axis=0)
-        kt = kaug.T.astype(BF16)
-        vT = qkvg[2 * width:3 * width].astype(BF16)
+    zero16 = jnp.zeros((2 * hd, res), BF16)
+    ones = jnp.ones((aug, res), BF16)
+
+    def scores(s, s_ref):
+        s = jnp.minimum(s, seqs - 1)
+        kt = kt_ref[s]
+        for t in range(npairs):
+            q16 = q_ref[s, t * 2 * hd:(t + 1) * 2 * hd]
+            qa = jnp.where(first, q16, zero16)
+            qb = jnp.where(first, zero16, q16)
+            left = jnp.concatenate([zero16] * t + [qa] + [zero16] * (npairs - 1 - t) + [ones], axis=0)
+            right = jnp.concatenate([zero16] * t + [qb] + [zero16] * (npairs - 1 - t) + [ones], axis=0)
+            s_ref[:, t * 2 * res:(t + 1) * 2 * res] = mm(kt, jnp.concatenate([left, right], axis=1))
+
+    def soft(s_ref, p_ref, l_ref):
+        for h in range(heads):
+            cols = slice(h * res, (h + 1) * res)
+            x = s_ref[:, cols] * scale2 + bias_ref[:, cols]
+            p = jnp.exp2(x - jnp.max(x, axis=0, keepdims=True))
+            l_ref[0:1, cols] = jnp.sum(p, axis=0, keepdims=True)
+            p_ref[:, cols] = p.astype(BF16)
+
+    def values(s, p_ref, l_ref):
+        s = jnp.maximum(s, 0)
         outs = []
         for t in range(npairs):
-            q16 = q[t * 16:(t + 1) * 16]
-            qa = jnp.where(first, q16, 0.0).astype(BF16)
-            qb = jnp.where(first, 0.0, q16).astype(BF16)
-            left = jnp.concatenate([zero16] * t + [qa] + [zero16] * (npairs - 1 - t) + [one16], axis=0)
-            right = jnp.concatenate([zero16] * t + [qb] + [zero16] * (npairs - 1 - t) + [one16], axis=0)
-            s = mm(kt, jnp.concatenate([left, right], axis=1))
-            s = s * scale2 + bias_ref[:, t * 2 * res:(t + 1) * 2 * res]
-            p = jnp.exp2(s - jnp.max(s, axis=0, keepdims=True))
-            inv = 1.0 / jnp.sum(p, axis=0, keepdims=True)
-            o = mm(vT[t * 16:(t + 1) * 16], p.astype(BF16)) * inv
-            outs += [o[0:hd, 0:res], o[hd:2 * hd, res:2 * res]]
+            cols = slice(t * 2 * res, (t + 1) * 2 * res)
+            o = mm(v_ref[s, t * 2 * hd:(t + 1) * 2 * hd], p_ref[:, cols])
+            inv = 1.0 / l_ref[0:1, cols]
+            outs += [o[0:hd, 0:res] * inv[:, 0:res], o[hd:2 * hd, res:2 * res] * inv[:, res:2 * res]]
         att = jnp.concatenate(outs, axis=0)
-        return (jax.nn.sigmoid(qkvg[3 * width:4 * width]) * att).astype(BF16)
+        y_ref[s] = (jax.nn.sigmoid(g_ref[s].astype(F32)) * att).astype(BF16)
+
+    scores(0, s0_ref)
 
     def body(it, _):
-        s0 = it * 2
-        xs = [m_ref[s0 + u].astype(F32) for u in range(2)]
-        lns = [ln_rows(x) for x in xs]
-        proj = mm(wqkvg_ref[...], jnp.concatenate(lns, axis=1)).astype(BF16).astype(F32)
-        mrows = [mask_ref[pl.ds(s0 + u, 1), :] for u in range(2)]
-        ys = [attend(proj[:, u * res:(u + 1) * res], mrows[u]) for u in range(2)]
-        upd = mm(wo_ref[...], jnp.concatenate(ys, axis=1))
-        ln1 = []
-        for u in range(2):
-            m1 = (xs[u] + upd[:, u * res:(u + 1) * res]).astype(BF16)
-            m1_ref[s0 + u] = m1
-            l1 = ln_rows(m1.astype(F32))
-            qsum_ref[...] += l1.astype(F32) * mrows[u]
-            ln1.append(l1)
-        kvg = mm(wkvg_ref[...], jnp.concatenate(ln1, axis=1)).astype(BF16)
-        for u in range(2):
-            kv_ref[pl.ds((s0 + u) * 2 * hd, 2 * hd), :] = kvg[0:2 * hd, u * res:(u + 1) * res].astype(F32)
-            g_ref[s0 + u] = kvg[2 * hd:, u * res:(u + 1) * res]
+        s = it * 2
+        values(s - 1, p1_ref, l1_ref)
+        scores(s + 1, s1_ref)
+        soft(s0_ref, p0_ref, l0_ref)
+        values(s, p0_ref, l0_ref)
+        scores(s + 2, s0_ref)
+        soft(s1_ref, p1_ref, l1_ref)
         return 0
 
     lax.fori_loop(0, seqs // 2, body, 0)
+    values(seqs - 1, p1_ref, l1_ref)
+
+
+def row_finish(m_ref, mask_ref, wo_ref, wkvg_ref, y_ref, m1_ref, kv_ref, g_ref, qsum_ref, hd, unroll=8):
+    seqs, chans, res = m_ref.shape
+
+    def body(it, _):
+        acc = jnp.zeros((chans, res), F32)
+        for n in range(unroll // 2):
+            s0 = it * unroll + n * 2
+            upd = mm(wo_ref[...], jnp.concatenate([y_ref[s0], y_ref[s0 + 1]], axis=1))
+            ln1 = []
+            for u in range(2):
+                m1 = (m_ref[s0 + u].astype(F32) + upd[:, u * res:(u + 1) * res]).astype(BF16)
+                m1_ref[s0 + u] = m1
+                l1 = ln_rows(m1.astype(F32))
+                acc = acc + l1.astype(F32) * mask_ref[pl.ds(s0 + u, 1), :]
+                ln1.append(l1)
+            kvg = mm(wkvg_ref[...], jnp.concatenate(ln1, axis=1)).astype(BF16)
+            for u in range(2):
+                kv_ref[pl.ds((s0 + u) * 2 * hd, 2 * hd), :] = kvg[0:2 * hd, u * res:(u + 1) * res].astype(F32)
+                g_ref[s0 + u] = kvg[2 * hd:, u * res:(u + 1) * res]
+        qsum_ref[...] += acc
+        return 0
+
+    lax.fori_loop(0, seqs // unroll, body, 0)
 
 
 def col_stats(qtot, cnt, kv_ref, mask_ref, wq_ref, planes_ref, stats_ref, heads, hd):
@@ -201,8 +260,7 @@
     wo_ref[...] = wout_ref[...].astype(F32).T.astype(BF16)
     o_ref[...] = combine_stats([stats_ref[d] for d in range(stats_ref.shape[0])], heads, hd)
 
-    def body(it, _):
-        s0 = it * 2
+    def pair(s0):
         ys = [(jax.nn.sigmoid(g_ref[s0 + u].astype(F32)) * o_ref[...]).astype(BF16) for u in range(2)]
         upd = mm(wo_ref[...], jnp.concatenate(ys, axis=1))
         lns = []
@@ -215,9 +273,13 @@
             mrow = mask_ref[pl.ds(s0 + u, 1), :]
             as_ref[pl.ds((s0 + u) * wide, wide), :] = ac[0:wide, u * res:(u + 1) * res] * mrow
             cs_ref[pl.ds((s0 + u) * wide, wide), :] = ac[wide:, u * res:(u + 1) * res] * mrow
+
+    def body(it, _):
+        for n in range(4):
+            pair(it * 8 + n * 2)
         return 0
 
-    lax.fori_loop(0, seqs // 2, body, 0)
+    lax.fori_loop(0, seqs // 8, body, 0)
 
     def planes(e, _):
         c_ref[e] = cs_ref[pl.ds(e, seqs, stride=wide), :].astype(BF16)
@@ -414,7 +476,10 @@
         m1, kv, g, qsum = call(
             functools.partial(row_kernel, heads=heads, hd=hd),
             [sds((seqs, chans, res), BF16), sds((seqs * 2 * hd, res), F32), sds((seqs, width, res), BF16), sds((chans, res), F32)], 6,
-            [VMEM((res, heads * res), F32), VMEM((chans, width), BF16)], 'row_attention',
+            [VMEM((res, heads * res), F32), VMEM((chans, width), BF16),
+             VMEM((seqs, width, res), BF16), VMEM((seqs, res, width + 16), BF16), VMEM((seqs, width, res), BF16), VMEM((seqs, width, res), BF16),
+             VMEM((res, heads * res), F32), VMEM((res, heads * res), F32), VMEM((res, heads * res), BF16), VMEM((res, heads * res), BF16),
+             VMEM((8, heads * res), F32), VMEM((8, heads * res), F32)], 'row_attention',
         )(m_t, braw, mask, wt(row_qkvg_w), row_out_w.reshape(width, chans), wkvg)
 
         qtot = lax.psum(qsum, 'dap')

time: 423 us -> 305 us (0.72)
  Pallas kernels: 249 us -> 131 us
    pallas_call x1, Pallas kernels: 151 us -> 47.1 us  [evoformer_block(): call(functools.partial(row_kernel, heads=heads, hd=hd), [sds((seqs, chans...]
    pallas_call x1, Pallas kernels: 33 us -> 18.7 us  [evoformer_block(): call(functools.partial(col2_kernel, heads=heads, hd=hd), [sds((seqs, chan...]
where the time goes in v2:
time: 305 us
  blocking collectives  153 us (50%)
  Pallas kernels  131 us (43%)
  matrix products  13 us (4%)
  other arithmetic  5.26 us (2%)
    pallas_call x1, Pallas kernels, evoformer_block(): call(functools.partial(opm_kernel, chips=chips), sds(pair_act.shape, BF16...  59.2 us
    pallas_call x1, Pallas kernels, evoformer_block(): call(functools.partial(row_kernel, heads=heads, hd=hd), [sds((seqs, chans...  47.1 us
    psum x1, blocking collectives, evoformer_block(): qtot = lax.psum(qsum, 'dap')  43 us
    all_gather x1, blocking collectives, evoformer_block(): braw = lax.all_gather(braw, 'dap', axis=0, tiled=True)  24.1 us
    all_gather x1, blocking collectives, evoformer_block(): stats = lax.all_gather(stats, 'dap', axis=0)  20.2 us
    all_gather x1, blocking collectives, evoformer_block(): lax.all_gather(matmul_bf('ijc,ch->hij', pair_ln, start_bias_w), 'dap', ax...  18.9 us
    pallas_call x1, Pallas kernels, evoformer_block(): call(functools.partial(col2_kernel, heads=heads, hd=hd), [sds((seqs, chan...  18.7 us
    all_to_all x1, blocking collectives, evoformer_block(): pair_out = lax.all_to_all(pair_cols, 'dap', 0, 1, tiled=True)  16.3 us

profile of v2, /device:TPU:21, one launch (start us, length us, event | category | flops | bytes accessed | tf_op | source)
XLA Modules:
  0.0 304.7 jit_solution(1506809461579955212)
XLA Ops:
  0.7 2.1 row_bias.1
  2.8 24.1 %all_gather.15.braw_ref = f32[1024,128]{1,0:T(8,128)} all-gather(f32[64,128]{1,0:T(8,128)} %row_bias.1), channel_id=1, replica_groups=mesh['data'=4,'dap'=16] {'dap'}, dimensions={0}, use_global_device_ids=true | all-gather | bytes 557056 | tf_op jit(solution)/shard_map/all_gather | solution.py:473
  26.9 1.5 dynamic-slice_convert_fusion.mask_ref
  28.3 0.6 pad_maximum_fusion.wkvg_ref
  28.9 47.1 %row_attention.1 = (bf16[128,64,128]{2,1,0:T(8,128)(2,1)}, f32[2048,128]{1,0:T(8,128)}, bf16[128,64,128]{2,1,0:T(8,128)(2,1)}, f32[64,128]{1,0:T(8,128)}) custom-call(bf16[128,64,128]{2,1,0:T(8,128)(2,1)} %bitcast.194, f32[1024,128]{1,0:T(8,128)} %all_gather.15.braw_ref, f32[128,128]{1,0:T(8,128)} %dynamic-slice_convert_fusion.mask_ref, ...), custom_call_target="tpu_custom_call" | custom-call | flops 1000000000 | bytes 1000000 | tf_op jit(solution)/shard_map/row_attention/pallas_call | solution.py:476
  76.0 43.0 %psum.7.qtot_ref = f32[64,128]{1,0:T(8,128)} all-reduce(f32[64,128]{1,0:T(8,128)} %get-tuple-element.9), channel_id=1, replica_groups=mesh['data'=4,'dap'=16] {'dap'}, use_global_device_ids=true, to_apply=%region_0.0 | all-reduce | flops 8192 | bytes 65536 | tf_op jit(solution)/shard_map/psum | solution.py:485
  119.0 3.7 %col_stats.1 = f32[80,128]{1,0:T(8,128)} custom-call(f32[64,128]{1,0:T(8,128)} %psum.7.qtot_ref, s32[2048,128]{1,0:T(8,128)} %mask_ref.1, f32[2048,128]{1,0:T(8,128)} %get-tuple-element.10.kv_ref, f32[128,128]{1,0:T(8,128)} %dynamic-slice_convert_fusion.mask_ref, bf16[64,64]{1,0:T(8,128)(2,1)} %bitcast.198), custom_call_target="tpu_custom_call" | custom-call | flops 1000000000 | bytes 1000000 | tf_op jit(solution)/shard_map/col_stats/pallas_call | solution.py:487
  122.7 20.2 %all-gather = f32[1280,128]{1,0:T(8,128)} all-gather(f32[80,128]{1,0:T(8,128)} %col_stats.1), channel_id=2, replica_groups=mesh['data'=4,'dap'=16] {'dap'}, dimensions={0}, use_global_device_ids=true | all-gather | bytes 696320 | tf_op jit(solution)/shard_map/all_gather | solution.py:491
  142.8 18.7 %col_out.1 = (bf16[128,64,128]{2,1,0:T(8,128)(2,1)}, bf16[4096,128]{1,0:T(8,128)(2,1)}, bf16[32,128,128]{2,1,0:T(8,128)(2,1)}) custom-call(f32[16,80,128]{2,1,0:T(8,128)} %bitcast.185, bf16[128,64,128]{2,1,0:T(8,128)(2,1)} %get-tuple-element.11.g_ref, bf16[128,64,128]{2,1,0:T(8,128)(2,1)} %get-tuple-element.12.m1_ref, ...), custom_call_target="tpu_custom_call" | custom-call | flops 1000000000 | bytes 1000000 | tf_op jit(solution)/shard_map/col_out/pallas_call | solution.py:493
  161.6 59.2 %outer_mean.1 = bf16[8,128,128]{2,1,0:T(8,128)(2,1)} custom-call(bf16[8,2,256,128]{3,2,1,0:T(8,128)(2,1)} %bitcast.187, bf16[32,128,128]{2,1,0:T(8,128)(2,1)} %get-tuple-element.15.c_ref, bf16[8,128,128]{2,1,0:T(8,128)(2,1)} %z_ref.3, s32[2048,128]{1,0:T(8,128)} %mask_ref.1, bf16[1024,128]{1,0:T(8,128)(2,1)} %bitcast.189), custom_call_target="tpu_custom_call" | custom-call | flops 1000000000 | bytes 1000000 | tf_op jit(solution)/shard_map/outer_mean/pallas_call | solution.py:502
  220.8 1.1 convert_reduce_fusion
  221.9 1.3 fusion.24
  223.3 1.6 fusion.4
  224.9 1.4 fusion.14
  226.3 18.9 %all_gather.18 = bf16[4,128,128]{2,0,1:T(4,128)(2,1)S(1)} all-gather(bf16[4,8,128]{2,0,1:T(4,128)(2,1)S(1)} %fusion.14), channel_id=1, replica_groups=mesh['data'=4,'dap'=16] {'dap'}, dimensions={1}, use_global_device_ids=true | all-gather | bytes 139264 | tf_op jit(solution)/shard_map/all_gather | solution.py:516
  245.4 2.3 fusion.64
  247.7 2.2 fusion.13
  250.1 15.4 %all_to_all.27 = bf16[8,128,128]{2,0,1:T(8,128)(2,1)S(1)} all-to-all(bf16[8,128,128]{2,0,1:T(8,128)(2,1)S(1)} %copy.46), channel_id=1, replica_groups=mesh['data'=4,'dap'=16] {'dap'}, dimensions={1} | all-to-all | bytes 524288 | tf_op jit(solution)/shard_map/all_to_all | solution.py:519
  266.9 0.6 fusion.5
  267.9 14.9 %all_gather.19 = bf16[4,128,128]{2,0,1:T(4,128)(2,1)S(1)} all-gather(bf16[4,8,128]{2,0,1:T(4,128)(2,1)S(1)} %fusion.15), channel_id=1, replica_groups=mesh['data'=4,'dap'=16] {'dap'}, dimensions={1}, use_global_device_ids=true | all-gather | bytes 139264 | tf_op jit(solution)/shard_map/all_gather | solution.py:521
  283.0 2.3 fusion.65
  285.3 2.2 fusion.12
  287.7 16.3 %all_to_all.28 = bf16[128,8,128]{2,1,0:T(8,128)(2,1)S(1)} all-to-all(bf16[128,8,128]{2,1,0:T(8,128)(2,1)S(1)} %copy.57), channel_id=1, replica_groups=mesh['data'=4,'dap'=16] {'dap'}, dimensions={0} | all-to-all | bytes 524288 | tf_op jit(solution)/shard_map/all_to_all | solution.py:523
  303.9 0.8 copy.77
  (42 shorter events, 2.5 us)
Async XLA Ops:
  0.6 222.6 %copy-start = (bf16[128,4,4,32]{0,3,2,1:T(8,128)(2,1)S(1)}, bf16[128,4,4,32]{0,3,2,1:T(8,128)(2,1)}, u32[]{:S(2)}) copy-start(bf16[128,4,4,32]{0,3,2,1:T(8,128)(2,1)} %param.33) | copy-start | bytes 393220
  0.7 27.7 %copy-start.3 = (bf16[64,8,8]{0,2,1:T(8,128)(2,1)S(1)}, bf16[64,8,8]{0,2,1:T(8,128)(2,1)}, u32[]{:S(2)}) copy-start(bf16[64,8,8]{0,2,1:T(8,128)(2,1)} %param.28) | copy-start | bytes 24580
  0.7 27.7 %copy-start.4 = (bf16[64,2,8]{0,2,1:T(8,128)(2,1)S(1)}, bf16[64,2,8]{0,2,1:T(8,128)(2,1)}, u32[]{:S(2)}) copy-start(bf16[64,2,8]{0,2,1:T(8,128)(2,1)} %param.27) | copy-start | bytes 6148
  161.6 63.3 %copy-start.8 = (bf16[128,4]{0,1:T(4,128)(2,1)S(1)}, bf16[128,4]{0,1:T(4,128)(2,1)}, u32[]{:S(2)}) copy-start(bf16[128,4]{0,1:T(4,128)(2,1)} %param.32) | copy-start | bytes 3076
  220.8 24.6 %copy-start.9 = (s32[128]{0:T(128)S(1)}, s32[128]{0:T(128)}, u32[]{:S(2)}) copy-start(s32[128]{0:T(128)} %param.22) | copy-start | bytes 1540
  245.4 2.3 copy-start.1
  245.4 2.3 copy-start.6
  249.9 16.9 %copy-start.2 = (bf16[128,4,4,32]{0,3,2,1:T(8,128)(2,1)S(1)}, bf16[128,4,4,32]{0,3,2,1:T(8,128)(2,1)}, u32[]{:S(2)}) copy-start(bf16[128,4,4,32]{0,3,2,1:T(8,128)(2,1)} %param.36) | copy-start | bytes 393220
  265.6 1.9 copy-start.5
  283.0 2.3 copy-start.7

commit v3 on v2

--- a/solution.py
+++ b/solution.py
@@ -13,43 +13,6 @@
 MESH = pl.DeviceIdType.MESH
 LOG2E = math.log2(math.e)
 VMEM = pltpu.VMEM
-
-
-def layer_norm(values):
-    widened = values.astype(jnp.float32)
-    mean_val = jnp.mean(widened, axis=-1, keepdims=True)
-    centered = widened - mean_val
-    variance = jnp.mean(centered * centered, axis=-1, keepdims=True)
-    return (centered * lax.rsqrt(variance + 1e-5)).astype(jnp.bfloat16)
-
-
-def mask_bias(mask_vals):
-    return (mask_vals.astype(jnp.float32) - 1.0) * 1e4
-
-
-def matmul_bf(einsum_form, left_arr, right_arr):
-    return jnp.einsum(einsum_form, left_arr, right_arr, preferred_element_type=jnp.float32).astype(jnp.bfloat16)
-
-
-def gated_out(einsum_form, gate_proj, attended, out_w):
-    gated_vals = (jax.nn.sigmoid(gate_proj.astype(jnp.float32)) * attended).astype(jnp.bfloat16)
-    return jnp.einsum(einsum_form, gated_vals, out_w, preferred_element_type=jnp.float32)
-
-
-def triangle_rows(pair_act, pair_ln, bias_full, res_mask, qkvg_w, out_w):
-    projected = matmul_bf('ijc,cahd->aijhd', pair_ln, qkvg_w)
-    logits = jnp.einsum('ijhd,ikhd->ihjk', projected[0], projected[1], preferred_element_type=jnp.float32) * (qkvg_w.shape[-1] ** -0.5) + bias_full[None] + mask_bias(res_mask)[None, None, None, :]
-    attn_probs = jax.nn.softmax(logits, axis=-1).astype(jnp.bfloat16)
-    attended = jnp.einsum('ihjk,ikhd->ijhd', attn_probs, projected[2], preferred_element_type=jnp.float32)
-    return (pair_act + gated_out('ijhd,hdc->ijc', projected[3], attended, out_w)).astype(jnp.bfloat16)
-
-
-def triangle_cols(pair_cols, pair_ln, bias_full, res_mask, qkvg_w, out_w):
-    projected = matmul_bf('ijc,cahd->aijhd', pair_ln, qkvg_w)
-    logits = jnp.einsum('ijhd,kjhd->jhik', projected[0], projected[1], preferred_element_type=jnp.float32) * (qkvg_w.shape[-1] ** -0.5) + bias_full[None] + mask_bias(res_mask)[None, None, None, :]
-    attn_probs = jax.nn.softmax(logits, axis=-1).astype(jnp.bfloat16)
-    attended = jnp.einsum('jhik,kjhd->ijhd', attn_probs, projected[2], preferred_element_type=jnp.float32)
-    return (pair_cols + gated_out('ijhd,hdc->ijc', projected[3], attended, out_w)).astype(jnp.bfloat16)
 
 
 def mm(left, right):
@@ -84,24 +47,53 @@
     return out
 
 
-def bias_kernel(z_ref, w_ref, out_ref):
+def group_barrier(me, ndap):
+    barrier = pltpu.get_barrier_semaphore()
+    for k in range(1, ndap):
+        pl.semaphore_signal(barrier, inc=1, device_id={'dap': lax.rem(me + k, ndap)}, device_id_type=MESH)
+    pl.semaphore_wait(barrier, ndap - 1)
+
+
+def far_first(ndap):
+    return sorted(range(1, ndap), key=lambda k: -min(k, ndap - k))
+
+
+def start_gather(src_ref, all_ref, me, ndap, send_sem, recv_sem):
+    copies = []
+    for k in far_first(ndap):
+        cp = pltpu.make_async_remote_copy(src_ref, all_ref.at[me], send_sem.at[k], recv_sem.at[k], device_id={'dap': lax.rem(me + k, ndap)}, device_id_type=MESH)
+        cp.start()
+        copies.append(cp)
+    all_ref[me] = src_ref[...]
+    return copies
+
+
+def start_swap(send_ref, recv_ref, me, ndap, send_sem, recv_sem):
+    copies = []
+    for k in far_first(ndap):
+        other = lax.rem(me + k, ndap)
+        cp = pltpu.make_async_remote_copy(send_ref.at[other], recv_ref.at[me], send_sem.at[k], recv_sem.at[k], device_id={'dap': other}, device_id_type=MESH)
+        cp.start()
+        copies.append(cp)
+    recv_ref[me] = send_ref[me]
+    return copies
+
+
+def finish(copies):
+    for cp in copies:
+        cp.wait_recv()
+
+
+def drain(copies):
+    for cp in copies:
+        cp.wait_send()
+
+
+def pair_bias(z_ref, w_ref, out_ref):
     heads = w_ref.shape[0]
     for r in range(z_ref.shape[0]):
         ln = ln_lanes(z_ref[r].astype(F32))
         out_ref[r * heads:(r + 1) * heads, :] = mm_nt(w_ref[...], ln).astype(BF16).astype(F32)
-
-
-def row_kernel(m_ref, braw_ref, mask_ref, wqkvg_ref, wout_ref, wkvg_ref, m1_ref, kv_ref, g_ref, qsum_ref, bias_ref, wo_ref, q_ref, kt_ref, v_ref, y_ref, s0_ref, s1_ref, p0_ref, p1_ref, l0_ref, l1_ref, *, heads, hd):
-    seqs, chans, res = m_ref.shape
-    width = heads * hd
-    wo_ref[...] = wout_ref[...].astype(F32).T.astype(BF16)
-    for h in range(heads):
-        plane = braw_ref[pl.ds(h, res, stride=heads), :]
-        bias_ref[:, h * res:(h + 1) * res] = plane.T * LOG2E
-    qsum_ref[...] = jnp.zeros_like(qsum_ref)
-    row_project(m_ref, mask_ref, wqkvg_ref, q_ref, kt_ref, v_ref, g_ref, heads, hd)
-    row_attend(bias_ref, q_ref, kt_ref, v_ref, g_ref, y_ref, s0_ref, s1_ref, p0_ref, p1_ref, l0_ref, l1_ref, heads, hd)
-    row_finish(m_ref, mask_ref, wo_ref, wkvg_ref, y_ref, m1_ref, kv_ref, g_ref, qsum_ref, hd)
 
 
 def row_project(m_ref, mask_ref, wqkvg_ref, q_ref, kt_ref, v_ref, g_ref, heads, hd, unroll=8):
@@ -212,12 +204,10 @@
     lax.fori_loop(0, seqs // unroll, body, 0)
 
 
-def col_stats(qtot, cnt, kv_ref, mask_ref, wq_ref, planes_ref, stats_ref, heads, hd):
+def col_stats(qtot, cnt, mask_ref, wq_ref, planes_ref, stats_ref, heads, hd):
     seqs, res = mask_ref.shape
     qbar = (qtot / (cnt + 1e-10)).astype(BF16)
     q = mm(wq_ref[...], qbar).astype(BF16).astype(F32)
-    for d in range(2 * hd):
-        planes_ref[d] = kv_ref[pl.ds(d, seqs, stride=2 * hd), :]
     mb = (mask_ref[...] - 1.0) * (1e4 * LOG2E)
     for h in range(heads):
         acc = q[h * hd:h * hd + 1] * planes_ref[0]
@@ -234,11 +224,6 @@
             stats_ref[r:r + 1, :] = jnp.sum(pb * planes_ref[hd + d], axis=0, keepdims=True)
 
 
-def col1_kernel(qtot_ref, fmask_ref, kv_ref, mask_ref, wq_ref, stats_ref, planes_ref, *, heads, hd):
-    cnt = jnp.sum(fmask_ref[...], axis=0, keepdims=True).astype(F32)
-    col_stats(qtot_ref[...], cnt, kv_ref, mask_ref, wq_ref, planes_ref, stats_ref, heads, hd)
-
-
 def combine_stats(stats, heads, hd):
     gm = stats[0][0:heads]
     for st in stats[1:]:
@@ -254,11 +239,9 @@
     return wv / totx
 
 
-def col2_kernel(stats_ref, g_ref, m1_ref, mask_ref, wout_ref, wac_ref, m2_ref, a_ref, c_ref, o_ref, wo_ref, as_ref, cs_ref, at_ref, *, heads, hd):
+def col_finish(g_ref, m1_ref, mask_ref, wac_ref, m2_ref, a_ref, c_ref, o_ref, wo_ref, as_ref, cs_ref, at_ref):
     seqs, chans, res = m1_ref.shape
     wide = wac_ref.shape[0] // 2
-    wo_ref[...] = wout_ref[...].astype(F32).T.astype(BF16)
-    o_ref[...] = combine_stats([stats_ref[d] for d in range(stats_ref.shape[0])], heads, hd)
 
     def pair(s0):
         ys = [(jax.nn.sigmoid(g_ref[s0 + u].astype(F32)) * o_ref[...]).astype(BF16) for u in range(2)]
@@ -281,21 +264,67 @@
 
     lax.fori_loop(0, seqs // 8, body, 0)
 
-    def planes(e, _):
-        c_ref[e] = cs_ref[pl.ds(e, seqs, stride=wide), :].astype(BF16)
-        at_ref[pl.ds(e, res, stride=wide), :] = as_ref[pl.ds(e, seqs, stride=wide), :].T
+    def planes(it, _):
+        for n in range(4):
+            e = it * 4 + n
+            c_ref[e] = cs_ref[pl.ds(e, seqs, stride=wide), :].astype(BF16)
+            at_ref[pl.ds(e, res, stride=wide), :] = as_ref[pl.ds(e, seqs, stride=wide), :].T
         return 0
 
-    lax.fori_loop(0, wide, planes, 0)
-    a_ref[...] = at_ref[...].astype(BF16)
+    lax.fori_loop(0, wide // 4, planes, 0)
+    per = a_ref.shape[2]
+    for b in range(a_ref.shape[0]):
+        for u in range(2):
+            r0 = (b * 2 + u) * per
+            a_ref[b, u] = at_ref[r0:r0 + per, :].astype(BF16)
+
+
+def msa_kernel(m_ref, z_ref, fmask_ref, wb_ref, wqkvg_ref, wout_ref, wq_ref, wkv_ref, wg_ref, wcout_ref, wac_ref,
+               m2_ref, a_ref, c_ref,
+               bsend_ref, ball_ref, qsum_ref, qall_ref, stat_ref, sall_ref, m1_ref, mask_ref, bias_ref, wo_ref, wco_ref, wkvg_ref,
+               q_ref, kt_ref, v_ref, g_ref, y_ref, s0_ref, s1_ref, p0_ref, p1_ref, l0_ref, l1_ref, kv_ref, planes_ref, o_ref, as_ref, cs_ref, at_ref,
+               send_sem, recv_sem, *, ndap, heads, hd):
+    seqs, chans, res = m_ref.shape
+    me = lax.axis_index('dap')
+    pair_bias(z_ref, wb_ref, bsend_ref)
+    group_barrier(me, ndap)
+    bias_copies = start_gather(bsend_ref, ball_ref, me, ndap, send_sem.at[0], recv_sem.at[0])
+    mask_ref[...] = fmask_ref[pl.ds(me * seqs, seqs), :].astype(F32)
+    wo_ref[...] = wout_ref[...].astype(F32).T.astype(BF16)
+    wco_ref[...] = wcout_ref[...].astype(F32).T.astype(BF16)
+    wkvg_ref[0:2 * hd] = wkv_ref[...]
+    wkvg_ref[2 * hd:] = wg_ref[...]
+    qsum_ref[...] = jnp.zeros_like(qsum_ref)
+    row_project(m_ref, mask_ref, wqkvg_ref, q_ref, kt_ref, v_ref, g_ref, heads, hd)
+    finish(bias_copies)
+    flat = ball_ref.reshape(ndap * bsend_ref.shape[0], res)
+    for h in range(heads):
+        bias_ref[:, h * res:(h + 1) * res] = flat[pl.ds(h, res, stride=heads), :].T * LOG2E
+    row_attend(bias_ref, q_ref, kt_ref, v_ref, g_ref, y_ref, s0_ref, s1_ref, p0_ref, p1_ref, l0_ref, l1_ref, heads, hd)
+    row_finish(m_ref, mask_ref, wo_ref, wkvg_ref, y_ref, m1_ref, kv_ref, g_ref, qsum_ref, hd)
+
+    sum_copies = start_gather(qsum_ref, qall_ref, me, ndap, send_sem.at[1], recv_sem.at[1])
+    cnt = jnp.sum(fmask_ref[...], axis=0, keepdims=True).astype(F32)
+    for d in range(2 * hd):
+        planes_ref[d] = kv_ref[pl.ds(d, seqs, stride=2 * hd), :]
+    finish(sum_copies)
+    qtot = qall_ref[0]
+    for d in range(1, ndap):
+        qtot = qtot + qall_ref[d]
+    col_stats(qtot, cnt, mask_ref, wq_ref, planes_ref, stat_ref, heads, hd)
+
+    stat_copies = start_gather(stat_ref, sall_ref, me, ndap, send_sem.at[2], recv_sem.at[2])
+    finish(stat_copies)
+    o_ref[...] = combine_stats([sall_ref[d] for d in range(ndap)], heads, hd)
+    col_finish(g_ref, m1_ref, mask_ref, wac_ref, m2_ref, a_ref, c_ref, o_ref, wco_ref, as_ref, cs_ref, at_ref)
+    drain(bias_copies + sum_copies + stat_copies)
 
 
 def dap_index(chip, core, chips):
     return lax.rem(chip + 2 * chips, chips) * 2 + core
 
 
-def opm_kernel(a_ref, c_ref, z_ref, mask_ref, w_ref, out_ref, ap_ref, cp_ref, part_ref, xhi_ref, xlo_ref, wt_ref, w32_ref, cnt_ref, pos_ref, neg_ref, ex_send, ex_recv, send_sem, recv_sem, *, chips):
-    me = lax.axis_index('dap')
+def outer_mean(me, a_ref, c_ref, z_ref, mask_ref, w_ref, zs_ref, ap_ref, cp_ref, part_ref, xhi_ref, xlo_ref, wt_ref, w32_ref, cnt_ref, pos_ref, neg_ref, ex_send, ex_recv, send_sem, recv_sem, chips):
     chip, core = me // 2, lax.rem(me, 2)
     wide, seqs, res = c_ref.shape
     rows = z_ref.shape[0]
@@ -304,11 +333,6 @@
     partner = chip * 2 + 1 - core
     peer = {1: dap_index(chip + 1, core, chips), -1: dap_index(chip - 1, core, chips)}
     half_chips = chips // 2
-
-    barrier = pltpu.get_barrier_semaphore()
-    for dev in (partner, peer[1], peer[-1]):
-        pl.semaphore_signal(barrier, inc=1, device_id={'dap': dev}, device_id_type=MESH)
-    pl.semaphore_wait(barrier, 3)
 
     swaps = []
     for n, (src, dst) in enumerate(((a_ref.at[:, 1 - core], ap_ref), (c_ref, cp_ref))):
@@ -424,9 +448,127 @@
             i = n * 2 + u
             cnt = cnt_ref[pl.ds(me * rows + i, 1), :] + 1e-3
             upd = (pair[:, u * res:(u + 1) * res] / cnt).T
-            out_ref[i] = (z_ref[i].astype(F32) + upd).astype(BF16)
-    for cp in sends:
-        cp.wait_send()
+            zs_ref[i * res:(i + 1) * res, :] = (z_ref[i].astype(F32) + upd).astype(BF16).astype(F32)
+    return sends
+
+
+def tri_bias(zs_ref, ln_ref, w_ref, out_ref, rows, res):
+    heads = w_ref.shape[0]
+    for r in range(0, rows, 2):
+        b = []
+        for u in range(2):
+            ln = ln_lanes(zs_ref[(r + u) * res:(r + u + 1) * res, :])
+            if ln_ref is not None:
+                ln_ref[(r + u) * res:(r + u + 1) * res, :] = ln
+            b.append(mm_nt(w_ref[...], ln)[0:heads].astype(BF16).astype(F32))
+        out_ref[r * heads:(r + 2) * heads, :] = jnp.concatenate(b, axis=0)
+
+
+def tri_project(ln_ref, w_ref, proj_ref):
+    step = 256
+    for r in range(0, ln_ref.shape[0], step):
+        proj_ref[r:r + step, :] = mm_nt(ln_ref[r:r + step, :], w_ref[...]).astype(BF16)
+
+
+def tri_attend(zs_ref, proj_ref, bias_ref, wout_ref, heads, rows, res):
+    width = proj_ref.shape[1] // 4
+    hd = width // heads
+    scale2 = hd ** -0.5 * LOG2E
+    lane = lax.broadcasted_iota(jnp.int32, (res, width), 1)
+    mine = [(lane >= h * hd) & (lane < (h + 1) * hd) for h in range(heads)]
+    zero = jnp.zeros((res, width), BF16)
+
+    def one(r0):
+        part = lambda n: proj_ref[pl.ds(r0, res), n * width:(n + 1) * width]
+        q, k, v, g = part(0), part(1), part(2), part(3)
+        s = mm_nt(q, jnp.concatenate([jnp.where(mine[h], k, zero) for h in range(heads)], axis=0))
+        ps = []
+        for h in range(heads):
+            cols = slice(h * res, (h + 1) * res)
+            x = s[:, cols] * scale2 + bias_ref[:, cols]
+            p = jnp.exp2(x - jnp.max(x, axis=1, keepdims=True))
+            ps.append((p * (1.0 / jnp.sum(p, axis=1, keepdims=True))).astype(BF16))
+        o = mm(jnp.concatenate(ps, axis=1), jnp.concatenate([jnp.where(mine[h], v, zero) for h in range(heads)], axis=0))
+        y = (jax.nn.sigmoid(g.astype(F32)) * o).astype(BF16)
+        upd = mm(y, wout_ref[...])
+        zs_ref[pl.ds(r0, res), :] = (zs_ref[pl.ds(r0, res), :] + upd).astype(BF16).astype(F32)
+
+    def body(it, _):
+        for n in range(4):
+            one(pl.multiple_of((it * 4 + n) * res, res))
+        return 0
+
+    lax.fori_loop(0, rows // 4, body, 0)
+
+
+def pack_blocks(zs_ref, send_ref, rows, res, ndap):
+    def one(q, _):
+        parts = [zs_ref[pl.ds(q * rows + u, rows, stride=res), :] for u in range(rows)]
+        send_ref[q] = jnp.concatenate(parts, axis=0).astype(BF16)
+        return 0
+
+    lax.fori_loop(0, ndap, one, 0)
+
+
+def unpack_blocks(recv_ref, put, rows, ndap):
+    for p in range(ndap):
+        blk = recv_ref[p].astype(F32)
+        for u in range(rows):
+            put(u, p, blk[u * rows:(u + 1) * rows, :])
+
+
+def pair_kernel(a_ref, c_ref, z_ref, mask_ref, rmask_ref, w_ref, wsb_ref, wsp_ref, wso_ref, web_ref, wep_ref, weo_ref,
+                out_ref,
+                ap_ref, cp_ref, part_ref, xhi_ref, xlo_ref, wt_ref, w32_ref, cnt_ref, pos_ref, neg_ref,
+                zs_ref, zc_ref, ln_ref, proj_ref, bias_ref, sb_ref, sball_ref, eb_ref, eball_ref, xs_ref, xr_ref, ys_ref, yr_ref,
+                ex_send, ex_recv, ring_send, ring_recv, send_sem, recv_sem, *, chips):
+    ndap = 2 * chips
+    me = lax.axis_index('dap')
+    rows, res, _ = z_ref.shape
+    heads = wsb_ref.shape[0]
+    group_barrier(me, ndap)
+    sends = outer_mean(me, a_ref, c_ref, z_ref, mask_ref, w_ref, zs_ref, ap_ref, cp_ref, part_ref, xhi_ref, xlo_ref, wt_ref, w32_ref, cnt_ref, pos_ref, neg_ref, ex_send, ex_recv, ring_send, ring_recv, chips)
+    kmask = (rmask_ref[...].astype(F32) - 1.0) * 1e4
+
+    tri_bias(zs_ref, ln_ref, wsb_ref, sb_ref, rows, res)
+    c1 = start_gather(sb_ref, sball_ref, me, ndap, send_sem.at[0], recv_sem.at[0])
+    tri_project(ln_ref, wsp_ref, proj_ref)
+    finish(c1)
+    flat = sball_ref.reshape(res * heads, res)
+    for h in range(heads):
+        bias_ref[:, h * res:(h + 1) * res] = (flat[pl.ds(h, res, stride=heads), :] + kmask) * LOG2E
+    tri_attend(zs_ref, proj_ref, bias_ref, wso_ref, heads, rows, res)
+
+    pack_blocks(zs_ref, xs_ref, rows, res, ndap)
+    c2 = start_swap(xs_ref, xr_ref, me, ndap, send_sem.at[1], recv_sem.at[1])
+    tri_bias(zs_ref, None, web_ref, eb_ref, rows, res)
+    c3 = start_gather(eb_ref, eball_ref, me, ndap, send_sem.at[2], recv_sem.at[2])
+    finish(c2)
+
+    def put_col(u, p, val):
+        zc_ref[u * res + p * rows:u * res + (p + 1) * rows, :] = val
+
+    unpack_blocks(xr_ref, put_col, rows, ndap)
+    for r in range(rows):
+        ln_ref[r * res:(r + 1) * res, :] = ln_lanes(zc_ref[r * res:(r + 1) * res, :])
+    tri_project(ln_ref, wep_ref, proj_ref)
+    finish(c3)
+    flat = eball_ref.reshape(res * heads, res)
+    for h in range(heads):
+        bias_ref[:, h * res:(h + 1) * res] = (flat[pl.ds(h, res, stride=heads), :].T + kmask) * LOG2E
+    tri_attend(zc_ref, proj_ref, bias_ref, weo_ref, heads, rows, res)
+
+    pack_blocks(zc_ref, ys_ref, rows, res, ndap)
+    c4 = start_swap(ys_ref, yr_ref, me, ndap, send_sem.at[3], recv_sem.at[3])
+    finish(c4)
+
+    def put_row(u, p, val):
+        zs_ref[u * res + p * rows:u * res + (p + 1) * rows, :] = val
+
+    unpack_blocks(yr_ref, put_row, rows, ndap)
+    for r in range(rows):
+        out_ref[r] = zs_ref[r * res:(r + 1) * res, :].astype(BF16)
+    drain(sends + c1 + c2 + c3 + c4)
 
 
 def vspec():
@@ -464,63 +606,50 @@
         width = heads * hd
         wide = opm_proj_w.shape[2]
         outc = opm_out_w.shape[2]
-        me = lax.axis_index('dap')
-        mask = lax.dynamic_slice_in_dim(full_mask, me * seqs, seqs, axis=0).astype(F32)
+        thd = start_qkvg_w.shape[2] * start_qkvg_w.shape[3]
+        theads = start_bias_w.shape[1]
         m_t = jnp.swapaxes(msa, 1, 2)
         wt = lambda w: w.reshape(w.shape[0], -1).T
-
-        braw = call(bias_kernel, sds((rows * heads, res), F32), 2, [], 'row_bias')(pair_act, row_bias_w.T)
-        braw = lax.all_gather(braw, 'dap', axis=0, tiled=True)
-
-        wkvg = jnp.concatenate([wt(col_kv_w), wt(col_gate_w)], axis=0)
-        m1, kv, g, qsum = call(
-            functools.partial(row_kernel, heads=heads, hd=hd),
-            [sds((seqs, chans, res), BF16), sds((seqs * 2 * hd, res), F32), sds((seqs, width, res), BF16), sds((chans, res), F32)], 6,
-            [VMEM((res, heads * res), F32), VMEM((chans, width), BF16),
-             VMEM((seqs, width, res), BF16), VMEM((seqs, res, width + 16), BF16), VMEM((seqs, width, res), BF16), VMEM((seqs, width, res), BF16),
+        dma = pltpu.SemaphoreType.DMA
+
+        nstat = 2 * heads + width
+        m2, a, c = call(
+            functools.partial(msa_kernel, ndap=ndap, heads=heads, hd=hd),
+            [sds((seqs, chans, res), BF16), sds((chips, 2, rows * wide, seqs), BF16), sds((wide, seqs, res), BF16)], 11,
+            [VMEM((rows * heads, res), F32), VMEM((ndap, rows * heads, res), F32),
+             VMEM((chans, res), F32), VMEM((ndap, chans, res), F32),
+             VMEM((nstat, res), F32), VMEM((ndap, nstat, res), F32),
+             VMEM((seqs, chans, res), BF16), VMEM((seqs, res), F32), VMEM((res, heads * res), F32),
+             VMEM((chans, width), BF16), VMEM((chans, width), BF16), VMEM((2 * hd + width, chans), BF16),
+             VMEM((seqs, width, res), BF16), VMEM((seqs, res, width + 16), BF16), VMEM((seqs, width, res), BF16), VMEM((seqs, width, res), BF16), VMEM((seqs, width, res), BF16),
              VMEM((res, heads * res), F32), VMEM((res, heads * res), F32), VMEM((res, heads * res), BF16), VMEM((res, heads * res), BF16),
-             VMEM((8, heads * res), F32), VMEM((8, heads * res), F32)], 'row_attention',
-        )(m_t, braw, mask, wt(row_qkvg_w), row_out_w.reshape(width, chans), wkvg)
-
-        qtot = lax.psum(qsum, 'dap')
-        nstat = 2 * heads + width
-        stats = call(
-            functools.partial(col1_kernel, heads=heads, hd=hd),
-            sds((nstat, res), F32), 5, [VMEM((2 * hd, seqs, res), F32)], 'col_stats',
-        )(qtot, full_mask, kv, mask, wt(col_query_w))
-        stats = lax.all_gather(stats, 'dap', axis=0)
-
-        m2, a, c = call(
-            functools.partial(col2_kernel, heads=heads, hd=hd),
-            [sds((seqs, chans, res), BF16), sds((res * wide, seqs), BF16), sds((wide, seqs, res), BF16)], 6,
-            [VMEM((width, res), F32), VMEM((chans, width), BF16), VMEM((seqs * wide, res), F32), VMEM((seqs * wide, res), F32), VMEM((res * wide, seqs), F32)], 'col_out',
-        )(stats, g, m1, mask, col_out_w.reshape(width, chans), wt(opm_proj_w))
+             VMEM((8, heads * res), F32), VMEM((8, heads * res), F32),
+             VMEM((seqs * 2 * hd, res), F32), VMEM((2 * hd, seqs, res), F32), VMEM((width, res), F32),
+             VMEM((seqs * wide, res), F32), VMEM((seqs * wide, res), F32), VMEM((res * wide, seqs), F32),
+             dma((3, ndap)), dma((3, ndap))],
+            'msa_stack', cid=0,
+        )(m_t, pair_act, full_mask, row_bias_w.T, wt(row_qkvg_w), row_out_w.reshape(width, chans), wt(col_query_w), wt(col_kv_w), wt(col_gate_w), col_out_w.reshape(width, chans), wt(opm_proj_w))
         msa_out = jnp.swapaxes(m2, 1, 2)
 
         npair = rows // 2
         nbuf = 2 * (chips // 2) - 1
-        pair_act = call(
-            functools.partial(opm_kernel, chips=chips),
-            sds(pair_act.shape, BF16), 5,
+        small = (rows * theads, res)
+        block = (ndap, rows * rows, outc)
+        pair_out = call(
+            functools.partial(pair_kernel, chips=chips),
+            sds(pair_act.shape, BF16), 12,
             [VMEM((chips, rows * wide, seqs), BF16), VMEM((wide, seqs, res), BF16),
              VMEM((chips, npair, outc, 2 * res), F32),
              VMEM((npair, wide * wide, 2 * res), BF16), VMEM((npair, wide * wide, 2 * res), BF16),
              VMEM((outc, wide * wide), BF16), VMEM((wide * wide, outc), F32), VMEM((res, res), F32),
              VMEM((nbuf, npair // 2, outc, 2 * res), F32), VMEM((nbuf, npair // 2, outc, 2 * res), F32),
-             pltpu.SemaphoreType.DMA((2,)), pltpu.SemaphoreType.DMA((2,)),
-             pltpu.SemaphoreType.DMA((2, nbuf)), pltpu.SemaphoreType.DMA((2, nbuf))],
-            'outer_mean', cid=1,
-        )(a.reshape(chips, 2, rows * wide, seqs), c, pair_act, full_mask, opm_out_w.reshape(wide * wide, outc))
-
-        pair_ln = layer_norm(pair_act)
-        start_full = lax.all_gather(matmul_bf('ijc,ch->hij', pair_ln, start_bias_w), 'dap', axis=1, tiled=True)
-        pair_act = triangle_rows(pair_act, pair_ln, start_full, res_mask, start_qkvg_w, start_out_w)
-
-        pair_cols = lax.all_to_all(pair_act, 'dap', 1, 0, tiled=True)
-        cols_ln = layer_norm(pair_cols)
-        end_full = lax.all_gather(matmul_bf('ijc,ch->hji', cols_ln, end_bias_w), 'dap', axis=1, tiled=True)
-        pair_cols = triangle_cols(pair_cols, cols_ln, end_full, res_mask, end_qkvg_w, end_out_w)
-        pair_out = lax.all_to_all(pair_cols, 'dap', 0, 1, tiled=True)
+             VMEM((rows * res, outc), F32), VMEM((rows * res, outc), F32), VMEM((rows * res, outc), BF16), VMEM((rows * res, 4 * thd), BF16), VMEM((res, theads * res), F32),
+             VMEM(small, F32), VMEM((ndap,) + small, F32), VMEM(small, F32), VMEM((ndap,) + small, F32),
+             VMEM(block, BF16), VMEM(block, BF16), VMEM(block, BF16), VMEM(block, BF16),
+             dma((2,)), dma((2,)), dma((2, nbuf)), dma((2, nbuf)), dma((4, ndap)), dma((4, ndap))],
+            'pair_stack', cid=1,
+        )(a, c, pair_act, full_mask, res_mask.reshape(1, res), opm_out_w.reshape(wide * wide, outc),
+          start_bias_w.T, wt(start_qkvg_w), start_out_w.reshape(thd, outc), end_bias_w.T, wt(end_qkvg_w), end_out_w.reshape(thd, outc))
         return msa_out, pair_out
 
     row_spec = P(('data', 'dap'), None, None)

time: 305 us -> 213 us (0.70)
  blocking collectives: 153 us -> 0 us
  Pallas kernels: 131 us -> 209 us
  matrix products: 13 us -> 0 us
  other arithmetic: 5.26 us -> 0 us
    pallas_call x5 -> x2, Pallas kernels: 131 us -> 209 us  [the longest x1 106 us: evoformer_block(): call(functools.partial(msa_kernel, ndap=ndap, heads=heads, hd=hd), [sds((...]
    all_gather x4 -> x0, blocking collectives: 78.1 us -> none  [the longest x1 24.1 us: evoformer_block(): braw = lax.all_gather(braw, 'dap', axis=0, tiled=True)]
    psum x1 -> x0, blocking collectives: 43 us -> none  [evoformer_block(): qtot = lax.psum(qsum, 'dap')]
    all_to_all x2 -> x0, blocking collectives: 31.6 us -> none  [the longest x1 16.3 us: evoformer_block(): pair_out = lax.all_to_all(pair_cols, 'dap', 0, 1, tiled=True)]
    dot_general x6 -> x0, matrix products: 8.41 us -> none  [the longest x2 4.38 us: gated_out(): jnp.einsum(einsum_form, gated_vals, out_w, preferred_element_type=jnp.flo...]
    sub x2 -> x0, matrix products: 4.63 us -> none  [the longest x1 2.32 us: triangle_rows(): attn_probs = jax.nn.softmax(logits, axis=-1).astype(jnp.bfloat16)]
where the time goes in v3:
time: 213 us; the launch traced here: 212 us
  Pallas kernels  209 us (98%)
    pallas_call x1, Pallas kernels, evoformer_block(): call(functools.partial(msa_kernel, ndap=ndap, heads=heads, hd=hd), [sds((...  106 us
    pallas_call x1, Pallas kernels, evoformer_block(): call(functools.partial(pair_kernel, chips=chips), sds(pair_act.shape, BF1...  104 us

profile of v3, /device:TPU:21, one launch (start us, length us, event | category | flops | bytes accessed | tf_op | source)
XLA Modules:
  0.0 212.0 jit_solution(2006893596258863348)
XLA Ops:
  0.6 105.5 %msa_stack.1 = (bf16[128,64,128]{2,1,0:T(8,128)(2,1)}, bf16[8,2,256,128]{3,2,1,0:T(8,128)(2,1)}, bf16[32,128,128]{2,1,0:T(8,128)(2,1)}) custom-call(bf16[128,64,128]{2,1,0:T(8,128)(2,1)} %bitcast.41, bf16[8,128,128]{2,1,0:T(8,128)(2,1)} %z_ref.3, s32[2048,128]{1,0:T(8,128)} %mask_ref.1, bf16[8,128]{1,0:T(8,128)(2,1)} %bitcast.49, bf16[256,64]{1,0:T(8,128)(2,1)} %bitcast.42, ...), custom_call_target="tpu_custom_call" | custom-call | flops 1000000000 | bytes 1000000 | tf_op jit(solution)/shard_map/msa_stack/pallas_call | solution.py:616
  106.2 0.0 copy-start
  106.2 103.8 %pair_stack.1 = bf16[8,128,128]{2,1,0:T(8,128)(2,1)} custom-call(bf16[8,2,256,128]{3,2,1,0:T(8,128)(2,1)} %get-tuple-element.6.a_ref, bf16[32,128,128]{2,1,0:T(8,128)(2,1)} %get-tuple-element.7.c_ref, bf16[8,128,128]{2,1,0:T(8,128)(2,1)} %z_ref.3, s32[2048,128]{1,0:T(8,128)} %mask_ref.1, s32[1,128]{1,0:T(1,128)} %bitcast.40, bf16[1024,128]{1,0:T(8,128)(2,1)} %bitcast.33, ...), custom_call_target="tpu_custom_call" | custom-call | flops 1000000000 | bytes 1000000 | tf_op jit(solution)/shard_map/pair_stack/pallas_call | solution.py:638
  210.0 0.0 copy-done
  210.0 0.0 copy-start.1
  210.0 1.3 copy.23
  211.3 0.0 copy-done.1
  211.3 0.7 copy.24
Async XLA Ops:
  106.2 103.8 %copy-start = (bf16[128,64,128]{2,1,0:T(8,128)(2,1)S(1)}, bf16[128,64,128]{2,1,0:T(8,128)(2,1)}, u32[]{:S(2)}) copy-start(bf16[128,64,128]{2,1,0:T(8,128)(2,1)} %get-tuple-element.5) | copy-start | bytes 6291460
  210.0 1.3 copy-start.1

commit v4 on v3

v4 whole, which is shorter than its diff:
```python
import functools
import math

import jax
import jax.numpy as jnp
from jax import lax
from jax.experimental import pallas as pl
from jax.experimental.pallas import tpu as pltpu
from jax.sharding import PartitionSpec as P

F32 = jnp.float32
BF16 = jnp.bfloat16
MESH = pl.DeviceIdType.MESH
LOG2E = math.log2(math.e)
VMEM = pltpu.VMEM


def mm(left, right):
    return jnp.dot(left, right, preferred_element_type=F32)


def mm_nt(left, right):
    return lax.dot_general(left, right, (((1,), (1,)), ((), ())), preferred_element_type=F32)


def span(n, width):
    return slice(n * width, (n + 1) * width)


def sum0(x):
    return jnp.sum(x, axis=0, keepdims=True)


def max0(x):
    return jnp.max(x, axis=0, keepdims=True)


def ln_rows(x):
    n = x.shape[0]
    xc = x - sum0(x) * (1.0 / n)
    var = sum0(xc * xc) * (1.0 / n)
    return (xc * lax.rsqrt(var + 1e-5)).astype(BF16)


def ln_lanes(x):
    n = x.shape[1]
    xc = x - jnp.sum(x, axis=1, keepdims=True) * (1.0 / n)
    var = jnp.sum(xc * xc, axis=1, keepdims=True) * (1.0 / n)
    return (xc * lax.rsqrt(var + 1e-5)).astype(BF16)


def bf16_split(value, terms):
    import numpy as np
    out = []
    for _ in range(terms):
        t = float(np.asarray(value, dtype=jnp.bfloat16))
        out.append(t)
        value = value - t
    return out


def group_barrier(me, ndap):
    barrier = pltpu.get_barrier_semaphore()
    for k in range(1, ndap):
        pl.semaphore_signal(barrier, inc=1, device_id={'dap': lax.rem(me + k, ndap)}, device_id_type=MESH)
    pl.semaphore_wait(barrier, ndap - 1)


def far_first(count):
    return sorted(range(1, count), key=lambda k: -min(k, count - k))


def remote(src, dst, send_sem, recv_sem, dev):
    cp = pltpu.make_async_remote_copy(src, dst, send_sem, recv_sem, device_id={'dap': dev}, device_id_type=MESH)
    cp.start()
    return cp


def start_gather(src_ref, slab_ref, chip, core, chips, send_sem, recv_sem):
    copies = [remote(src_ref, slab_ref.at[chip], send_sem.at[k], recv_sem.at[k], dap_index(chip + k, core, chips)) for k in far_first(chips)]
    slab_ref[chip] = src_ref[...]
    return copies


def start_swap(send_ref, recv_ref, me, ndap, send_sem, recv_sem):
    copies = []
    for k in far_first(ndap):
        other = lax.rem(me + k, ndap)
        cp = pltpu.make_async_remote_copy(send_ref.at[other], recv_ref.at[me], send_sem.at[k], recv_sem.at[k], device_id={'dap': other}, device_id_type=MESH)
        cp.start()
        copies.append(cp)
    recv_ref[me] = send_ref[me]
    return copies


def finish(copies):
    for cp in copies:
        cp.wait_recv()


def drain(copies):
    for cp in copies:
        cp.wait_send()


def strided(ref, row):
    return ref.reshape(ref.shape[0] * ref.shape[1], ref.shape[2])[pl.ds(row, ref.shape[0], stride=ref.shape[1]), :]


def pair_bias(z_ref, w_ref, out_ref):
    vals = [mm_nt(w_ref[...], ln_lanes(z_ref[r].astype(F32))) for r in range(z_ref.shape[0])]
    out_ref[...] = jnp.concatenate(vals, axis=0).astype(BF16)


def bias_plane(wide_ref, h, heads):
    rows = wide_ref.shape[2] // heads
    return jnp.concatenate([wide_ref[u, c, pl.ds(h, rows, stride=heads), :] for c in range(wide_ref.shape[1]) for u in range(2)], axis=0)


def row_project(m_ref, mask_ref, wqkvg_ref, q_ref, kt_ref, v_ref, g_ref, heads, hd, unroll=8):
    seqs, chans, res = m_ref.shape
    width = heads * hd
    aug = kt_ref.shape[2] - width
    terms = bf16_split(1e4 / hd ** -0.5, 3)
    rowi = lax.broadcasted_iota(jnp.int32, (aug, res), 0)
    mvec = jnp.where(rowi == 0, terms[0], jnp.where(rowi == 1, terms[1], jnp.where(rowi == 2, terms[2], 0.0)))

    def body(it, _):
        for n in range(unroll // 2):
            s0 = it * unroll + n * 2
            lns = [ln_rows(m_ref[s0 + u].astype(F32)) for u in range(2)]
            proj = mm(wqkvg_ref[...], jnp.concatenate(lns, axis=1))
            for u in range(2):
                cols = span(u, res)
                s = s0 + u
                q_ref[s] = proj[0:width, cols].astype(BF16)
                mrow = mask_ref[pl.ds(s, 1), :] - 1.0
                k = proj[width:2 * width, cols].astype(BF16).astype(F32)
                kt_ref[s] = jnp.concatenate([k, mrow * mvec], axis=0).T.astype(BF16)
                v_ref[s] = proj[2 * width:3 * width, cols].astype(BF16)
                g_ref[s] = proj[3 * width:, cols].astype(BF16)
        return 0

    lax.fori_loop(0, seqs // unroll, body, 0)


def row_attend(bias_ref, q_ref, kt_ref, v_ref, g_ref, y_ref, s_refs, p_refs, l_refs, heads, hd):
    seqs, width, res = q_ref.shape
    scale2 = hd ** -0.5 * LOG2E
    npairs = heads // 2
    aug = kt_ref.shape[2] - width
    two, both = 2 * hd, 2 * res
    first = lax.broadcasted_iota(jnp.int32, (two, res), 0) < hd
    zero16 = jnp.zeros((two, res), BF16)
    ones = jnp.ones((aug, res), BF16)

    def scores(s, s_ref, t):
        s = jnp.minimum(s, seqs - 1)
        q16 = q_ref[s, span(t, two)]
        halves = [jnp.concatenate([zero16] * t + [part] + [zero16] * (npairs - 1 - t) + [ones], axis=0)
                  for part in (jnp.where(first, q16, zero16), jnp.where(first, zero16, q16))]
        s_ref[:, span(t, both)] = mm(kt_ref[s], jnp.concatenate(halves, axis=1))

    def soft(s_ref, p_ref, l_ref, t):
        for h in (2 * t, 2 * t + 1):
            cols = span(h, res)
            x = s_ref[:, cols] * scale2 + bias_ref[:, cols]
            p = jnp.exp2(x - max0(x))
            l_ref[:, cols] = sum0(p)
            p_ref[h] = p.astype(BF16)

    def values(s, p_ref, l_ref, t):
        s = jnp.maximum(s, 0)
        o = mm(v_ref[s, span(t, two)], jnp.concatenate([p_ref[2 * t], p_ref[2 * t + 1]], axis=1))
        inv = 1.0 / l_ref[:, span(t, both)]
        att = jnp.concatenate([o[:hd, :res] * inv[:, :res], o[hd:, res:] * inv[:, res:]], axis=0)
        y_ref[s, span(t, two)] = (jax.nn.sigmoid(g_ref[s, span(t, two)].astype(F32)) * att).astype(BF16)

    depth = len(s_refs)
    lead = depth // 2
    for n in range(lead):
        for t in range(npairs):
            scores(n, s_refs[n], t)

    def body(it, _):
        for n in range(depth):
            s = it * depth + n
            far = (n + lead) % depth
            for t in range(npairs):
                values(s - lead, p_refs[far], l_refs[far], t)
                scores(s + lead, s_refs[far], t)
                soft(s_refs[n], p_refs[n], l_refs[n], t)
        return 0

    lax.fori_loop(0, seqs // depth, body, 0)
    for n in range(lead, depth):
        for t in range(npairs):
            values(seqs - depth + n, p_refs[n], l_refs[n], t)


def row_finish(m_ref, mask_ref, wo_ref, wkvg_ref, y_ref, m1_ref, kv_ref, g_ref, qsum_ref, hd, unroll=8):
    seqs, chans, res = m_ref.shape

    def body(it, _):
        acc = jnp.zeros((chans, res), F32)
        for n in range(unroll // 2):
            s0 = it * unroll + n * 2
            upd = mm(wo_ref[...], jnp.concatenate([y_ref[s0], y_ref[s0 + 1]], axis=1))
            ln1 = []
            for u in range(2):
                m1 = (m_ref[s0 + u].astype(F32) + upd[:, span(u, res)]).astype(BF16)
                m1_ref[s0 + u] = m1
                l1 = ln_rows(m1.astype(F32))
                acc = acc + l1.astype(F32) * mask_ref[pl.ds(s0 + u, 1), :]
                ln1.append(l1)
            kvg = mm(wkvg_ref[...], jnp.concatenate(ln1, axis=1)).astype(BF16)
            for u in range(2):
                kv_ref[s0 + u, 0:2 * hd] = kvg[0:2 * hd, span(u, res)].astype(F32)
                g_ref[s0 + u] = kvg[2 * hd:, span(u, res)]
        qsum_ref[...] += acc
        return 0

    lax.fori_loop(0, seqs // unroll, body, 0)


def col_stats(qtot, cnt, mask_ref, wq_ref, planes_ref, stats_ref, heads, hd):
    seqs, res = mask_ref.shape
    qbar = (qtot / (cnt + 1e-10)).astype(BF16)
    q = mm(wq_ref[...], qbar).astype(BF16).astype(F32)
    mb = (mask_ref[...] - 1.0) * (1e4 * LOG2E)
    for h in range(heads):
        acc = q[h * hd:h * hd + 1] * planes_ref[0]
        for d in range(1, hd):
            acc = acc + q[h * hd + d:h * hd + d + 1] * planes_ref[d]
        t = acc * (hd ** -0.5 * LOG2E) + mb
        mx = max0(t)
        p = jnp.exp2(t - mx)
        half, k = h // (heads // 2), h % (heads // 2)
        stats_ref[half, k:k + 1, :] = mx
        stats_ref[half, heads // 2 + k:heads // 2 + k + 1, :] = sum0(p)
        pb = p.astype(BF16).astype(F32)
        for d in range(hd):
            r = heads + k * hd + d
            stats_ref[half, r:r + 1, :] = sum0(pb * planes_ref[hd + d])


def combine_stats(stats, heads, hd):
    gm = functools.reduce(jnp.maximum, [st[0:heads] for st in stats])
    spread = lambda f: jnp.concatenate([jnp.broadcast_to(f[h:h + 1], (hd, f.shape[1])) for h in range(heads)], axis=0)
    tot = wv = 0.0
    for st in stats:
        f = jnp.exp2(st[0:heads] - gm)
        tot = tot + f * st[heads:2 * heads]
        wv = wv + spread(f) * st[2 * heads:]
    return gm, tot, wv, spread


def col_finish(g_ref, m1_ref, mask_ref, wac_ref, m2_ref, a_ref, c_ref, o_ref, wo_ref, as_ref, cs_ref, at_ref):
    seqs, chans, res = m1_ref.shape
    wide = wac_ref.shape[0] // 2

    def pair(s0):
        ys = [(jax.nn.sigmoid(g_ref[s0 + u].astype(F32)) * o_ref[...]).astype(BF16) for u in range(2)]
        upd = mm(wo_ref[...], jnp.concatenate(ys, axis=1))
        lns = []
        for u in range(2):
            m2 = (m1_ref[s0 + u].astype(F32) + upd[:, span(u, res)]).astype(BF16)
            m2_ref[s0 + u] = m2
            lns.append(ln_rows(m2.astype(F32)))
        ac = mm(wac_ref[...], jnp.concatenate(lns, axis=1)).astype(BF16).astype(F32)
        for u in range(2):
            mrow = mask_ref[pl.ds(s0 + u, 1), :]
            as_ref[s0 + u, 0:wide] = ac[0:wide, span(u, res)] * mrow
            cs_ref[s0 + u, 0:wide] = ac[wide:, span(u, res)] * mrow

    def body(it, _):
        for n in range(4):
            pair(it * 8 + n * 2)
        return 0

    lax.fori_loop(0, seqs // 8, body, 0)

    def planes(it, _):
        for n in range(8):
            e = it * 8 + n
            c_ref[e] = strided(cs_ref, e).astype(BF16)
            flat = at_ref.reshape(res * at_ref.shape[1], seqs)
            flat[pl.ds(e, res, stride=at_ref.shape[1]), :] = strided(as_ref, e).T
        return 0

    lax.fori_loop(0, wide // 8, planes, 0)
    rows = a_ref.shape[2] // wide
    for n in range(res):
        b, r = n // rows, n % rows
        a_ref[b // 2, b % 2, span(r, wide)] = at_ref[n, 0:wide].astype(BF16)


def msa_kernel(m_ref, z_ref, fmask_ref, wb_ref, wqkvg_ref, wout_ref, wq_ref, wkv_ref, wg_ref, wcout_ref, wac_ref,
               m2_ref, a_ref, c_ref,
               bsend_ref, ball_ref, bwide_ref, qsum_ref, qpart_ref, qhalf_ref, qall_ref, qfin_ref, stat_ref, spart_ref, smerge_ref, sall_ref, m1_ref, mask_ref, bias_ref, wo_ref, wco_ref, wkvg_ref,
               q_ref, kt_ref, v_ref, g_ref, y_ref, s_refs, p_refs, l_refs, kv_ref, planes_ref, o_ref, as_ref, cs_ref, at_ref,
               send_sem, recv_sem, psend_sem, precv_sem, *, ndap, heads, hd):
    seqs, chans, res = m_ref.shape
    me = lax.axis_index('dap')
    chip, core = me // 2, lax.rem(me, 2)
    chips = ndap // 2
    partner = chip * 2 + 1 - core
    pair_bias(z_ref, wb_ref, bsend_ref)
    group_barrier(me, ndap)
    bias_copies = start_gather(bsend_ref, ball_ref.at[core], chip, core, chips, send_sem.at[0], recv_sem.at[0])
    mask_ref[...] = fmask_ref[pl.ds(me * seqs, seqs), :].astype(F32)
    wo_ref[...] = wout_ref[...].astype(F32).T.astype(BF16)
    wco_ref[...] = wcout_ref[...].astype(F32).T.astype(BF16)
    wkvg_ref[0:2 * hd] = wkv_ref[...]
    wkvg_ref[2 * hd:] = wg_ref[...]
    qsum_ref[...] = jnp.zeros_like(qsum_ref)
    row_project(m_ref, mask_ref, wqkvg_ref, q_ref, kt_ref, v_ref, g_ref, heads, hd)
    finish(bias_copies)
    bias_swap = remote(ball_ref.at[core], ball_ref.at[core], psend_sem.at[0], precv_sem.at[0], partner)
    bias_swap.wait_recv()
    bwide_ref[...] = ball_ref[...].astype(F32)
    for h in range(heads):
        bias_ref[:, span(h, res)] = bias_plane(bwide_ref, h, heads).T * LOG2E
    row_attend(bias_ref, q_ref, kt_ref, v_ref, g_ref, y_ref, s_refs, p_refs, l_refs, heads, hd)
    row_finish(m_ref, mask_ref, wo_ref, wkvg_ref, y_ref, m1_ref, kv_ref, g_ref, qsum_ref, hd)

    half = chans // 2
    mine, other = pl.ds(core * half, half), pl.ds((1 - core) * half, half)
    sum_swap = remote(qsum_ref.at[other], qpart_ref, psend_sem.at[1], precv_sem.at[1], partner)
    cnt = sum0(fmask_ref[...]).astype(F32)
    sum_swap.wait_recv()
    qhalf_ref[...] = qsum_ref[mine, :] + qpart_ref[...]
    sum_copies = start_gather(qhalf_ref, qall_ref, chip, core, chips, send_sem.at[1], recv_sem.at[1])
    for d in range(2 * hd):
        planes_ref[d] = strided(kv_ref, d)
    finish(sum_copies)
    qfin_ref[mine, :] = functools.reduce(lambda x, y: x + y, [qall_ref[d] for d in range(chips)])
    fin_swap = remote(qfin_ref.at[mine], qfin_ref.at[mine], psend_sem.at[2], precv_sem.at[2], partner)
    fin_swap.wait_recv()
    col_stats(qfin_ref[...], cnt, mask_ref, wq_ref, planes_ref, stat_ref, heads, hd)

    stat_swap = remote(stat_ref.at[1 - core], spart_ref, psend_sem.at[3], precv_sem.at[3], partner)
    stat_swap.wait_recv()
    hh = heads // 2
    gm, tot, wv, _ = combine_stats([stat_ref[core], spart_ref[...]], hh, hd)
    smerge_ref[0:hh] = gm
    smerge_ref[hh:2 * hh] = tot
    smerge_ref[2 * hh:] = wv
    stat_copies = start_gather(smerge_ref, sall_ref, chip, core, chips, send_sem.at[2], recv_sem.at[2])
    finish(stat_copies)
    gm, tot, wv, spread = combine_stats([sall_ref[d] for d in range(chips)], hh, hd)
    omine = pl.ds(core * hh * hd, hh * hd)
    o_ref[omine, :] = wv / spread(tot)
    out_swap = remote(o_ref.at[omine], o_ref.at[omine], psend_sem.at[4], precv_sem.at[4], partner)
    out_swap.wait_recv()
    col_finish(g_ref, m1_ref, mask_ref, wac_ref, m2_ref, a_ref, c_ref, o_ref, wco_ref, as_ref, cs_ref, at_ref)
    drain(bias_copies + sum_copies + stat_copies + [bias_swap, sum_swap, fin_swap, stat_swap, out_swap])


def dap_index(chip, core, chips):
    return lax.rem(chip + 2 * chips, chips) * 2 + core


def outer_mean(me, a_ref, c_ref, z_ref, mask_ref, w_ref, zs_ref, ap_ref, cp_ref, part_ref, x_ref, wt_ref, w32_ref, cnt_ref, pos_ref, neg_ref, ex_send, ex_recv, send_sem, recv_sem, chips):
    chip, core = me // 2, lax.rem(me, 2)
    wide, seqs, res = c_ref.shape
    rows = z_ref.shape[0]
    brow = rows * wide
    outc = w_ref.shape[1]
    partner = chip * 2 + 1 - core
    peer = {1: dap_index(chip + 1, core, chips), -1: dap_index(chip - 1, core, chips)}
    half_chips = chips // 2
    depth, unroll = wide * wide, 4

    swaps = []
    for n, (src, dst) in enumerate(((a_ref.at[:, 1 - core], ap_ref), (c_ref, cp_ref))):
        cp = pltpu.make_async_remote_copy(src, dst, ex_send.at[n], ex_recv.at[n], device_id={'dap': partner}, device_id_type=MESH)
        cp.start()
        swaps.append(cp)

    w32_ref[...] = w_ref[...].astype(F32)
    per = 128 // wide
    for b in range(wide // per):
        cols = [w32_ref[pl.ds(b * per + f, wide, stride=wide), :] for f in range(per)]
        wt_ref[:, span(b, 128)] = jnp.concatenate(cols, axis=0).T.astype(BF16)
    wt_ref[:, depth:] = wt_ref[:, :depth]

    def count_step(n, acc):
        blk = mask_ref[pl.ds(n * 128, 128), :].astype(F32)
        return acc + mm(blk.T.astype(BF16), blk.astype(BF16))

    cnt_ref[...] = lax.fori_loop(0, mask_ref.shape[0] // 128, count_step, jnp.zeros((res, res), F32))

    for cp in swaps:
        cp.wait()

    def block(dest, slot):
        lhs = jnp.concatenate([a_ref[dest, core], ap_ref[dest]], axis=1)

        def outer(it, _):
            for n in range(unroll):
                f0 = (it * unroll + n) * 2
                rhs = [jnp.concatenate([c[f0], c[f0 + 1]], axis=1) for c in (c_ref, cp_ref)]
                o = mm(lhs, jnp.concatenate(rhs, axis=0))
                hi = o.astype(BF16)
                lo = (o - hi.astype(F32)).astype(BF16)
                for m, val in enumerate((hi, lo)):
                    for i in range(rows):
                        for u in range(2):
                            r0 = pl.multiple_of((f0 + u) * wide + m * depth, wide)
                            x_ref[i, pl.ds(r0, wide)] = val[span(i, wide), span(u, res)]
            return 0

        lax.fori_loop(0, wide // 2 // unroll, outer, 0)
        for n in range(rows // 2):
            part_ref[slot, n] = mm(wt_ref[...], jnp.concatenate([x_ref[2 * n], x_ref[2 * n + 1]], axis=1))

    sends = []
    arrivals = {}
    bufs = {1: pos_ref, -1: neg_ref}
    hq = rows // 4

    def hops(d, half):
        return half_chips if (half == 1) == (d == 1) else half_chips - 1

    slot_of = {}
    nbuf = 2 * half_chips - 1

    def buf_index(d, half, k):
        return (k - 1) + (0 if (half == 1) == (d == 1) else half_chips)

    def message(d, half, k, slot):
        idx = buf_index(d, half, k)
        src = part_ref.at[slot, pl.ds(half * hq, hq)]
        cp = pltpu.make_async_remote_copy(src, bufs[d].at[idx], send_sem.at[(d + 1) // 2, idx], recv_sem.at[(d + 1) // 2, idx], device_id={'dap': peer[d]}, device_id_type=MESH)
        arrivals[(d, half, k)] = cp
        sends.append(cp)
        cp.start()

    def take(d, half, k, slot):
        arrivals[(d, half, k)].wait_recv()
        part_ref[slot, span(half, hq)] += bufs[d][buf_index(d, half, k)]

    def dest_of(d, k):
        return lax.rem(chip + d * k + 2 * chips, chips)

    far = half_chips
    long_half = {1: 1, -1: 0}
    slots = {}

    def forward(long, k):
        for d in (1, -1):
            half = long_half[d] if long else 1 - long_half[d]
            take(d, half, k + 1, slots[(d, k)])
            message(d, half, k, slots[(d, k)])

    moves = []
    for k in range(far - 1, 0, -1):
        moves.append((True, k))
        if k > 1:
            moves.append((False, k - 1))
    todo = [(1, far)] + [(d, k) for k in range(far - 1, 0, -1) for d in (1, -1)] + [(1, 0)]
    for slot, (d, k) in enumerate(todo):
        slots[(d, k)] = slot
        block(dest_of(d, k), slot)
        if k == far:
            message(1, 1, far, slot)
            message(-1, 0, far, slot)
        elif k == far - 1:
            message(d, 1 - long_half[d], k, slot)
        if slot >= 3 and slot % 2 == 1 and slot < len(todo) - 1:
            forward(*moves.pop(0))
    for move in moves:
        forward(*move)
    for half in (0, 1):
        for d in (1, -1):
            take(d, half, 1, slot)
    for n in range(rows // 2):
        pair = part_ref[slot, n]
        for u in range(2):
            i = n * 2 + u
            cnt = cnt_ref[pl.ds(me * rows + i, 1), :] + 1e-3
            upd = (pair[:, span(u, res)] / cnt).T
            zs_ref[span(i, res), :] = (z_ref[i].astype(F32) + upd).astype(BF16).astype(F32)
    return sends


def tri_bias(zs_ref, ln_ref, w_ref, out_ref, rows, res):
    heads = w_ref.shape[0]
    vals = []
    for r in range(rows):
        ln = ln_lanes(zs_ref[span(r, res), :])
        if ln_ref is not None:
            ln_ref[span(r, res), :] = ln
        vals.append(mm_nt(w_ref[...], ln)[0:heads])
    out_ref[...] = jnp.concatenate(vals, axis=0).astype(BF16)


def tri_project(ln_ref, w_ref, proj_ref):
    step = 256
    for r in range(0, ln_ref.shape[0], step):
        proj_ref[r:r + step, :] = mm_nt(ln_ref[r:r + step, :], w_ref[...]).astype(BF16)


def tri_attend(zs_ref, proj_ref, bias_ref, wout_ref, heads, rows, res):
    width = proj_ref.shape[1] // 4
    hd = width // heads
    scale2 = hd ** -0.5 * LOG2E
    lane = lax.broadcasted_iota(jnp.int32, (res, width), 1)
    mine = [(lane >= h * hd) & (lane < (h + 1) * hd) for h in range(heads)]
    zero = jnp.zeros((res, width), BF16)

    def one(r0):
        part = lambda n: proj_ref[pl.ds(r0, res), span(n, width)]
        q, k, v, g = part(0), part(1), part(2), part(3)
        s = mm_nt(q, jnp.concatenate([jnp.where(mine[h], k, zero) for h in range(heads)], axis=0))
        ps = []
        for h in range(heads):
            cols = span(h, res)
            x = s[:, cols] * scale2 + bias_ref[:, cols]
            p = jnp.exp2(x - jnp.max(x, axis=1, keepdims=True))
            ps.append((p * (1.0 / jnp.sum(p, axis=1, keepdims=True))).astype(BF16))
        o = mm(jnp.concatenate(ps, axis=1), jnp.concatenate([jnp.where(mine[h], v, zero) for h in range(heads)], axis=0))
        y = (jax.nn.sigmoid(g.astype(F32)) * o).astype(BF16)
        upd = mm(y, wout_ref[...])
        zs_ref[pl.ds(r0, res), :] = (zs_ref[pl.ds(r0, res), :] + upd).astype(BF16).astype(F32)

    def body(it, _):
        for n in range(4):
            one(pl.multiple_of((it * 4 + n) * res, res))
        return 0

    lax.fori_loop(0, rows // 4, body, 0)


def pack_blocks(zs_ref, send_ref, rows, res, ndap):
    def one(q, _):
        parts = [zs_ref[pl.ds(q * rows + u, rows, stride=res), :] for u in range(rows)]
        send_ref[q] = jnp.concatenate(parts, axis=0).astype(BF16)
        return 0

    lax.fori_loop(0, ndap, one, 0)


def unpack_blocks(recv_ref, put, rows, ndap):
    for p in range(ndap):
        blk = recv_ref[p].astype(F32)
        for u in range(rows):
            put(u, p, blk[span(u, rows), :])


def pair_kernel(a_ref, c_ref, z_ref, mask_ref, rmask_ref, w_ref, wsb_ref, wsp_ref, wso_ref, web_ref, wep_ref, weo_ref,
                out_ref,
                ap_ref, cp_ref, part_ref, x_ref, wt_ref, w32_ref, cnt_ref, pos_ref, neg_ref,
                zs_ref, zc_ref, ln_ref, proj_ref, bias_ref, bwide_ref, sb_ref, sball_ref, eb_ref, eball_ref, xs_ref, xr_ref, ys_ref, yr_ref,
                ex_send, ex_recv, ring_send, ring_recv, send_sem, recv_sem, gsend, grecv, psend, precv, *, chips):
    ndap = 2 * chips
    me = lax.axis_index('dap')
    rows, res, _ = z_ref.shape
    heads = wsb_ref.shape[0]
    chip, core = me // 2, lax.rem(me, 2)
    partner = chip * 2 + 1 - core
    group_barrier(me, ndap)
    sends = outer_mean(me, a_ref, c_ref, z_ref, mask_ref, w_ref, zs_ref, ap_ref, cp_ref, part_ref, x_ref, wt_ref, w32_ref, cnt_ref, pos_ref, neg_ref, ex_send, ex_recv, ring_send, ring_recv, chips)
    kmask = (rmask_ref[...].astype(F32) - 1.0) * 1e4

    tri_bias(zs_ref, ln_ref, wsb_ref, sb_ref, rows, res)
    c1 = start_gather(sb_ref, sball_ref.at[core], chip, core, chips, gsend.at[0], grecv.at[0])
    tri_project(ln_ref, wsp_ref, proj_ref)
    finish(c1)
    p1 = remote(sball_ref.at[core], sball_ref.at[core], psend.at[0], precv.at[0], partner)
    p1.wait_recv()
    bwide_ref[...] = sball_ref[...].astype(F32)
    for h in range(heads):
        bias_ref[:, span(h, res)] = (bias_plane(bwide_ref, h, heads) + kmask) * LOG2E
    tri_attend(zs_ref, proj_ref, bias_ref, wso_ref, heads, rows, res)

    pack_blocks(zs_ref, xs_ref, rows, res, ndap)
    c2 = start_swap(xs_ref, xr_ref, me, ndap, send_sem.at[0], recv_sem.at[0])
    tri_bias(zs_ref, None, web_ref, eb_ref, rows, res)
    c3 = start_gather(eb_ref, eball_ref.at[core], chip, core, chips, gsend.at[1], grecv.at[1])
    finish(c2)
    finish(c3)
    p3 = remote(eball_ref.at[core], eball_ref.at[core], psend.at[1], precv.at[1], partner)

    def put_col(u, p, val):
        zc_ref[u * res + p * rows:u * res + (p + 1) * rows, :] = val

    unpack_blocks(xr_ref, put_col, rows, ndap)
    for r in range(rows):
        ln_ref[span(r, res), :] = ln_lanes(zc_ref[span(r, res), :])
    tri_project(ln_ref, wep_ref, proj_ref)
    p3.wait_recv()
    bwide_ref[...] = eball_ref[...].astype(F32)
    for h in range(heads):
        bias_ref[:, span(h, res)] = (bias_plane(bwide_ref, h, heads).T + kmask) * LOG2E
    tri_attend(zc_ref, proj_ref, bias_ref, weo_ref, heads, rows, res)

    pack_blocks(zc_ref, ys_ref, rows, res, ndap)
    c4 = start_swap(ys_ref, yr_ref, me, ndap, send_sem.at[1], recv_sem.at[1])
    finish(c4)

    def put_row(u, p, val):
        zs_ref[u * res + p * rows:u * res + (p + 1) * rows, :] = val

    unpack_blocks(yr_ref, put_row, rows, ndap)
    for r in range(rows):
        out_ref[r] = zs_ref[span(r, res), :].astype(BF16)
    drain(sends + c1 + c2 + c3 + c4 + [p1, p3])


def vspec():
    return pl.BlockSpec(memory_space=VMEM)


def call(kernel, outs, n_in, scratch, name, cid=None, flops=10 ** 9):
    params = dict(vmem_limit_bytes=60 * 2 ** 20)
    if cid is not None:
        params.update(collective_id=cid, has_side_effects=True)
    return pl.pallas_call(
        kernel,
        out_shape=outs,
        in_specs=[vspec()] * n_in,
        out_specs=jax.tree.map(lambda _: vspec(), outs),
        scratch_shapes=scratch,
        compiler_params=pltpu.CompilerParams(**params),
        cost_estimate=pl.CostEstimate(flops=flops, bytes_accessed=10 ** 6, transcendentals=0),
        name=name,
    )


def sds(shape, dtype):
    return jax.ShapeDtypeStruct(shape, dtype)


def solution(mesh):
    ndap = mesh.shape['dap']
    chips = ndap // 2

    def evoformer_block(msa, pair_act, full_mask, res_mask, row_bias_w, row_qkvg_w, row_out_w, col_query_w, col_kv_w, col_gate_w, col_out_w, opm_proj_w, opm_out_w, start_bias_w, start_qkvg_w, start_out_w, end_bias_w, end_qkvg_w, end_out_w):
        seqs, res, chans = msa.shape
        rows = pair_act.shape[0]
        heads, hd = row_qkvg_w.shape[2], row_qkvg_w.shape[3]
        width = heads * hd
        wide = opm_proj_w.shape[2]
        outc = opm_out_w.shape[2]
        thd = start_qkvg_w.shape[2] * start_qkvg_w.shape[3]
        theads = start_bias_w.shape[1]
        m_t = jnp.swapaxes(msa, 1, 2)
        wt = lambda w: w.reshape(w.shape[0], -1).T
        dma = pltpu.SemaphoreType.DMA

        nstat = heads + width // 2
        depth = 2
        m2, a, c = call(
            functools.partial(msa_kernel, ndap=ndap, heads=heads, hd=hd),
            [sds((seqs, chans, res), BF16), sds((chips, 2, rows * wide, seqs), BF16), sds((wide, seqs, res), BF16)], 11,
            [VMEM((rows * heads, res), BF16), VMEM((2, chips, rows * heads, res), BF16), VMEM((2, chips, rows * heads, res), F32),
             VMEM((chans, res), F32), VMEM((chans // 2, res), F32), VMEM((chans // 2, res), F32), VMEM((chips, chans // 2, res), F32), VMEM((chans, res), F32),
             VMEM((2, nstat, res), F32), VMEM((nstat, res), F32), VMEM((nstat, res), F32), VMEM((chips, nstat, res), F32),
             VMEM((seqs, chans, res), BF16), VMEM((seqs, res), F32), VMEM((res, heads * res), F32),
             VMEM((chans, width), BF16), VMEM((chans, width), BF16), VMEM((2 * hd + width, chans), BF16),
             VMEM((seqs, width, res), BF16), VMEM((seqs, res, width + 16), BF16), VMEM((seqs, width, res), BF16), VMEM((seqs, width, res), BF16), VMEM((seqs, width, res), BF16),
             [VMEM((res, heads * res), F32)] * depth, [VMEM((heads, res, res), BF16)] * depth, [VMEM((1, heads * res), F32)] * depth,
             VMEM((seqs, 3 * hd, res), F32), VMEM((2 * hd, seqs, res), F32), VMEM((width, res), F32),
             VMEM((seqs, wide + 8, res), F32), VMEM((seqs, wide + 8, res), F32), VMEM((res, wide + 8, seqs), F32),
             dma((3, chips)), dma((3, chips)), dma((5,)), dma((5,))],
            'msa_stack', cid=0,
        )(m_t, pair_act, full_mask, row_bias_w.T, wt(row_qkvg_w), row_out_w.reshape(width, chans), wt(col_query_w), wt(col_kv_w), wt(col_gate_w), col_out_w.reshape(width, chans), wt(opm_proj_w))
        msa_out = jnp.swapaxes(m2, 1, 2)

        npair = rows // 2
        nbuf = 2 * (chips // 2) - 1
        small = (rows * theads, res)
        block = (ndap, rows * rows, outc)
        pair_out = call(
            functools.partial(pair_kernel, chips=chips),
            sds(pair_act.shape, BF16), 12,
            [VMEM((chips, rows * wide, seqs), BF16), VMEM((wide, seqs, res), BF16),
             VMEM((chips, npair, outc, 2 * res), F32),
             VMEM((rows, 2 * wide * wide, res), BF16),
             VMEM((outc, 2 * wide * wide), BF16), VMEM((wide * wide, outc), F32), VMEM((res, res), F32),
             VMEM((nbuf, npair // 2, outc, 2 * res), F32), VMEM((nbuf, npair // 2, outc, 2 * res), F32),
             VMEM((rows * res, outc), F32), VMEM((rows * res, outc), F32), VMEM((rows * res, outc), BF16), VMEM((rows * res, 4 * thd), BF16), VMEM((res, theads * res), F32),
             VMEM((2, chips) + small, F32), VMEM(small, BF16), VMEM((2, chips) + small, BF16), VMEM(small, BF16), VMEM((2, chips) + small, BF16),
             VMEM(block, BF16), VMEM(block, BF16), VMEM(block, BF16), VMEM(block, BF16),
             dma((2,)), dma((2,)), dma((2, nbuf)), dma((2, nbuf)), dma((2, ndap)), dma((2, ndap)), dma((2, chips)), dma((2, chips)), dma((2,)), dma((2,))],
            'pair_stack', cid=1,
        )(a, c, pair_act, full_mask, res_mask.reshape(1, res), opm_out_w.reshape(wide * wide, outc),
          start_bias_w.T, wt(start_qkvg_w), start_out_w.reshape(thd, outc), end_bias_w.T, wt(end_qkvg_w), end_out_w.reshape(thd, outc))
        return msa_out, pair_out

    row_spec = P(('data', 'dap'), None, None)
    in_specs = (row_spec, row_spec, P('data', None), P('data')) + (P(),) * 15
    return jax.shard_map(evoformer_block, mesh=mesh, in_specs=in_specs, out_specs=(row_spec, row_spec), check_vma=False)
```

time: 213 us -> 174 us (0.82)
  Pallas kernels: 209 us -> 171 us
    pallas_call x1, Pallas kernels: 106 us -> 82.7 us  [evoformer_block(): call(functools.partial(msa_kernel, ndap=ndap, heads=heads, hd=hd), [sds((...]
    pallas_call x1, Pallas kernels: 104 us -> 88.4 us  [evoformer_block(): call(functools.partial(pair_kernel, chips=chips), sds(pair_act.shape, BF1...]
where the time goes in v4:
time: 174 us
  Pallas kernels  171 us (98%)
  local copies, waits for them, and re-layouts  2.03 us (1%)
    pallas_call x1, Pallas kernels, evoformer_block(): call(functools.partial(pair_kernel, chips=chips), sds(pair_act.shape, BF1...  88.4 us
    pallas_call x1, Pallas kernels, evoformer_block(): call(functools.partial(msa_kernel, ndap=ndap, heads=heads, hd=hd), [sds((...  82.7 us

profile of v4, /device:TPU:21, one launch (start us, length us, event | category | flops | bytes accessed | tf_op | source)
XLA Modules:
  0.0 173.8 jit_solution(7200890766239749220)
XLA Ops:
  0.6 82.7 %msa_stack.1 = (bf16[128,64,128]{2,1,0:T(8,128)(2,1)}, bf16[8,2,256,128]{3,2,1,0:T(8,128)(2,1)}, bf16[32,128,128]{2,1,0:T(8,128)(2,1)}) custom-call(bf16[128,64,128]{2,1,0:T(8,128)(2,1)} %bitcast.41, bf16[8,128,128]{2,1,0:T(8,128)(2,1)} %z_ref.3, s32[2048,128]{1,0:T(8,128)} %mask_ref.1, bf16[8,128]{1,0:T(8,128)(2,1)} %bitcast.49, bf16[256,64]{1,0:T(8,128)(2,1)} %bitcast.42, ...), custom_call_target="tpu_custom_call" | custom-call | flops 1000000000 | bytes 1000000 | tf_op jit(solution)/shard_map/msa_stack/pallas_call | solution.py:655
  83.3 0.0 copy-start
  83.3 88.4 %pair_stack.1 = bf16[8,128,128]{2,1,0:T(8,128)(2,1)} custom-call(bf16[8,2,256,128]{3,2,1,0:T(8,128)(2,1)} %get-tuple-element.6.a_ref, bf16[32,128,128]{2,1,0:T(8,128)(2,1)} %get-tuple-element.7.c_ref, bf16[8,128,128]{2,1,0:T(8,128)(2,1)} %z_ref.3, s32[2048,128]{1,0:T(8,128)} %mask_ref.1, s32[1,128]{1,0:T(1,128)} %bitcast.40, bf16[1024,128]{1,0:T(8,128)(2,1)} %bitcast.33, ...), custom_call_target="tpu_custom_call" | custom-call | flops 1000000000 | bytes 1000000 | tf_op jit(solution)/shard_map/pair_stack/pallas_call | solution.py:676
  171.7 0.0 copy-done
  171.8 0.0 copy-start.1
  171.8 1.3 copy.23
  173.1 0.0 copy-done.1
  173.1 0.7 copy.24
Async XLA Ops:
  83.3 88.4 %copy-start = (bf16[128,64,128]{2,1,0:T(8,128)(2,1)S(1)}, bf16[128,64,128]{2,1,0:T(8,128)(2,1)}, u32[]{:S(2)}) copy-start(bf16[128,64,128]{2,1,0:T(8,128)(2,1)} %get-tuple-element.5) | copy-start | bytes 6291460
  171.8 1.3 copy-start.1

commit v5 on v4

--- a/solution.py
+++ b/solution.py
@@ -255,7 +255,7 @@
     return gm, tot, wv, spread
 
 
-def col_finish(g_ref, m1_ref, mask_ref, wac_ref, m2_ref, a_ref, c_ref, o_ref, wo_ref, as_ref, cs_ref, at_ref):
+def col_finish(g_ref, m1_ref, mask_ref, wac_ref, m2_ref, a_ref, c_ref, o_ref, wo_ref, as_ref, cs_ref, at_ref, write_out, send_c, send_a):
     seqs, chans, res = m1_ref.shape
     wide = wac_ref.shape[0] // 2
 
@@ -280,26 +280,36 @@
 
     lax.fori_loop(0, seqs // 8, body, 0)
 
-    def planes(it, _):
-        for n in range(8):
-            e = it * 8 + n
+    write_out()
+    unroll = 8
+
+    def planes_c(it, _):
+        for n in range(unroll):
+            e = it * unroll + n
             c_ref[e] = strided(cs_ref, e).astype(BF16)
-            flat = at_ref.reshape(res * at_ref.shape[1], seqs)
+        return 0
+
+    def planes_a(it, _):
+        flat = at_ref.reshape(res * at_ref.shape[1], seqs)
+        for n in range(unroll):
+            e = it * unroll + n
             flat[pl.ds(e, res, stride=at_ref.shape[1]), :] = strided(as_ref, e).T
         return 0
 
-    lax.fori_loop(0, wide // 8, planes, 0)
+    lax.fori_loop(0, wide // unroll, planes_c, 0)
+    send_c()
+    lax.fori_loop(0, wide // unroll, planes_a, 0)
     rows = a_ref.shape[2] // wide
     for n in range(res):
         b, r = n // rows, n % rows
         a_ref[b // 2, b % 2, span(r, wide)] = at_ref[n, 0:wide].astype(BF16)
-
-
-def msa_kernel(m_ref, z_ref, fmask_ref, wb_ref, wqkvg_ref, wout_ref, wq_ref, wkv_ref, wg_ref, wcout_ref, wac_ref,
-               m2_ref, a_ref, c_ref,
+    send_a()
+
+
+def msa_part(m_ref, z_ref, fmask_ref, wb_ref, wqkvg_ref, wout_ref, wq_ref, wkv_ref, wg_ref, wcout_ref, wac_ref, m2_ref, a_ref, c_ref, idle, hooks,
                bsend_ref, ball_ref, bwide_ref, qsum_ref, qpart_ref, qhalf_ref, qall_ref, qfin_ref, stat_ref, spart_ref, smerge_ref, sall_ref, m1_ref, mask_ref, bias_ref, wo_ref, wco_ref, wkvg_ref,
                q_ref, kt_ref, v_ref, g_ref, y_ref, s_refs, p_refs, l_refs, kv_ref, planes_ref, o_ref, as_ref, cs_ref, at_ref,
-               send_sem, recv_sem, psend_sem, precv_sem, *, ndap, heads, hd):
+               send_sem, recv_sem, psend_sem, precv_sem, ndap, heads, hd):
     seqs, chans, res = m_ref.shape
     me = lax.axis_index('dap')
     chip, core = me // 2, lax.rem(me, 2)
@@ -347,52 +357,45 @@
     smerge_ref[hh:2 * hh] = tot
     smerge_ref[2 * hh:] = wv
     stat_copies = start_gather(smerge_ref, sall_ref, chip, core, chips, send_sem.at[2], recv_sem.at[2])
+    idle()
     finish(stat_copies)
     gm, tot, wv, spread = combine_stats([sall_ref[d] for d in range(chips)], hh, hd)
     omine = pl.ds(core * hh * hd, hh * hd)
     o_ref[omine, :] = wv / spread(tot)
     out_swap = remote(o_ref.at[omine], o_ref.at[omine], psend_sem.at[4], precv_sem.at[4], partner)
     out_swap.wait_recv()
-    col_finish(g_ref, m1_ref, mask_ref, wac_ref, m2_ref, a_ref, c_ref, o_ref, wco_ref, as_ref, cs_ref, at_ref)
-    drain(bias_copies + sum_copies + stat_copies + [bias_swap, sum_swap, fin_swap, stat_swap, out_swap])
+    col_finish(g_ref, m1_ref, mask_ref, wac_ref, m2_ref, a_ref, c_ref, o_ref, wco_ref, as_ref, cs_ref, at_ref, *hooks)
+    return bias_copies + sum_copies + stat_copies + [bias_swap, sum_swap, fin_swap, stat_swap, out_swap]
 
 
 def dap_index(chip, core, chips):
     return lax.rem(chip + 2 * chips, chips) * 2 + core
 
 
-def outer_mean(me, a_ref, c_ref, z_ref, mask_ref, w_ref, zs_ref, ap_ref, cp_ref, part_ref, x_ref, wt_ref, w32_ref, cnt_ref, pos_ref, neg_ref, ex_send, ex_recv, send_sem, recv_sem, chips):
+def outer_prepare(mask_ref, w_ref, wt_ref, w32_ref, cnt_ref, wide):
+    depth, lanes = w_ref.shape
+    w32_ref[...] = w_ref[...].astype(F32)
+    per = lanes // wide
+    for b in range(wide // per):
+        cols = [w32_ref[pl.ds(b * per + f, wide, stride=wide), :] for f in range(per)]
+        wt_ref[:, span(b, lanes)] = jnp.concatenate(cols, axis=0).T.astype(BF16)
+    wt_ref[:, depth:] = wt_ref[:, :depth]
+    res = mask_ref.shape[1]
+
+    def count_step(n, acc):
+        blk = mask_ref[pl.ds(n * res, res), :].astype(F32)
+        return acc + mm(blk.T.astype(BF16), blk.astype(BF16))
+
+    cnt_ref[...] = lax.fori_loop(0, mask_ref.shape[0] // res, count_step, jnp.zeros((res, res), F32))
+
+
+def outer_mean(me, a_ref, c_ref, z_ref, zs_ref, ap_ref, cp_ref, part_ref, x_ref, wt_ref, cnt_ref, pos_ref, neg_ref, send_sem, recv_sem, chips):
     chip, core = me // 2, lax.rem(me, 2)
     wide, seqs, res = c_ref.shape
     rows = z_ref.shape[0]
-    brow = rows * wide
-    outc = w_ref.shape[1]
-    partner = chip * 2 + 1 - core
     peer = {1: dap_index(chip + 1, core, chips), -1: dap_index(chip - 1, core, chips)}
     half_chips = chips // 2
     depth, unroll = wide * wide, 4
-
-    swaps = []
-    for n, (src, dst) in enumerate(((a_ref.at[:, 1 - core], ap_ref), (c_ref, cp_ref))):
-        cp = pltpu.make_async_remote_copy(src, dst, ex_send.at[n], ex_recv.at[n], device_id={'dap': partner}, device_id_type=MESH)
-        cp.start()
-        swaps.append(cp)
-
-    w32_ref[...] = w_ref[...].astype(F32)
-    per = 128 // wide
-    for b in range(wide // per):
-        cols = [w32_ref[pl.ds(b * per + f, wide, stride=wide), :] for f in range(per)]
-        wt_ref[:, span(b, 128)] = jnp.concatenate(cols, axis=0).T.astype(BF16)
-    wt_ref[:, depth:] = wt_ref[:, :depth]
-
-    def count_step(n, acc):
-        blk = mask_ref[pl.ds(n * 128, 128), :].astype(F32)
-        return acc + mm(blk.T.astype(BF16), blk.astype(BF16))
-
-    cnt_ref[...] = lax.fori_loop(0, mask_ref.shape[0] // 128, count_step, jnp.zeros((res, res), F32))
-
-    for cp in swaps:
-        cp.wait()
 
     def block(dest, slot):
         lhs = jnp.concatenate([a_ref[dest, core], ap_ref[dest]], axis=1)
@@ -502,7 +505,7 @@
         proj_ref[r:r + step, :] = mm_nt(ln_ref[r:r + step, :], w_ref[...]).astype(BF16)
 
 
-def tri_attend(zs_ref, proj_ref, bias_ref, wout_ref, heads, rows, res):
+def tri_attend(zs_ref, proj_ref, bias_ref, wout_ref, heads, rows, res, after):
     width = proj_ref.shape[1] // 4
     hd = width // heads
     scale2 = hd ** -0.5 * LOG2E
@@ -525,43 +528,60 @@
         upd = mm(y, wout_ref[...])
         zs_ref[pl.ds(r0, res), :] = (zs_ref[pl.ds(r0, res), :] + upd).astype(BF16).astype(F32)
 
-    def body(it, _):
-        for n in range(4):
-            one(pl.multiple_of((it * 4 + n) * res, res))
+    part_rows = rows // 2
+    for half in range(2):
+        for n in range(part_rows):
+            one((half * part_rows + n) * res)
+        after(half)
+
+
+def pack_blocks(zs_ref, send_ref, half, rows, res, ndap):
+    few = rows // 2
+
+    def one(q, _):
+        parts = [zs_ref[pl.ds(half * few * res + q * rows + u, few, stride=res), :] for u in range(rows)]
+        send_ref[half, q] = jnp.concatenate(parts, axis=0).astype(BF16)
         return 0
 
-    lax.fori_loop(0, rows // 4, body, 0)
-
-
-def pack_blocks(zs_ref, send_ref, rows, res, ndap):
-    def one(q, _):
-        parts = [zs_ref[pl.ds(q * rows + u, rows, stride=res), :] for u in range(rows)]
-        send_ref[q] = jnp.concatenate(parts, axis=0).astype(BF16)
-        return 0
-
     lax.fori_loop(0, ndap, one, 0)
 
 
-def unpack_blocks(recv_ref, put, rows, ndap):
-    for p in range(ndap):
-        blk = recv_ref[p].astype(F32)
-        for u in range(rows):
-            put(u, p, blk[span(u, rows), :])
-
-
-def pair_kernel(a_ref, c_ref, z_ref, mask_ref, rmask_ref, w_ref, wsb_ref, wsp_ref, wso_ref, web_ref, wep_ref, weo_ref,
-                out_ref,
-                ap_ref, cp_ref, part_ref, x_ref, wt_ref, w32_ref, cnt_ref, pos_ref, neg_ref,
-                zs_ref, zc_ref, ln_ref, proj_ref, bias_ref, bwide_ref, sb_ref, sball_ref, eb_ref, eball_ref, xs_ref, xr_ref, ys_ref, yr_ref,
-                ex_send, ex_recv, ring_send, ring_recv, send_sem, recv_sem, gsend, grecv, psend, precv, *, chips):
-    ndap = 2 * chips
+def unpack_blocks(recv_ref, dst_ref, rows, res, ndap):
+    few = rows // 2
+    for half in range(2):
+        for p in range(ndap):
+            blk = recv_ref[half, p].astype(F32)
+            for u in range(rows):
+                r0 = u * res + p * rows + half * few
+                dst_ref[r0:r0 + few, :] = blk[span(u, few), :]
+
+
+def block_kernel(m_ref, z_ref, fmask_ref, wb_ref, wqkvg_ref, wout_ref, wq_ref, wkv_ref, wg_ref, wcout_ref, wac_ref,
+                 rmask_ref, w_ref, wsb_ref, wsp_ref, wso_ref, web_ref, wep_ref, weo_ref,
+                 m2_ref, out_ref, msa_refs, pair_refs, *, ndap, heads, hd):
+    (a_ref, c_ref, m2v_ref, out_sem, ap_ref, cp_ref, part_ref, x_ref, wt_ref, w32_ref, cnt_ref, pos_ref, neg_ref,
+     zs_ref, zc_ref, ln_ref, proj_ref, bias_ref, bwide_ref, sb_ref, sball_ref, eb_ref, eball_ref, xs_ref, xr_ref, ys_ref, yr_ref,
+     ex_send, ex_recv, ring_send, ring_recv, send_sem, recv_sem, gsend, grecv, psend, precv) = pair_refs
+    chips = ndap // 2
     me = lax.axis_index('dap')
     rows, res, _ = z_ref.shape
-    heads = wsb_ref.shape[0]
     chip, core = me // 2, lax.rem(me, 2)
     partner = chip * 2 + 1 - core
-    group_barrier(me, ndap)
-    sends = outer_mean(me, a_ref, c_ref, z_ref, mask_ref, w_ref, zs_ref, ap_ref, cp_ref, part_ref, x_ref, wt_ref, w32_ref, cnt_ref, pos_ref, neg_ref, ex_send, ex_recv, ring_send, ring_recv, chips)
+    swaps = []
+    out_copy = pltpu.make_async_copy(m2v_ref, m2_ref, out_sem)
+
+    def send_c():
+        swaps.append(remote(c_ref, cp_ref, ex_send.at[0], ex_recv.at[0], partner))
+
+    def send_a():
+        swaps.append(remote(a_ref.at[:, 1 - core], ap_ref, ex_send.at[1], ex_recv.at[1], partner))
+
+    idle = lambda: outer_prepare(fmask_ref, w_ref, wt_ref, w32_ref, cnt_ref, c_ref.shape[0])
+    early = msa_part(m_ref, z_ref, fmask_ref, wb_ref, wqkvg_ref, wout_ref, wq_ref, wkv_ref, wg_ref, wcout_ref, wac_ref, m2v_ref, a_ref, c_ref,
+                     idle, (out_copy.start, send_c, send_a), *msa_refs, ndap, heads, hd)
+    finish(swaps)
+    sends = outer_mean(me, a_ref, c_ref, z_ref, zs_ref, ap_ref, cp_ref, part_ref, x_ref, wt_ref, cnt_ref, pos_ref, neg_ref, ring_send, ring_recv, chips)
+    heads = wsb_ref.shape[0]
     kmask = (rmask_ref[...].astype(F32) - 1.0) * 1e4
 
     tri_bias(zs_ref, ln_ref, wsb_ref, sb_ref, rows, res)
@@ -573,20 +593,21 @@
     bwide_ref[...] = sball_ref[...].astype(F32)
     for h in range(heads):
         bias_ref[:, span(h, res)] = (bias_plane(bwide_ref, h, heads) + kmask) * LOG2E
-    tri_attend(zs_ref, proj_ref, bias_ref, wso_ref, heads, rows, res)
-
-    pack_blocks(zs_ref, xs_ref, rows, res, ndap)
-    c2 = start_swap(xs_ref, xr_ref, me, ndap, send_sem.at[0], recv_sem.at[0])
+    moved = []
+
+    def swap_after(src_ref, send_ref, recv_ref, stage):
+        def after(half):
+            pack_blocks(src_ref, send_ref, half, rows, res, ndap)
+            moved.append(start_swap(send_ref.at[half], recv_ref.at[half], me, ndap, send_sem.at[stage, half], recv_sem.at[stage, half]))
+        return after
+
+    tri_attend(zs_ref, proj_ref, bias_ref, wso_ref, heads, rows, res, swap_after(zs_ref, xs_ref, xr_ref, 0))
     tri_bias(zs_ref, None, web_ref, eb_ref, rows, res)
     c3 = start_gather(eb_ref, eball_ref.at[core], chip, core, chips, gsend.at[1], grecv.at[1])
-    finish(c2)
+    finish(moved[0] + moved[1])
     finish(c3)
     p3 = remote(eball_ref.at[core], eball_ref.at[core], psend.at[1], precv.at[1], partner)
-
-    def put_col(u, p, val):
-        zc_ref[u * res + p * rows:u * res + (p + 1) * rows, :] = val
-
-    unpack_blocks(xr_ref, put_col, rows, ndap)
+    unpack_blocks(xr_ref, zc_ref, rows, res, ndap)
     for r in range(rows):
         ln_ref[span(r, res), :] = ln_lanes(zc_ref[span(r, res), :])
     tri_project(ln_ref, wep_ref, proj_ref)
@@ -594,39 +615,13 @@
     bwide_ref[...] = eball_ref[...].astype(F32)
     for h in range(heads):
         bias_ref[:, span(h, res)] = (bias_plane(bwide_ref, h, heads).T + kmask) * LOG2E
-    tri_attend(zc_ref, proj_ref, bias_ref, weo_ref, heads, rows, res)
-
-    pack_blocks(zc_ref, ys_ref, rows, res, ndap)
-    c4 = start_swap(ys_ref, yr_ref, me, ndap, send_sem.at[1], recv_sem.at[1])
-    finish(c4)
-
-    def put_row(u, p, val):
-        zs_ref[u * res + p * rows:u * res + (p + 1) * rows, :] = val
-
-    unpack_blocks(yr_ref, put_row, rows, ndap)
+    tri_attend(zc_ref, proj_ref, bias_ref, weo_ref, heads, rows, res, swap_after(zc_ref, ys_ref, yr_ref, 1))
+    finish(moved[2] + moved[3])
+    unpack_blocks(yr_ref, zs_ref, rows, res, ndap)
     for r in range(rows):
         out_ref[r] = zs_ref[span(r, res), :].astype(BF16)
-    drain(sends + c1 + c2 + c3 + c4 + [p1, p3])
-
-
-def vspec():
-    return pl.BlockSpec(memory_space=VMEM)
-
-
-def call(kernel, outs, n_in, scratch, name, cid=None, flops=10 ** 9):
-    params = dict(vmem_limit_bytes=60 * 2 ** 20)
-    if cid is not None:
-        params.update(collective_id=cid, has_side_effects=True)
-    return pl.pallas_call(
-        kernel,
-        out_shape=outs,
-        in_specs=[vspec()] * n_in,
-        out_specs=jax.tree.map(lambda _: vspec(), outs),
-        scratch_shapes=scratch,
-        compiler_params=pltpu.CompilerParams(**params),
-        cost_estimate=pl.CostEstimate(flops=flops, bytes_accessed=10 ** 6, transcendentals=0),
-        name=name,
-    )
+    drain(early + swaps + sends + c1 + c3 + sum(moved, []) + [p1, p3])
+    out_copy.wait()
 
 
 def sds(shape, dtype):
@@ -652,9 +647,11 @@
 
         nstat = heads + width // 2
         depth = 2
-        m2, a, c = call(
-            functools.partial(msa_kernel, ndap=ndap, heads=heads, hd=hd),
-            [sds((seqs, chans, res), BF16), sds((chips, 2, rows * wide, seqs), BF16), sds((wide, seqs, res), BF16)], 11,
+        npair = rows // 2
+        nbuf = 2 * (chips // 2) - 1
+        small = (rows * theads, res)
+        block = (2, ndap, rows * rows // 2, outc)
+        msa_scratch = (
             [VMEM((rows * heads, res), BF16), VMEM((2, chips, rows * heads, res), BF16), VMEM((2, chips, rows * heads, res), F32),
              VMEM((chans, res), F32), VMEM((chans // 2, res), F32), VMEM((chans // 2, res), F32), VMEM((chips, chans // 2, res), F32), VMEM((chans, res), F32),
              VMEM((2, nstat, res), F32), VMEM((nstat, res), F32), VMEM((nstat, res), F32), VMEM((chips, nstat, res), F32),
@@ -664,19 +661,10 @@
              [VMEM((res, heads * res), F32)] * depth, [VMEM((heads, res, res), BF16)] * depth, [VMEM((1, heads * res), F32)] * depth,
              VMEM((seqs, 3 * hd, res), F32), VMEM((2 * hd, seqs, res), F32), VMEM((width, res), F32),
              VMEM((seqs, wide + 8, res), F32), VMEM((seqs, wide + 8, res), F32), VMEM((res, wide + 8, seqs), F32),
-             dma((3, chips)), dma((3, chips)), dma((5,)), dma((5,))],
-            'msa_stack', cid=0,
-        )(m_t, pair_act, full_mask, row_bias_w.T, wt(row_qkvg_w), row_out_w.reshape(width, chans), wt(col_query_w), wt(col_kv_w), wt(col_gate_w), col_out_w.reshape(width, chans), wt(opm_proj_w))
-        msa_out = jnp.swapaxes(m2, 1, 2)
-
-        npair = rows // 2
-        nbuf = 2 * (chips // 2) - 1
-        small = (rows * theads, res)
-        block = (ndap, rows * rows, outc)
-        pair_out = call(
-            functools.partial(pair_kernel, chips=chips),
-            sds(pair_act.shape, BF16), 12,
-            [VMEM((chips, rows * wide, seqs), BF16), VMEM((wide, seqs, res), BF16),
+             dma((3, chips)), dma((3, chips)), dma((5,)), dma((5,))])
+        pair_scratch = (
+            [VMEM((chips, 2, rows * wide, seqs), BF16), VMEM((wide, seqs, res), BF16), VMEM((seqs, chans, res), BF16), dma(()),
+             VMEM((chips, rows * wide, seqs), BF16), VMEM((wide, seqs, res), BF16),
              VMEM((chips, npair, outc, 2 * res), F32),
              VMEM((rows, 2 * wide * wide, res), BF16),
              VMEM((outc, 2 * wide * wide), BF16), VMEM((wide * wide, outc), F32), VMEM((res, res), F32),
@@ -684,11 +672,20 @@
              VMEM((rows * res, outc), F32), VMEM((rows * res, outc), F32), VMEM((rows * res, outc), BF16), VMEM((rows * res, 4 * thd), BF16), VMEM((res, theads * res), F32),
              VMEM((2, chips) + small, F32), VMEM(small, BF16), VMEM((2, chips) + small, BF16), VMEM(small, BF16), VMEM((2, chips) + small, BF16),
              VMEM(block, BF16), VMEM(block, BF16), VMEM(block, BF16), VMEM(block, BF16),
-             dma((2,)), dma((2,)), dma((2, nbuf)), dma((2, nbuf)), dma((2, ndap)), dma((2, ndap)), dma((2, chips)), dma((2, chips)), dma((2,)), dma((2,))],
-            'pair_stack', cid=1,
-        )(a, c, pair_act, full_mask, res_mask.reshape(1, res), opm_out_w.reshape(wide * wide, outc),
+             dma((2,)), dma((2,)), dma((2, nbuf)), dma((2, nbuf)), dma((2, 2, ndap)), dma((2, 2, ndap)), dma((2, chips)), dma((2, chips)), dma((2,)), dma((2,))])
+        vspec = pl.BlockSpec(memory_space=VMEM)
+        m2, pair_out = pl.pallas_call(
+            functools.partial(block_kernel, ndap=ndap, heads=heads, hd=hd),
+            out_shape=[sds((seqs, chans, res), BF16), sds(pair_act.shape, BF16)],
+            in_specs=[vspec] * 19,
+            out_specs=[pl.BlockSpec(memory_space=pl.ANY), vspec],
+            scratch_shapes=[msa_scratch, pair_scratch],
+            compiler_params=pltpu.CompilerParams(vmem_limit_bytes=63 * 2 ** 20, collective_id=0, has_side_effects=True),
+            name='evoformer_block',
+        )(m_t, pair_act, full_mask, row_bias_w.T, wt(row_qkvg_w), row_out_w.reshape(width, chans), wt(col_query_w), wt(col_kv_w), wt(col_gate_w), col_out_w.reshape(width, chans), wt(opm_proj_w),
+          res_mask.reshape(1, res), opm_out_w.reshape(wide * wide, outc),
           start_bias_w.T, wt(start_qkvg_w), start_out_w.reshape(thd, outc), end_bias_w.T, wt(end_qkvg_w), end_out_w.reshape(thd, outc))
-        return msa_out, pair_out
+        return jnp.swapaxes(m2, 1, 2), pair_out
 
     row_spec = P(('data', 'dap'), None, None)
     in_specs = (row_spec, row_spec, P('data', None), P('data')) + (P(),) * 15

time: 174 us -> 164 us (0.943)
  Pallas kernels: 171 us -> 160 us
  local copies, waits for them, and re-layouts: 2.03 us -> 3.83 us
    pallas_call x2 -> x1, Pallas kernels: 171 us -> 160 us  [evoformer_block(): pl.pallas_call(functools.partial(block_kernel, ndap=ndap, heads=heads, hd...]
    unnamed x6 -> x4, local copies, waits for them, and re-layouts: 2.03 us -> 3.83 us
where the time goes in v5:
time: 164 us
  Pallas kernels  160 us (98%)
  local copies, waits for them, and re-layouts  3.83 us (2%)
    pallas_call x1, Pallas kernels, evoformer_block(): pl.pallas_call(functools.partial(block_kernel, ndap=ndap, heads=heads, hd...  160 us
    unnamed x4, local copies, waits for them, and re-layouts  3.83 us

profile of v5, /device:TPU:21, one launch (start us, length us, event | category | flops | bytes accessed | tf_op | source)
XLA Modules:
  0.0 164.3 jit_solution(4280773794055746476)
XLA Ops:
  0.6 159.9 %evoformer_block.1 = (bf16[128,64,128]{2,1,0:T(8,128)(2,1)}, bf16[8,128,128]{2,1,0:T(8,128)(2,1)}) custom-call(bf16[128,64,128]{2,1,0:T(8,128)(2,1)} %bitcast.32, bf16[8,128,128]{2,1,0:T(8,128)(2,1)} %z_ref.1, s32[2048,128]{1,0:T(8,128)} %fmask_ref.1, bf16[8,128]{1,0:T(8,128)(2,1)} %bitcast.46, bf16[256,64]{1,0:T(8,128)(2,1)} %bitcast.37, ...), custom_call_target="tpu_custom_call" | custom-call | tf_op jit(solution)/shard_map/evoformer_block/pallas_call | solution.py:677
  160.5 0.0 copy-start
  160.5 3.1 %copy.23 = bf16[128,128,64]{1,2,0:T(8,128)(2,1)} copy(bf16[128,128,64]{1,2,0:T(8,128)(2,1)} %bitcast.33) | data formatting | bytes 4194304
  163.6 0.0 copy-done
  163.6 0.7 copy.24
Async XLA Ops:
  160.5 3.1 %copy-start = (bf16[8,128,128]{2,1,0:T(8,128)(2,1)S(1)}, bf16[8,128,128]{2,1,0:T(8,128)(2,1)}, u32[]{:S(2)}) copy-start(bf16[8,128,128]{2,1,0:T(8,128)(2,1)} %get-tuple-element.9) | copy-start | bytes 786436

commit v6 on v5

--- a/solution.py
+++ b/solution.py
@@ -17,6 +17,15 @@
 
 def mm(left, right):
     return jnp.dot(left, right, preferred_element_type=F32)
+
+
+def paired(w_ref, arrs):
+    outs = []
+    for n in range(0, len(arrs), 2):
+        both = mm(w_ref[...], jnp.concatenate(arrs[n:n + 2], axis=1))
+        width = arrs[n].shape[1]
+        outs += [both[:, :width], both[:, width:]]
+    return outs
 
 
 def mm_nt(left, right):
@@ -59,11 +68,13 @@
     return out
 
 
-def group_barrier(me, ndap):
-    barrier = pltpu.get_barrier_semaphore()
+def greet(me, ndap):
     for k in range(1, ndap):
-        pl.semaphore_signal(barrier, inc=1, device_id={'dap': lax.rem(me + k, ndap)}, device_id_type=MESH)
-    pl.semaphore_wait(barrier, ndap - 1)
+        pl.semaphore_signal(pltpu.get_barrier_semaphore(), inc=1, device_id={'dap': lax.rem(me + k, ndap)}, device_id_type=MESH)
+
+
+def await_group(ndap):
+    pl.semaphore_wait(pltpu.get_barrier_semaphore(), ndap - 1)
 
 
 def far_first(count):
@@ -117,7 +128,7 @@
     return jnp.concatenate([wide_ref[u, c, pl.ds(h, rows, stride=heads), :] for c in range(wide_ref.shape[1]) for u in range(2)], axis=0)
 
 
-def row_project(m_ref, mask_ref, wqkvg_ref, q_ref, kt_ref, v_ref, g_ref, heads, hd, unroll=8):
+def row_project(m_ref, mask_ref, wqkvg_ref, q_ref, kt_ref, v_ref, g_ref, heads, hd, unroll=32):
     seqs, chans, res = m_ref.shape
     width = heads * hd
     aug = kt_ref.shape[2] - width
@@ -126,25 +137,17 @@
     mvec = jnp.where(rowi == 0, terms[0], jnp.where(rowi == 1, terms[1], jnp.where(rowi == 2, terms[2], 0.0)))
 
     def body(it, _):
-        for n in range(unroll // 2):
-            s0 = it * unroll + n * 2
-            lns = [ln_rows(m_ref[s0 + u].astype(F32)) for u in range(2)]
-            proj = mm(wqkvg_ref[...], jnp.concatenate(lns, axis=1))
-            for u in range(2):
-                cols = span(u, res)
-                s = s0 + u
-                q_ref[s] = proj[0:width, cols].astype(BF16)
-                mrow = mask_ref[pl.ds(s, 1), :] - 1.0
-                k = proj[width:2 * width, cols].astype(BF16).astype(F32)
-                kt_ref[s] = jnp.concatenate([k, mrow * mvec], axis=0).T.astype(BF16)
-                v_ref[s] = proj[2 * width:3 * width, cols].astype(BF16)
-                g_ref[s] = proj[3 * width:, cols].astype(BF16)
+        ids = [it * unroll + n for n in range(unroll)]
+        for s, proj in zip(ids, paired(wqkvg_ref, [ln_rows(m_ref[s].astype(F32)) for s in ids])):
+            q, k, v, g = [proj[span(n, width)].astype(BF16) for n in range(4)]
+            q_ref[s], v_ref[s], g_ref[s] = q, v, g
+            kt_ref[s] = jnp.concatenate([k.astype(F32), (mask_ref[pl.ds(s, 1), :] - 1.0) * mvec], axis=0).T.astype(BF16)
         return 0
 
     lax.fori_loop(0, seqs // unroll, body, 0)
 
 
-def row_attend(bias_ref, q_ref, kt_ref, v_ref, g_ref, y_ref, s_refs, p_refs, l_refs, heads, hd):
+def row_attend(bias_ref, q_ref, kt_ref, v_ref, g_ref, y_ref, s_refs, p_refs, l_refs, heads, hd, reps=4):
     seqs, width, res = q_ref.shape
     scale2 = hd ** -0.5 * LOG2E
     npairs = heads // 2
@@ -183,8 +186,9 @@
             scores(n, s_refs[n], t)
 
     def body(it, _):
-        for n in range(depth):
-            s = it * depth + n
+        for m in range(depth * reps):
+            s = it * depth * reps + m
+            n = m % depth
             far = (n + lead) % depth
             for t in range(npairs):
                 values(s - lead, p_refs[far], l_refs[far], t)
@@ -192,32 +196,30 @@
                 soft(s_refs[n], p_refs[n], l_refs[n], t)
         return 0
 
-    lax.fori_loop(0, seqs // depth, body, 0)
+    lax.fori_loop(0, seqs // (depth * reps), body, 0)
     for n in range(lead, depth):
         for t in range(npairs):
             values(seqs - depth + n, p_refs[n], l_refs[n], t)
 
 
-def row_finish(m_ref, mask_ref, wo_ref, wkvg_ref, y_ref, m1_ref, kv_ref, g_ref, qsum_ref, hd, unroll=8):
+def row_finish(m_ref, mask_ref, wo_ref, wkvg_ref, y_ref, m1_ref, kv_ref, g_ref, qsum_ref, hd, unroll=32):
     seqs, chans, res = m_ref.shape
 
     def body(it, _):
+        ids = [it * unroll + n for n in range(unroll)]
+        upds = paired(wo_ref, [y_ref[s] for s in ids])
+        lns = []
         acc = jnp.zeros((chans, res), F32)
-        for n in range(unroll // 2):
-            s0 = it * unroll + n * 2
-            upd = mm(wo_ref[...], jnp.concatenate([y_ref[s0], y_ref[s0 + 1]], axis=1))
-            ln1 = []
-            for u in range(2):
-                m1 = (m_ref[s0 + u].astype(F32) + upd[:, span(u, res)]).astype(BF16)
-                m1_ref[s0 + u] = m1
-                l1 = ln_rows(m1.astype(F32))
-                acc = acc + l1.astype(F32) * mask_ref[pl.ds(s0 + u, 1), :]
-                ln1.append(l1)
-            kvg = mm(wkvg_ref[...], jnp.concatenate(ln1, axis=1)).astype(BF16)
-            for u in range(2):
-                kv_ref[s0 + u, 0:2 * hd] = kvg[0:2 * hd, span(u, res)].astype(F32)
-                g_ref[s0 + u] = kvg[2 * hd:, span(u, res)]
+        for s, upd in zip(ids, upds):
+            m1 = (m_ref[s].astype(F32) + upd).astype(BF16)
+            m1_ref[s] = m1
+            lns.append(ln_rows(m1.astype(F32)))
+            acc = acc + lns[-1].astype(F32) * mask_ref[pl.ds(s, 1), :]
         qsum_ref[...] += acc
+        for s, kvg in zip(ids, paired(wkvg_ref, lns)):
+            kvg = kvg.astype(BF16)
+            kv_ref[s, 0:2 * hd] = kvg[0:2 * hd].astype(F32)
+            g_ref[s] = kvg[2 * hd:]
         return 0
 
     lax.fori_loop(0, seqs // unroll, body, 0)
@@ -259,27 +261,23 @@
     seqs, chans, res = m1_ref.shape
     wide = wac_ref.shape[0] // 2
 
-    def pair(s0):
-        ys = [(jax.nn.sigmoid(g_ref[s0 + u].astype(F32)) * o_ref[...]).astype(BF16) for u in range(2)]
-        upd = mm(wo_ref[...], jnp.concatenate(ys, axis=1))
+    unroll = 32
+
+    def body(it, _):
+        ids = [it * unroll + n for n in range(unroll)]
+        upds = paired(wo_ref, [(jax.nn.sigmoid(g_ref[s].astype(F32)) * o_ref[...]).astype(BF16) for s in ids])
         lns = []
-        for u in range(2):
-            m2 = (m1_ref[s0 + u].astype(F32) + upd[:, span(u, res)]).astype(BF16)
-            m2_ref[s0 + u] = m2
+        for s, upd in zip(ids, upds):
+            m2 = (m1_ref[s].astype(F32) + upd).astype(BF16)
+            m2_ref[s] = m2
             lns.append(ln_rows(m2.astype(F32)))
-        ac = mm(wac_ref[...], jnp.concatenate(lns, axis=1)).astype(BF16).astype(F32)
-        for u in range(2):
-            mrow = mask_ref[pl.ds(s0 + u, 1), :]
-            as_ref[s0 + u, 0:wide] = ac[0:wide, span(u, res)] * mrow
-            cs_ref[s0 + u, 0:wide] = ac[wide:, span(u, res)] * mrow
-
-    def body(it, _):
-        for n in range(4):
-            pair(it * 8 + n * 2)
+        for s, ac in zip(ids, paired(wac_ref, lns)):
+            ac = ac.astype(BF16).astype(F32) * mask_ref[pl.ds(s, 1), :]
+            as_ref[s, 0:wide] = ac[0:wide]
+            cs_ref[s, 0:wide] = ac[wide:]
         return 0
 
-    lax.fori_loop(0, seqs // 8, body, 0)
-
+    lax.fori_loop(0, seqs // unroll, body, 0)
     write_out()
     unroll = 8
 
@@ -315,8 +313,9 @@
     chip, core = me // 2, lax.rem(me, 2)
     chips = ndap // 2
     partner = chip * 2 + 1 - core
+    greet(me, ndap)
     pair_bias(z_ref, wb_ref, bsend_ref)
-    group_barrier(me, ndap)
+    await_group(ndap)
     bias_copies = start_gather(bsend_ref, ball_ref.at[core], chip, core, chips, send_sem.at[0], recv_sem.at[0])
     mask_ref[...] = fmask_ref[pl.ds(me * seqs, seqs), :].astype(F32)
     wo_ref[...] = wout_ref[...].astype(F32).T.astype(BF16)
@@ -502,7 +501,7 @@
 def tri_project(ln_ref, w_ref, proj_ref):
     step = 256
     for r in range(0, ln_ref.shape[0], step):
-        proj_ref[r:r + step, :] = mm_nt(ln_ref[r:r + step, :], w_ref[...]).astype(BF16)
+        proj_ref[r:r + step, :] = mm(ln_ref[r:r + step, :], w_ref[...]).astype(BF16)
 
 
 def tri_attend(zs_ref, proj_ref, bias_ref, wout_ref, heads, rows, res, after):
@@ -511,12 +510,15 @@
     scale2 = hd ** -0.5 * LOG2E
     lane = lax.broadcasted_iota(jnp.int32, (res, width), 1)
     mine = [(lane >= h * hd) & (lane < (h + 1) * hd) for h in range(heads)]
+    deep = lax.broadcasted_iota(jnp.int32, (width, res), 0)
+    under = [(deep >= h * hd) & (deep < (h + 1) * hd) for h in range(heads)]
     zero = jnp.zeros((res, width), BF16)
 
     def one(r0):
         part = lambda n: proj_ref[pl.ds(r0, res), span(n, width)]
         q, k, v, g = part(0), part(1), part(2), part(3)
-        s = mm_nt(q, jnp.concatenate([jnp.where(mine[h], k, zero) for h in range(heads)], axis=0))
+        kt = k.T
+        s = mm(q, jnp.concatenate([jnp.where(under[h], kt, zero) for h in range(heads)], axis=1))
         ps = []
         for h in range(heads):
             cols = span(h, res)
@@ -560,7 +562,7 @@
                  rmask_ref, w_ref, wsb_ref, wsp_ref, wso_ref, web_ref, wep_ref, weo_ref,
                  m2_ref, out_ref, msa_refs, pair_refs, *, ndap, heads, hd):
     (a_ref, c_ref, m2v_ref, out_sem, ap_ref, cp_ref, part_ref, x_ref, wt_ref, w32_ref, cnt_ref, pos_ref, neg_ref,
-     zs_ref, zc_ref, ln_ref, proj_ref, bias_ref, bwide_ref, sb_ref, sball_ref, eb_ref, eball_ref, xs_ref, xr_ref, ys_ref, yr_ref,
+     zs_ref, zc_ref, ln_ref, proj_ref, bias_ref, bwide_ref, sb_ref, sball_ref, eb_ref, eball_ref, xs_ref, xr_ref, ys_ref, yr_ref, wsn_ref, wen_ref,
      ex_send, ex_recv, ring_send, ring_recv, send_sem, recv_sem, gsend, grecv, psend, precv) = pair_refs
     chips = ndap // 2
     me = lax.axis_index('dap')
@@ -576,7 +578,11 @@
     def send_a():
         swaps.append(remote(a_ref.at[:, 1 - core], ap_ref, ex_send.at[1], ex_recv.at[1], partner))
 
-    idle = lambda: outer_prepare(fmask_ref, w_ref, wt_ref, w32_ref, cnt_ref, c_ref.shape[0])
+    def idle():
+        outer_prepare(fmask_ref, w_ref, wt_ref, w32_ref, cnt_ref, c_ref.shape[0])
+        wsn_ref[...] = wsp_ref[...].T
+        wen_ref[...] = wep_ref[...].T
+
     early = msa_part(m_ref, z_ref, fmask_ref, wb_ref, wqkvg_ref, wout_ref, wq_ref, wkv_ref, wg_ref, wcout_ref, wac_ref, m2v_ref, a_ref, c_ref,
                      idle, (out_copy.start, send_c, send_a), *msa_refs, ndap, heads, hd)
     finish(swaps)
@@ -586,7 +592,7 @@
 
     tri_bias(zs_ref, ln_ref, wsb_ref, sb_ref, rows, res)
     c1 = start_gather(sb_ref, sball_ref.at[core], chip, core, chips, gsend.at[0], grecv.at[0])
-    tri_project(ln_ref, wsp_ref, proj_ref)
+    tri_project(ln_ref, wsn_ref, proj_ref)
     finish(c1)
     p1 = remote(sball_ref.at[core], sball_ref.at[core], psend.at[0], precv.at[0], partner)
     p1.wait_recv()
@@ -604,23 +610,25 @@
     tri_attend(zs_ref, proj_ref, bias_ref, wso_ref, heads, rows, res, swap_after(zs_ref, xs_ref, xr_ref, 0))
     tri_bias(zs_ref, None, web_ref, eb_ref, rows, res)
     c3 = start_gather(eb_ref, eball_ref.at[core], chip, core, chips, gsend.at[1], grecv.at[1])
+    drain(early + swaps)
     finish(moved[0] + moved[1])
     finish(c3)
     p3 = remote(eball_ref.at[core], eball_ref.at[core], psend.at[1], precv.at[1], partner)
     unpack_blocks(xr_ref, zc_ref, rows, res, ndap)
     for r in range(rows):
         ln_ref[span(r, res), :] = ln_lanes(zc_ref[span(r, res), :])
-    tri_project(ln_ref, wep_ref, proj_ref)
+    tri_project(ln_ref, wen_ref, proj_ref)
     p3.wait_recv()
     bwide_ref[...] = eball_ref[...].astype(F32)
     for h in range(heads):
         bias_ref[:, span(h, res)] = (bias_plane(bwide_ref, h, heads).T + kmask) * LOG2E
     tri_attend(zc_ref, proj_ref, bias_ref, weo_ref, heads, rows, res, swap_after(zc_ref, ys_ref, yr_ref, 1))
+    drain(sends + c1 + c3 + moved[0] + moved[1] + [p1, p3])
     finish(moved[2] + moved[3])
     unpack_blocks(yr_ref, zs_ref, rows, res, ndap)
     for r in range(rows):
         out_ref[r] = zs_ref[span(r, res), :].astype(BF16)
-    drain(early + swaps + sends + c1 + c3 + sum(moved, []) + [p1, p3])
+    drain(moved[2] + moved[3])
     out_copy.wait()
 
 
@@ -671,7 +679,7 @@
              VMEM((nbuf, npair // 2, outc, 2 * res), F32), VMEM((nbuf, npair // 2, outc, 2 * res), F32),
              VMEM((rows * res, outc), F32), VMEM((rows * res, outc), F32), VMEM((rows * res, outc), BF16), VMEM((rows * res, 4 * thd), BF16), VMEM((res, theads * res), F32),
              VMEM((2, chips) + small, F32), VMEM(small, BF16), VMEM((2, chips) + small, BF16), VMEM(small, BF16), VMEM((2, chips) + small, BF16),
-             VMEM(block, BF16), VMEM(block, BF16), VMEM(block, BF16), VMEM(block, BF16),
+             VMEM(block, BF16), VMEM(block, BF16), VMEM(block, BF16), VMEM(block, BF16), VMEM((outc, 4 * thd), BF16), VMEM((outc, 4 * thd), BF16),
              dma((2,)), dma((2,)), dma((2, nbuf)), dma((2, nbuf)), dma((2, 2, ndap)), dma((2, 2, ndap)), dma((2, chips)), dma((2, chips)), dma((2,)), dma((2,))])
         vspec = pl.BlockSpec(memory_space=VMEM)
         m2, pair_out = pl.pallas_call(

time: 164 us -> 151 us (0.921)
  Pallas kernels: 160 us -> 146 us
    pallas_call x1, Pallas kernels: 160 us -> 146 us  [evoformer_block(): pl.pallas_call(functools.partial(block_kernel, ndap=ndap, heads=heads, hd...]
where the time goes in v6:
time: 151 us
  Pallas kernels  146 us (97%)
  local copies, waits for them, and re-layouts  3.83 us (3%)
    pallas_call x1, Pallas kernels, evoformer_block(): pl.pallas_call(functools.partial(block_kernel, ndap=ndap, heads=heads, hd...  146 us
    unnamed x4, local copies, waits for them, and re-layouts  3.83 us

profile of v6, /device:TPU:21, one launch (start us, length us, event | category | flops | bytes accessed | tf_op | source)
XLA Modules:
  0.0 150.8 jit_solution(5933319239965550468)
XLA Ops:
  0.6 146.3 %evoformer_block.1 = (bf16[128,64,128]{2,1,0:T(8,128)(2,1)}, bf16[8,128,128]{2,1,0:T(8,128)(2,1)}) custom-call(bf16[128,64,128]{2,1,0:T(8,128)(2,1)} %bitcast.32, bf16[8,128,128]{2,1,0:T(8,128)(2,1)} %z_ref.1, s32[2048,128]{1,0:T(8,128)} %fmask_ref.1, bf16[8,128]{1,0:T(8,128)(2,1)} %bitcast.46, bf16[256,64]{1,0:T(8,128)(2,1)} %bitcast.37, ...), custom_call_target="tpu_custom_call" | custom-call | tf_op jit(solution)/shard_map/evoformer_block/pallas_call | solution.py:685
  147.0 0.0 copy-start
  147.0 3.1 %copy.23 = bf16[128,128,64]{1,2,0:T(8,128)(2,1)} copy(bf16[128,128,64]{1,2,0:T(8,128)(2,1)} %bitcast.33) | data formatting | bytes 4194304
  150.1 0.0 copy-done
  150.1 0.7 copy.24
Async XLA Ops:
  147.0 3.1 %copy-start = (bf16[8,128,128]{2,1,0:T(8,128)(2,1)S(1)}, bf16[8,128,128]{2,1,0:T(8,128)(2,1)}, u32[]{:S(2)}) copy-start(bf16[8,128,128]{2,1,0:T(8,128)(2,1)} %get-tuple-element.9) | copy-start | bytes 786436

commit v7 on v6

--- a/solution.py
+++ b/solution.py
@@ -147,7 +147,7 @@
     lax.fori_loop(0, seqs // unroll, body, 0)
 
 
-def row_attend(bias_ref, q_ref, kt_ref, v_ref, g_ref, y_ref, s_refs, p_refs, l_refs, heads, hd, reps=4):
+def row_attend(bias_ref, q_ref, kt_ref, v_ref, g_ref, y_ref, s_refs, p_refs, l_refs, heads, hd, reps=8):
     seqs, width, res = q_ref.shape
     scale2 = hd ** -0.5 * LOG2E
     npairs = heads // 2
@@ -279,7 +279,7 @@
 
     lax.fori_loop(0, seqs // unroll, body, 0)
     write_out()
-    unroll = 8
+    unroll = 16
 
     def planes_c(it, _):
         for n in range(unroll):
@@ -510,30 +510,32 @@
     scale2 = hd ** -0.5 * LOG2E
     lane = lax.broadcasted_iota(jnp.int32, (res, width), 1)
     mine = [(lane >= h * hd) & (lane < (h + 1) * hd) for h in range(heads)]
-    deep = lax.broadcasted_iota(jnp.int32, (width, res), 0)
-    under = [(deep >= h * hd) & (deep < (h + 1) * hd) for h in range(heads)]
     zero = jnp.zeros((res, width), BF16)
 
-    def one(r0):
-        part = lambda n: proj_ref[pl.ds(r0, res), span(n, width)]
-        q, k, v, g = part(0), part(1), part(2), part(3)
-        kt = k.T
-        s = mm(q, jnp.concatenate([jnp.where(under[h], kt, zero) for h in range(heads)], axis=1))
+    def part(r, n):
+        return proj_ref[r * res:(r + 1) * res, span(n, width)]
+
+    def weights(s):
         ps = []
         for h in range(heads):
-            cols = span(h, res)
-            x = s[:, cols] * scale2 + bias_ref[:, cols]
+            x = s[:, span(h, res)] * scale2 + bias_ref[:, span(h, res)]
             p = jnp.exp2(x - jnp.max(x, axis=1, keepdims=True))
             ps.append((p * (1.0 / jnp.sum(p, axis=1, keepdims=True))).astype(BF16))
-        o = mm(jnp.concatenate(ps, axis=1), jnp.concatenate([jnp.where(mine[h], v, zero) for h in range(heads)], axis=0))
-        y = (jax.nn.sigmoid(g.astype(F32)) * o).astype(BF16)
-        upd = mm(y, wout_ref[...])
-        zs_ref[pl.ds(r0, res), :] = (zs_ref[pl.ds(r0, res), :] + upd).astype(BF16).astype(F32)
-
-    part_rows = rows // 2
+        return jnp.concatenate(ps, axis=1)
+
+    def by_head(val):
+        return jnp.concatenate([jnp.where(mine[h], val, zero) for h in range(heads)], axis=0)
+
+    few = rows // 2
     for half in range(2):
-        for n in range(part_rows):
-            one((half * part_rows + n) * res)
+        ids = range(half * few, (half + 1) * few)
+        logits = [mm_nt(part(r, 0), by_head(part(r, 1))) for r in ids]
+        probs = [weights(s) for s in logits]
+        outs = [mm(p, by_head(part(r, 2))) for r, p in zip(ids, probs)]
+        gated = [(jax.nn.sigmoid(part(r, 3).astype(F32)) * o).astype(BF16) for r, o in zip(ids, outs)]
+        upds = [mm(y, wout_ref[...]) for y in gated]
+        for r, upd in zip(ids, upds):
+            zs_ref[span(r, res), :] = (zs_ref[span(r, res), :] + upd).astype(BF16).astype(F32)
         after(half)
 
 

time: 151 us -> 149 us (0.987)
    pallas_call x1, Pallas kernels: 146 us -> 145 us  [evoformer_block(): pl.pallas_call(functools.partial(block_kernel, ndap=ndap, heads=heads, hd...]
where the time goes in v7:
time: 149 us
  Pallas kernels  145 us (97%)
  local copies, waits for them, and re-layouts  3.83 us (3%)
    pallas_call x1, Pallas kernels, evoformer_block(): pl.pallas_call(functools.partial(block_kernel, ndap=ndap, heads=heads, hd...  145 us
    unnamed x4, local copies, waits for them, and re-layouts  3.83 us

profile of v7, /device:TPU:21, one launch (start us, length us, event | category | flops | bytes accessed | tf_op | source)
XLA Modules:
  0.0 149.1 jit_solution(14385006076236309848)
XLA Ops:
  0.6 144.7 %evoformer_block.1 = (bf16[128,64,128]{2,1,0:T(8,128)(2,1)}, bf16[8,128,128]{2,1,0:T(8,128)(2,1)}) custom-call(bf16[128,64,128]{2,1,0:T(8,128)(2,1)} %bitcast.32, bf16[8,128,128]{2,1,0:T(8,128)(2,1)} %z_ref.1, s32[2048,128]{1,0:T(8,128)} %fmask_ref.1, bf16[8,128]{1,0:T(8,128)(2,1)} %bitcast.46, bf16[256,64]{1,0:T(8,128)(2,1)} %bitcast.37, ...), custom_call_target="tpu_custom_call" | custom-call | tf_op jit(solution)/shard_map/evoformer_block/pallas_call | solution.py:687
  145.3 0.0 copy-start
  145.3 3.1 %copy.23 = bf16[128,128,64]{1,2,0:T(8,128)(2,1)} copy(bf16[128,128,64]{1,2,0:T(8,128)(2,1)} %bitcast.33) | data formatting | bytes 4194304
  148.4 0.0 copy-done
  148.4 0.7 copy.24
Async XLA Ops:
  145.3 3.1 %copy-start = (bf16[8,128,128]{2,1,0:T(8,128)(2,1)S(1)}, bf16[8,128,128]{2,1,0:T(8,128)(2,1)}, u32[]{:S(2)}) copy-start(bf16[8,128,128]{2,1,0:T(8,128)(2,1)} %get-tuple-element.9) | copy-start | bytes 786436
